TPU v7x, 128 devices: a whole 4x4x4 slice. The times are simulated.
128 devices in a mesh: seq: 32 (over y, z_hi, x), sub: 4 (over z_lo, core).
Axes of the slice: x: 4, y: 4, z: 4 (z_hi: 2, z_lo: 2; z = z_hi * 2 + z_lo), core: 2. Of those that a mesh axis runs over, the one named last changes fastest.
Arguments:
- tokens: bfloat16 [8192, 4096], P('seq'), may hold values from -6 to 6
- w_split: bfloat16 [4096, 4096], P(None, 'sub'), may hold values from -0.09375 to 0.09375
- w_merge: bfloat16 [4096, 4096], P('sub'), may hold values from -0.09375 to 0.09375
- expert_in: bfloat16 [128, 1024, 2048], P(('seq', 'sub')), may hold values from -0.1875 to 0.1875
- expert_out: bfloat16 [128, 1024, 1024], P(('seq', 'sub')), may hold values from -0.1875 to 0.1875
- expert_ids: int32 [4, 8192, 2], P('sub', 'seq'), may hold values from 0 to 127, all different within a row; in each aligned block of 256 rows (0 to 255, 256 to 511, ..., all dimensions but the last counted through in order) at most 6 rows name the same one
- combine_q: int32 [4, 8192, 2], P('sub', 'seq'), may hold values from 4096 to 65536
- capacity: int32 [128], replicated, may hold values from 3 to 6
Outputs:
- mixed: bfloat16 [8192, 4096], P('seq', 'sub')
Inputs may be any that keep to these rules, and one draw needn't show every extreme that they name: `expert_ids`: in each block of 256 positions of one sub-head, the ids of a position differ, no expert is named more than 6 times, a bound that some block reaches.
All inputs are finite; a program needn't handle non-finite values.
Results may differ from a plain program's by a relative error of at most 0.0076.
Values may be sent and summed in bfloat16 or wider, within the bound.
No kernel may reach another device: no remote copies, remote signals or barrier semaphores. Data moves between devices by JAX's collectives and lax.ppermute only.
A program may use at most 128 MiB of HBM per device.

v0:
```python
import jax
import jax.numpy as jnp
from jax import lax
from jax.sharding import PartitionSpec as P


def split_up(shard, dim, peers):
    lengths = shard.shape
    blocks = shard.reshape(*lengths[:dim], peers, lengths[dim] // peers, *lengths[dim + 1 :])
    return jnp.moveaxis(blocks, dim, 0)


def summed_on_arrival(shard, axis, dim):
    blocks = split_up(shard, dim, lax.axis_size(axis))
    arrived = lax.all_to_all(blocks, axis, split_axis=0, concat_axis=0, tiled=True)
    return arrived.astype(jnp.float32).sum(axis=0)


def expert_rows(received, expert_in, expert_out):
    dims_in = received.shape
    rows_flat = received.reshape(-1, dims_in[-1])
    gate_up = jnp.dot(rows_flat, expert_in[0], preferred_element_type=jnp.float32)
    ffe_width = expert_out.shape[1]
    hidden = (jax.nn.silu(gate_up[:, :ffe_width]) * gate_up[:, ffe_width:]).astype(jnp.bfloat16)
    result = jnp.dot(hidden, expert_out[0], preferred_element_type=jnp.float32).astype(jnp.bfloat16)
    return result.reshape(dims_in)


def body(tokens, w_split, w_merge, expert_in, expert_out, expert_ids, combine_q, capacity):
    sub_tok = jnp.dot(tokens, w_split, preferred_element_type=jnp.float32).astype(jnp.bfloat16)
    tok_rows = tokens.shape[0]
    experts = capacity.shape[0]
    slot_count = 3 * tok_rows // experts
    expert_of = expert_ids[0].reshape(-1)
    onehot = (expert_of[:, None] == jnp.arange(experts, dtype=jnp.int32)[None, :]).astype(jnp.int32)
    order_rank = jnp.sum((jnp.cumsum(onehot, axis=0) - onehot) * onehot, axis=1)
    cap_limit = jnp.sum(onehot * capacity[None, :], axis=1)
    is_kept = order_rank < cap_limit
    slot_index = jnp.where(is_kept, expert_of * slot_count + order_rank, -1)
    target = jnp.arange(experts * slot_count, dtype=jnp.int32)
    chosen = jnp.any(
        target[:, None, None] == slot_index.reshape(tok_rows, -1)[None, :, :], axis=2
    ).astype(jnp.bfloat16)
    packed = jnp.dot(chosen, sub_tok, preferred_element_type=jnp.float32).astype(jnp.bfloat16)
    packed = packed.reshape(experts, slot_count, -1)
    answered = expert_rows(
        lax.all_to_all(packed, ("seq", "sub"), split_axis=0, concat_axis=0, tiled=True),
        expert_in,
        expert_out,
    )
    returned_rows = lax.all_to_all(
        answered, ("seq", "sub"), split_axis=0, concat_axis=0, tiled=True
    )
    returned_rows = returned_rows.reshape(experts * slot_count, -1)
    gathered = returned_rows[jnp.maximum(slot_index, 0)].astype(jnp.float32)
    weight = jnp.where(is_kept, combine_q[0].reshape(-1).astype(jnp.float32) / 65536.0, 0.0)
    weighted = (weight[:, None] * gathered).reshape(tok_rows, -1, gathered.shape[1])
    head_out = jnp.sum(weighted, axis=1).astype(jnp.bfloat16)
    partial_value = jnp.dot(head_out, w_merge, preferred_element_type=jnp.float32)
    return summed_on_arrival(partial_value.astype(jnp.bfloat16), "sub", 1).astype(jnp.bfloat16)


def solution(mesh):
    in_specs = (
        P("seq", None),
        P(None, "sub"),
        P("sub", None),
        P(("seq", "sub"), None, None),
        P(("seq", "sub"), None, None),
        P("sub", "seq", None),
        P("sub", "seq", None),
        P(),
    )
    out_specs = P("seq", "sub")
    return jax.shard_map(body, mesh=mesh, in_specs=in_specs, out_specs=out_specs, check_vma=False)
```

profile of v0, /device:TPU:1, one launch (start us, length us, event | category | flops | bytes accessed | tf_op | source)
XLA Modules:
  0.0 160.0 jit_solution(17669332753127285432)
XLA Ops:
  0.0 0.0 copy-start
  0.0 1.0 copy.24
  1.0 0.1 eq.44
  1.1 0.1 eq.40
  1.3 0.1 copy.26
  1.4 0.2 fusion.13
  1.7 1.0 select_reduce_fusion
  2.6 0.1 reduce_sum.49
  2.8 0.1 reduce_sum.50
  3.0 0.1 copy.30
  3.1 0.3 fusion.9
  3.3 0.0 copy-done
  3.4 7.3 %convolution_convert_fusion.1 = bf16[768,1024]{1,0:T(8,128)(2,1)} fusion(pred[768,256]{1,0:T(8,128)(4,1)S(1)} %fusion.9, bf16[256,4096]{1,0:T(8,128)(2,1)S(1)} %copy-done, bf16[4096,1024]{1,0:T(8,128)(2,1)} %param.9), kind=kOutput, calls=%fused_computation.11 | convolution fusion | flops 2551185408 | bytes 12255232 | tf_op jit(solution)/shard_map/dot_general | solution.py:44
  10.6 3.7 %reshape.109 = bf16[128,6,1024]{2,1,0:T(8,128)(2,1)} reshape(bf16[768,1024]{1,0:T(8,128)(2,1)} %convolution_convert_fusion.1) | data formatting | bytes 3145728 | tf_op jit(solution)/shard_map/reshape | solution.py:45
  14.3 41.5 %all_to_all.15 = bf16[128,6,1024]{2,1,0:T(8,128)(2,1)} all-to-all(bf16[128,6,1024]{2,1,0:T(8,128)(2,1)} %reshape.109), channel_id=1, replica_groups=mesh['seq'=32,'sub'=4] {'seq','sub'}, dimensions={0} | all-to-all | bytes 3145728 | tf_op jit(solution)/shard_map/all_to_all | solution.py:47
  55.9 3.7 %reshape.110 = bf16[768,1024]{1,0:T(8,128)(2,1)} reshape(bf16[128,6,1024]{2,1,0:T(8,128)(2,1)} %all_to_all.15) | data formatting | bytes 3145728 | tf_op jit(solution)/shard_map/reshape | solution.py:21
  59.6 5.8 %fusion = f32[768,2048]{1,0:T(8,128)S(1)} fusion(bf16[768,1024]{1,0:T(8,128)(2,1)} %reshape.110, bf16[1,1024,2048]{2,1,0:T(8,128)(2,1)} %param.11), kind=kOutput, calls=%fused_computation.2 | convolution fusion | flops 3221225472 | bytes 12058624 | tf_op jit(solution)/shard_map/dot_general | solution.py:22
  65.4 3.0 %fusion.5 = bf16[768,1024]{1,0:T(8,128)(2,1)} fusion(bf16[1,1024,1024]{2,1,0:T(8,128)(2,1)S(1)} %copy-done.2, f32[768,2048]{1,0:T(8,128)S(1)} %fusion), kind=kOutput, calls=%fused_computation.10 | convolution fusion | flops 1616117760 | bytes 9961472 | tf_op jit(solution)/shard_map/dot_general | solution.py:25
  68.4 3.7 %reshape.111 = bf16[128,6,1024]{2,1,0:T(8,128)(2,1)} reshape(bf16[768,1024]{1,0:T(8,128)(2,1)} %fusion.5) | data formatting | bytes 3145728 | tf_op jit(solution)/shard_map/reshape | solution.py:26
  72.1 5.7 %all-to-all-start.1 = ((bf16[128,6,1024]{2,1,0:T(8,128)(2,1)}), bf16[128,6,1024]{2,1,0:T(8,128)(2,1)}, u32[]{:S(2)}, u32[]{:S(2)}) async-start(bf16[128,6,1024]{2,1,0:T(8,128)(2,1)} %reshape.111), calls=%async_computation.1 | async-start | bytes 4194304 | tf_op jit(solution)/shard_map/all_to_all | solution.py:51
  77.8 0.1 mul.52
  78.0 0.2 lt.29
  78.2 0.1 copy.28
  78.4 29.1 %all-to-all-done.1 = bf16[128,6,1024]{2,1,0:T(8,128)(2,1)} async-done(((bf16[128,6,1024]{2,1,0:T(8,128)(2,1)}), bf16[128,6,1024]{2,1,0:T(8,128)(2,1)}, u32[]{:S(2)}, u32[]{:S(2)}) %all-to-all-start.1) | async-done | bytes 1572896 | tf_op jit(solution)/shard_map/all_to_all | solution.py:51
  107.5 3.7 %reshape.112 = bf16[768,1024]{1,0:T(8,128)(2,1)} reshape(bf16[128,6,1024]{2,1,0:T(8,128)(2,1)} %all-to-all-done.1) | data formatting | bytes 3145728 | tf_op jit(solution)/shard_map/reshape | solution.py:54
  111.2 4.3 %gather_fusion = bf16[512,1024]{1,0:T(8,128)(2,1)S(1)} fusion(bf16[768,1024]{1,0:T(8,128)(2,1)} %reshape.112, s32[1024]{0:T(1024)S(1)} %pad_clamp_fusion), kind=kCustom, calls=%fused_computation | custom fusion | bytes 2099200 | tf_op jit(solution)/shard_map/gather | solution.py:55
  115.6 2.4 %reshape.114 = f32[256,2,1024]{2,1,0:T(2,128)} reshape(bf16[512,1024]{1,0:T(8,128)(2,1)S(1)} %gather_fusion) | data formatting | bytes 3145728 | tf_op jit(solution)/shard_map/convert_element_type | solution.py:55
  117.9 4.3 %multiply_reduce_fusion = bf16[256,1024]{1,0:T(8,128)(2,1)S(1)} fusion(f32[256,2,1024]{2,1,0:T(2,128)} %reshape.114, f32[256,2]{1,0:T(8,128)S(1)} %bitcast_select_fusion), kind=kLoop, calls=%fused_computation.9 | loop fusion | flops 786432 | bytes 2623488 | tf_op jit(solution)/shard_map/reduce_sum | solution.py:58
  122.3 5.7 %convolution_convert_fusion = bf16[256,4096]{1,0:T(8,128)(2,1)S(1)} fusion(bf16[1024,4096]{1,0:T(8,128)(2,1)} %param.10, bf16[256,1024]{1,0:T(8,128)(2,1)S(1)} %multiply_reduce_fusion), kind=kOutput, calls=%fused_computation.1 | convolution fusion | flops 2148532224 | bytes 11010048 | tf_op jit(solution)/shard_map/dot_general | solution.py:59
  128.0 0.2 copy.34
  128.2 28.9 %all_to_all.16 = bf16[4,256,1024]{2,1,0:T(8,128)(2,1)} all-to-all(bf16[4,256,1024]{2,1,0:T(8,128)(2,1)S(1)} %bitcast.41), channel_id=1, replica_groups=mesh['seq'=32,'sub'=4] {'sub'}, dimensions={0} | all-to-all | bytes 4194304 | tf_op jit(solution)/shard_map/all_to_all | solution.py:15
  157.1 2.9 %reduce_sum.54 = bf16[256,1024]{1,0:T(8,128)(2,1)} reduce(bf16[4,256,1024]{2,1,0:T(8,128)(2,1)} %all_to_all.16, bf16[]{:T(256)} %constant.25.clone.1), dimensions={0}, to_apply=%region_6.7 | reduce | flops 786432 | bytes 2621442 | tf_op jit(solution)/shard_map/reduce_sum | solution.py:16
  (16 shorter events, 0.2 us)
Async XLA Ops:
  0.0 3.4 %copy-start = (bf16[256,4096]{1,0:T(8,128)(2,1)S(1)}, bf16[256,4096]{1,0:T(8,128)(2,1)}, u32[]{:S(2)}) copy-start(bf16[256,4096]{1,0:T(8,128)(2,1)} %param.8) | copy-start | bytes 6291460
  59.6 5.8 %copy-start.2 = (bf16[1,1024,1024]{2,1,0:T(8,128)(2,1)S(1)}, bf16[1,1024,1024]{2,1,0:T(8,128)(2,1)}, u32[]{:S(2)}) copy-start(bf16[1,1024,1024]{2,1,0:T(8,128)(2,1)} %param.12) | copy-start | bytes 6291460
  72.1 6.1 %copy-start.1 = (s32[1,256,2]{1,2,0:T(2,128)S(1)}, s32[1,256,2]{1,2,0:T(2,128)}, u32[]{:S(2)}) copy-start(s32[1,256,2]{1,2,0:T(2,128)} %param.14) | copy-start | bytes 6148
  72.1 35.4 %all-to-all-start.1 = ((bf16[128,6,1024]{2,1,0:T(8,128)(2,1)}), bf16[128,6,1024]{2,1,0:T(8,128)(2,1)}, u32[]{:S(2)}, u32[]{:S(2)}) async-start(bf16[128,6,1024]{2,1,0:T(8,128)(2,1)} %reshape.111), calls=%async_computation.1 | async-start | bytes 4194304 | tf_op jit(solution)/shard_map/all_to_all | solution.py:51
where the time goes:
time: 161 us; the launch traced here: 160 us
  blocking collectives  70.5 us (44%)
  waiting for transfers between devices  29.1 us (18%)
  local copies, waits for them, and re-layouts  23.9 us (15%)
  matrix products  21.8 us (14%)
  other arithmetic  8.83 us (5%)
  starting transfers between devices  5.72 us (4%)
    all_to_all x1, blocking collectives, body(): lax.all_to_all(packed, ('seq', 'sub'), split_axis=0, concat_axis=0, tiled...  41.5 us
    all_to_all x1, waiting for transfers between devices, body(): lax.all_to_all(answered, ('seq', 'sub'), split_axis=0, concat_axis=0, til...  29.1 us
    all_to_all x1, blocking collectives, summed_on_arrival(): lax.all_to_all(blocks, axis, split_axis=0, concat_axis=0, tiled=True)  28.9 us
    dot_general x1, matrix products, body(): jnp.dot(chosen, sub_tok, preferred_element_type=jnp.float32)  7.27 us
    dot_general x1, matrix products, expert_rows(): jnp.dot(rows_flat, expert_in[0], preferred_element_type=jnp.float32)  5.8 us
    dot_general x1, matrix products, body(): jnp.dot(head_out, w_merge, preferred_element_type=jnp.float32)  5.72 us
    all_to_all x1, starting transfers between devices, body(): lax.all_to_all(answered, ('seq', 'sub'), split_axis=0, concat_axis=0, til...  5.72 us
    gather x1, local copies, waits for them, and re-layouts, body(): gathered = returned_rows[jnp.maximum(slot_index, 0)].astype(jnp.float32)  4.34 us
  transfers between devices with their start and end apart: 1, of which 1 were waited for; matrix products, arithmetic and copies ran while one was open for 0% of the time, Pallas kernels for 0%

commit v1 on v0

v1 whole, which is shorter than its diff:
```python
import jax
import jax.numpy as jnp
from jax import lax
from jax.experimental import pallas as pl
from jax.experimental.pallas import tpu as pltpu
from jax.sharding import PartitionSpec as P

F32 = jnp.float32
BF16 = jnp.bfloat16
I32 = jnp.int32

SLOTS = 6
ROWS = 8
WIDE = 768
LANES = 256
TAILS = 3
NONE = -4.0


def iota(shape, dim):
    return lax.broadcasted_iota(I32, shape, dim)


def dot(a, b):
    return jnp.dot(a, b, preferred_element_type=F32)


def slot_of_row(row, part):
    if part is None:
        return jnp.where(row < SLOTS, row, -2)
    return jnp.where(row < SLOTS, -2, part + TAILS * (row - SLOTS))


def slot_keys(ids, capacity):
    experts = capacity.shape[1]
    tokens = ids.shape[1]
    expert = iota((experts, tokens), 0)
    named = (ids[0:1, :] == expert) | (ids[1:2, :] == expert)
    earlier = (iota((tokens, tokens), 0) < iota((tokens, tokens), 1)).astype(F32).astype(BF16)
    rank = dot(named.astype(F32).astype(BF16), earlier)
    own = iota((experts, experts), 0) == iota((experts, experts), 1)
    limit = jnp.sum(jnp.where(own, capacity.astype(F32), 0.0), axis=1, keepdims=True)
    return jnp.where(named & (rank < limit), rank, NONE)


def pack_body(ids_ref, cap_ref, tok_ref, w_ref, out_ref, acc_ref, pick_ref):
    step = pl.program_id(0)
    rows = out_ref.shape[0]

    @pl.when(step == 0)
    def _():
        key = slot_keys(ids_ref[...], cap_ref[...])
        experts = key.shape[0]
        spread = ((iota((rows, experts), 0) >> 3) == iota((rows, experts), 1)).astype(F32).astype(BF16)
        key = dot(spread, key.astype(BF16))
        row = iota(key.shape, 0) & (ROWS - 1)
        for n, part in enumerate((None, 0, 1, 2)):
            pick_ref[n] = (key == slot_of_row(row, part).astype(F32)).astype(F32).astype(BF16)
        acc_ref[...] = dot(tok_ref[...], w_ref[...])

    @pl.when(step > 0)
    def _():
        acc_ref[...] += dot(tok_ref[...], w_ref[...])

    @pl.when(step == pl.num_programs(0) - 1)
    def _():
        sub = acc_ref[...].astype(BF16)
        tail = sub[:, WIDE:]
        for k in range(TAILS):
            cols = slice(k * LANES, (k + 1) * LANES)
            packed = dot(pick_ref[0], sub[:, cols]) + dot(pick_ref[k + 1], tail)
            out_ref[:, cols] = packed.astype(BF16)


def split_and_pack(ids, capacity, tokens, w_split, steps=4):
    count, depth = tokens.shape
    width = w_split.shape[1]
    rows = capacity.shape[1] * ROWS
    part = depth // steps
    return pl.pallas_call(
        pack_body,
        grid=(steps,),
        in_specs=[
            pl.BlockSpec(ids.shape, lambda i: (0, 0)),
            pl.BlockSpec(capacity.shape, lambda i: (0, 0)),
            pl.BlockSpec((count, part), lambda i: (0, i)),
            pl.BlockSpec((part, width), lambda i: (i, 0)),
        ],
        out_specs=pl.BlockSpec((rows, WIDE), lambda i: (0, 0)),
        out_shape=jax.ShapeDtypeStruct((rows, WIDE), BF16),
        scratch_shapes=[pltpu.VMEM((count, width), F32), pltpu.VMEM((4, rows, count), BF16)],
        compiler_params=pltpu.CompilerParams(vmem_limit_bytes=24 << 20),
        name="split_pack",
    )(ids, capacity, tokens, w_split)


def weights_body(ids_ref, cap_ref, q_ref, out_ref):
    ids = ids_ref[...]
    key = slot_keys(ids, cap_ref[...])
    experts, tokens = key.shape
    expert = iota((experts, tokens), 0)
    scale = q_ref[...].astype(F32) / 65536.0
    weight = jnp.where(ids[0:1, :] == expert, scale[0:1, :], 0.0) + jnp.where(ids[1:2, :] == expert, scale[1:2, :], 0.0)
    cols = out_ref.shape[2]
    spread = ((iota((experts, cols), 1) >> 3) == iota((experts, cols), 0)).astype(F32).astype(BF16)
    key = dot(key.T.astype(BF16), spread)
    weight = dot(weight.T.astype(BF16), spread)
    row = iota(key.shape, 1) & (ROWS - 1)
    for n, part in enumerate((None, 0, 1, 2)):
        out_ref[n] = jnp.where(key == slot_of_row(row, part).astype(F32), weight, 0.0).astype(BF16)


def combine_weights(ids, capacity, q):
    tokens = ids.shape[1]
    cols = capacity.shape[1] * ROWS
    return pl.pallas_call(
        weights_body,
        out_shape=jax.ShapeDtypeStruct((4, tokens, cols), BF16),
        compiler_params=pltpu.CompilerParams(vmem_limit_bytes=24 << 20),
        name="combine_weights",
    )(ids, capacity, q)


GROUP = 16


def sixth(x):
    return (x * 43) >> 8


def unpack_picks():
    shape = (GROUP * SLOTS, GROUP * ROWS)
    to, frm = iota(shape, 0), iota(shape, 1)
    slot = to - sixth(to) * SLOTS
    same = sixth(to) == (frm >> 3)
    row = frm & (ROWS - 1)
    return [(same & (slot_of_row(row, part) == slot)).astype(F32).astype(BF16) for part in (None, 0, 1, 2)]


def pack_picks():
    shape = (GROUP * ROWS, GROUP * SLOTS)
    frm, to = iota(shape, 1), iota(shape, 0)
    slot = frm - sixth(frm) * SLOTS
    same = sixth(frm) == (to >> 3)
    row = to & (ROWS - 1)
    return [(same & (slot_of_row(row, part) == slot)).astype(F32).astype(BF16) for part in (None, 0, 1, 2)]


def expert_body(x_ref, gate_ref, up_ref, down_ref, out_ref, rows_ref, act_ref, tail_ref):
    step = pl.program_id(0)
    half = pl.num_programs(0) // 2
    groups = x_ref.shape[0] // (GROUP * ROWS)

    @pl.when(step == 0)
    def _():
        picks = unpack_picks()
        for g in range(groups):
            tiles = x_ref[g * GROUP * ROWS : (g + 1) * GROUP * ROWS, :]
            into = slice(g * GROUP * SLOTS, (g + 1) * GROUP * SLOTS)
            rows_ref[into, :WIDE] = dot(picks[0], tiles).astype(BF16)
            tail = dot(picks[1], tiles[:, :LANES])
            for k in range(1, TAILS):
                tail += dot(picks[k + 1], tiles[:, k * LANES : (k + 1) * LANES])
            rows_ref[into, WIDE:] = tail.astype(BF16)

    for j in range(4):

        @pl.when(step == j)
        def _():
            rows = rows_ref[...]
            gate = dot(rows, gate_ref[0])
            up = dot(rows, up_ref[0])
            act_ref[:, j * LANES : (j + 1) * LANES] = (gate / (1.0 + jnp.exp(-gate)) * up).astype(BF16)

    @pl.when(step == half)
    def _():
        tail_ref[...] = dot(act_ref[...], down_ref[0]).astype(BF16)

    for k in range(TAILS):

        @pl.when(step == half + 1 + k)
        def _():
            answer = dot(act_ref[...], down_ref[0]).astype(BF16)
            picks = pack_picks()
            for g in range(groups):
                frm = slice(g * GROUP * SLOTS, (g + 1) * GROUP * SLOTS)
                packed = dot(picks[0], answer[frm, :]) + dot(picks[k + 1], tail_ref[frm, :])
                out_ref[g * GROUP * ROWS : (g + 1) * GROUP * ROWS, k * LANES : (k + 1) * LANES] = packed.astype(BF16)


def expert_rows(tiles, expert_in, expert_out):
    rows = tiles.shape[0]
    slots = rows // ROWS * SLOTS
    width = expert_in.shape[1]
    hidden = expert_out.shape[1]
    return pl.pallas_call(
        expert_body,
        grid=(8,),
        in_specs=[
            pl.BlockSpec((rows, WIDE), lambda i: (0, 0)),
            pl.BlockSpec((1, width, LANES), lambda i: (0, 0, jnp.minimum(i, 3))),
            pl.BlockSpec((1, width, LANES), lambda i: (0, 0, 4 + jnp.minimum(i, 3))),
            pl.BlockSpec((1, hidden, LANES), lambda i: (0, 0, jnp.where(i < 5, 3, i - 5))),
        ],
        out_specs=pl.BlockSpec((rows, WIDE), lambda i: (0, 0)),
        out_shape=jax.ShapeDtypeStruct((rows, WIDE), BF16),
        scratch_shapes=[
            pltpu.VMEM((slots, width), BF16),
            pltpu.VMEM((slots, hidden), BF16),
            pltpu.VMEM((slots, LANES), BF16),
        ],
        compiler_params=pltpu.CompilerParams(vmem_limit_bytes=32 << 20),
        name="experts",
    )(tiles, expert_in, expert_in, expert_out)


def combine_body(at_ref, v_ref, b_ref, w_ref, head_ref, send_ref, keep_ref):
    step = pl.program_id(0)
    del at_ref

    @pl.when(step == 0)
    def _():
        tail = jnp.zeros((head_ref.shape[0], LANES), F32)
        for k in range(TAILS):
            cols = slice(k * LANES, (k + 1) * LANES)
            back = b_ref[:, cols]
            head_ref[:, cols] = dot(v_ref[0], back).astype(BF16)
            tail += dot(v_ref[k + 1], back)
        head_ref[:, WIDE:] = tail.astype(BF16)

    part = dot(head_ref[...], w_ref[...]).astype(BF16)
    width = part.shape[1]
    for j in range(2):

        @pl.when(step == j)
        def _():
            send_ref[:, j * width : (j + 1) * width] = part

        @pl.when(step == 2 + j)
        def _():
            keep_ref[:, j * width : (j + 1) * width] = part


def combine_and_merge(at, v, back, w_merge):
    tokens = v.shape[1]
    width = w_merge.shape[0]
    whole = lambda i, at: (0, 0)
    return pl.pallas_call(
        combine_body,
        grid_spec=pltpu.PrefetchScalarGridSpec(
            num_scalar_prefetch=1,
            grid=(4,),
            in_specs=[
                pl.BlockSpec(v.shape, lambda i, at: (0, 0, 0)),
                pl.BlockSpec(back.shape, whole),
                pl.BlockSpec((width, width // 2), lambda i, at: (0, at[i // 2] * 2 + i % 2)),
            ],
            out_specs=[pl.BlockSpec((tokens, width), whole)] * 3,
        ),
        out_shape=[jax.ShapeDtypeStruct((tokens, width), BF16)] * 3,
        compiler_params=pltpu.CompilerParams(vmem_limit_bytes=32 << 20),
        name="combine_merge",
    )(at, v, back, w_merge)


def merge_body(at_ref, head_ref, w_ref, send_ref, keep_ref):
    step = pl.program_id(0)
    del at_ref
    part = dot(head_ref[...], w_ref[...]).astype(BF16)
    width = part.shape[1]
    for j in range(2):

        @pl.when(step == j)
        def _():
            send_ref[:, j * width : (j + 1) * width] = part

        @pl.when(step == 2 + j)
        def _():
            keep_ref[:, j * width : (j + 1) * width] = part


def merge_own(at, head, w_merge):
    tokens, width = head.shape
    whole = lambda i, at: (0, 0)
    return pl.pallas_call(
        merge_body,
        grid_spec=pltpu.PrefetchScalarGridSpec(
            num_scalar_prefetch=1,
            grid=(4,),
            in_specs=[
                pl.BlockSpec(head.shape, whole),
                pl.BlockSpec((width, width // 2), lambda i, at: (0, at[i // 2] * 2 + i % 2)),
            ],
            out_specs=[pl.BlockSpec((tokens, width), whole)] * 2,
        ),
        out_shape=[jax.ShapeDtypeStruct((tokens, width), BF16)] * 2,
        compiler_params=pltpu.CompilerParams(vmem_limit_bytes=32 << 20),
        name="merge_own",
    )(at, head, w_merge)


def exchange(tiles, axes):
    peers = tiles.shape[0] // ROWS
    return lax.all_to_all(tiles.reshape(peers, ROWS, WIDE), axes, split_axis=0, concat_axis=0, tiled=True).reshape(tiles.shape)


def added(a, b):
    return (a.astype(F32) + b.astype(F32)).astype(BF16)


def body(tokens, w_split, w_merge, expert_in, expert_out, expert_ids, combine_q, capacity):
    ids = expert_ids[0].T
    q = combine_q[0].T
    limit = capacity.reshape(1, -1)
    tiles = exchange(split_and_pack(ids, limit, tokens, w_split), ("seq", "sub"))
    v = combine_weights(ids, limit, q)
    back = exchange(expert_rows(tiles, expert_in, expert_out), ("seq", "sub"))

    me = lax.axis_index("sub")
    core = [(i, i ^ 1) for i in range(4)]
    chip = [(i, i ^ 2) for i in range(4)]
    head, far_send, far_keep = combine_and_merge(jnp.stack([me ^ 3, me ^ 2]), v, back, w_merge)
    far_in = lax.ppermute(far_send, "sub", core)
    own_send, own_keep = merge_own(jnp.stack([me ^ 1, me]), head, w_merge)
    cross = lax.ppermute(added(far_keep, far_in), "sub", chip)
    own_in = lax.ppermute(own_send, "sub", core)
    return (own_keep.astype(F32) + own_in.astype(F32) + cross.astype(F32)).astype(BF16)


def solution(mesh):
    in_specs = (
        P("seq", None),
        P(None, "sub"),
        P("sub", None),
        P(("seq", "sub"), None, None),
        P(("seq", "sub"), None, None),
        P("sub", "seq", None),
        P("sub", "seq", None),
        P(),
    )
    out_specs = P("seq", "sub")
    return jax.shard_map(body, mesh=mesh, in_specs=in_specs, out_specs=out_specs, check_vma=False)
```

time: 161 us -> 120 us (0.75)
  blocking collectives: 70.5 us -> 36 us
  Pallas kernels: 0 us -> 26 us
  matrix products: 21.8 us -> 0 us
  local copies, waits for them, and re-layouts: 23.9 us -> 13.1 us
  other arithmetic: 8.83 us -> 1.41 us
  waiting for transfers between devices: 29.1 us -> 36.2 us
    all_to_all x2 -> x1, blocking collectives: 70.5 us -> 36 us  [exchange(): lax.all_to_all(tiles.reshape(peers, ROWS, WIDE), axes, split_axis=0, conc...]
    pallas_call x0 -> x5, Pallas kernels: none -> 26 us  [the longest x1 11.5 us: expert_rows(): pl.pallas_call(expert_body, grid=(8,), in_specs=[pl.BlockSpec((rows, WIDE...]
    dot_general x4 -> x0, matrix products: 21.8 us -> none  [the longest x1 7.27 us: body(): jnp.dot(chosen, sub_tok, preferred_element_type=jnp.float32)]
    reshape x5 -> x0, local copies, waits for them, and re-layouts: 15 us -> none  [the longest x1 3.73 us: expert_rows(): rows_flat = received.reshape(-1, dims_in[-1])]
    ppermute x0 -> x3, waiting for transfers between devices: none -> 12.6 us  [the longest x1 11.4 us: body(): cross = lax.ppermute(added(far_keep, far_in), 'sub', chip)]
    unnamed x8 -> x22, local copies, waits for them, and re-layouts: 0.97 us -> 13.1 us
    reduce_sum x3 -> x0, other arithmetic: 8.21 us -> none  [the longest x1 4.33 us: body(): head_out = jnp.sum(weighted, axis=1).astype(jnp.bfloat16)]
    all_to_all x1, waiting for transfers between devices: 29.1 us -> 23.6 us  [exchange(): lax.all_to_all(tiles.reshape(peers, ROWS, WIDE), axes, split_axis=0, conc...]
  transfers between devices with their start and end apart: 1 -> 4, of which waited for: 1 -> 3; matrix products, arithmetic and copies ran while one was open for 0% -> 0% of each run, Pallas kernels for 0% -> 3%
where the time goes in v1:
time: 120 us; the launch traced here: 119 us
  waiting for transfers between devices  36.2 us (30%)
  blocking collectives  36 us (30%)
  Pallas kernels  26 us (22%)
  local copies, waits for them, and re-layouts  13.1 us (11%)
  starting transfers between devices  6.52 us (5%)
  other arithmetic  1.41 us (1%)
    all_to_all x1, blocking collectives, exchange(): lax.all_to_all(tiles.reshape(peers, ROWS, WIDE), axes, split_axis=0, conc...  36 us
    all_to_all x1, waiting for transfers between devices, exchange(): lax.all_to_all(tiles.reshape(peers, ROWS, WIDE), axes, split_axis=0, conc...  23.6 us
    unnamed x22, local copies, waits for them, and re-layouts  13.1 us
    pallas_call x1, Pallas kernels, expert_rows(): pl.pallas_call(expert_body, grid=(8,), in_specs=[pl.BlockSpec((rows, WIDE...  11.5 us
    ppermute x1, waiting for transfers between devices, body(): cross = lax.ppermute(added(far_keep, far_in), 'sub', chip)  11.4 us
    pallas_call x1, Pallas kernels, combine_and_merge(): pl.pallas_call(combine_body, grid_spec=pltpu.PrefetchScalarGridSpec(num_s...  5.95 us
    all_to_all x1, starting transfers between devices, exchange(): lax.all_to_all(tiles.reshape(peers, ROWS, WIDE), axes, split_axis=0, conc...  5.26 us
    pallas_call x1, Pallas kernels, split_and_pack(): pl.pallas_call(pack_body, grid=(steps,), in_specs=[pl.BlockSpec(ids.shape...  4.85 us
  transfers between devices with their start and end apart: 4, of which 3 were waited for; matrix products, arithmetic and copies ran while one was open for 0% of the time, Pallas kernels for 3%

profile of v1, /device:TPU:1, one launch (start us, length us, event | category | flops | bytes accessed | tf_op | source)
XLA Modules:
  0.0 119.3 jit_solution(11762373613711326338)
XLA Ops:
  0.0 0.0 copy-start.3
  0.0 3.4 %copy-done.3 = bf16[4096,1024]{1,0:T(8,128)(2,1)S(1)} copy-done((bf16[4096,1024]{1,0:T(8,128)(2,1)S(1)}, bf16[4096,1024]{1,0:T(8,128)(2,1)}, u32[]{:S(2)}) %copy-start.3) | copy-done | bytes 8388632
  3.4 0.0 copy-start.4
  3.4 1.6 %copy-done.4 = bf16[256,4096]{1,0:T(8,128)(2,1)S(1)} copy-done((bf16[256,4096]{1,0:T(8,128)(2,1)S(1)}, bf16[256,4096]{1,0:T(8,128)(2,1)}, u32[]{:S(2)}) %copy-start.4) | copy-done | bytes 2097176
  5.0 0.7 copy-done.6
  5.7 0.7 copy-done.9
  6.3 4.8 %split_pack.1 = bf16[1024,768]{1,0:T(8,128)(2,1)S(1)} custom-call(s32[2,256]{1,0:T(2,128)S(1)} %bitcast.17, s32[1,128]{1,0:T(1,128)S(1)} %bitcast.20, bf16[256,4096]{1,0:T(8,128)(2,1)S(1)} %copy-done.4, bf16[4096,1024]{1,0:T(8,128)(2,1)S(1)} %copy-done.3), custom_call_target="tpu_custom_call" | custom-call | tf_op jit(solution)/shard_map/split_pack/pallas_call | solution.py:80
  11.2 0.0 copy-start.5
  11.2 36.0 %all_to_all.10 = bf16[128,8,768]{2,1,0:T(8,128)(2,1)S(1)} all-to-all(bf16[128,8,768]{2,1,0:T(8,128)(2,1)S(1)} %bitcast.15), channel_id=1, replica_groups=mesh['seq'=32,'sub'=4] {'seq','sub'}, dimensions={0} | all-to-all | bytes 3145728 | tf_op jit(solution)/shard_map/all_to_all | solution.py:304
  47.2 0.0 copy-done.2
  47.2 0.0 copy-done.5
  47.2 11.5 %experts.1 = bf16[1024,768]{1,0:T(8,128)(2,1)} custom-call(bf16[1024,768]{1,0:T(8,128)(2,1)S(1)} %bitcast.16, bf16[1,1024,2048]{2,1,0:T(8,128)(2,1)S(1)} %copy-done.2, bf16[1,1024,2048]{2,1,0:T(8,128)(2,1)S(1)} %copy-done.2, bf16[1,1024,1024]{2,1,0:T(8,128)(2,1)S(1)} %copy-done.5), custom_call_target="tpu_custom_call" | custom-call | tf_op jit(solution)/shard_map/experts/pallas_call | solution.py:196
  58.7 5.3 %all-to-all-start.1 = ((bf16[128,8,768]{2,1,0:T(8,128)(2,1)}), bf16[128,8,768]{2,1,0:T(8,128)(2,1)}, u32[]{:S(2)}, u32[]{:S(2)}) async-start(bf16[128,8,768]{2,1,0:T(8,128)(2,1)} %bitcast.12), calls=%async_computation.1 | async-start | bytes 3145728 | tf_op jit(solution)/shard_map/all_to_all | solution.py:304
  64.0 0.0 copy-done.7
  64.0 0.0 copy-done.8
  64.0 0.0 copy-done.10
  64.0 0.8 combine_weights.1.v_ref
  64.9 0.1 pad_add_fusion.1.at_ref
  64.9 23.6 %all-to-all-done.1 = bf16[128,8,768]{2,1,0:T(8,128)(2,1)} async-done(((bf16[128,8,768]{2,1,0:T(8,128)(2,1)}), bf16[128,8,768]{2,1,0:T(8,128)(2,1)}, u32[]{:S(2)}, u32[]{:S(2)}) %all-to-all-start.1) | async-done | bytes 1572896 | tf_op jit(solution)/shard_map/all_to_all | solution.py:304
  88.5 3.4 %copy-done = bf16[1024,4096]{1,0:T(8,128)(2,1)S(1)} copy-done((bf16[1024,4096]{1,0:T(8,128)(2,1)S(1)}, bf16[1024,4096]{1,0:T(8,128)(2,1)}, u32[]{:S(2)}) %copy-start) | copy-done | bytes 8388632
  91.9 6.0 %combine_merge.1 = (bf16[256,1024]{1,0:T(8,128)(2,1)S(1)}, bf16[256,1024]{1,0:T(8,128)(2,1)}, bf16[256,1024]{1,0:T(8,128)(2,1)S(1)}) custom-call(s32[2]{0:T(128)S(1)} %pad_add_fusion.1.at_ref, bf16[4,256,1024]{2,1,0:T(8,128)(2,1)S(1)} %combine_weights.1.v_ref, bf16[1024,768]{1,0:T(8,128)(2,1)} %bitcast.13.b_ref, bf16[1024,4096]{1,0:T(8,128)(2,1)S(1)} %copy-done), custom_call_target="tpu_custom_call" | custom-call | tf_op jit(solution)/shard_map/combine_merge/pallas_call | solution.py:248
  97.9 0.7 collective-permute-start.1
  98.5 0.1 pad_add_fusion.at_ref
  98.6 3.4 %copy-done.1 = bf16[1024,4096]{1,0:T(8,128)(2,1)S(1)} copy-done((bf16[1024,4096]{1,0:T(8,128)(2,1)S(1)}, bf16[1024,4096]{1,0:T(8,128)(2,1)}, u32[]{:S(2)}) %copy-start.1) | copy-done | bytes 8388632
  102.0 2.9 %merge_own.1 = (bf16[256,1024]{1,0:T(8,128)(2,1)S(1)}, bf16[256,1024]{1,0:T(8,128)(2,1)S(1)}) custom-call(s32[2]{0:T(128)S(1)} %pad_add_fusion.at_ref, bf16[256,1024]{1,0:T(8,128)(2,1)S(1)} %get-tuple-element.10.head_ref, bf16[1024,4096]{1,0:T(8,128)(2,1)S(1)} %copy-done.1), custom_call_target="tpu_custom_call" | custom-call | tf_op jit(solution)/shard_map/merge_own/pallas_call | solution.py:285
  104.9 0.1 collective-permute-start
  105.0 0.0 collective-permute-done.1
  105.0 0.2 add_convert_fusion.1
  105.2 0.5 collective-permute-start.2
  105.7 1.2 %collective-permute-done = bf16[256,1024]{1,0:T(8,128)(2,1)S(1)} collective-permute-done((bf16[256,1024]{1,0:T(8,128)(2,1)S(1)}, bf16[256,1024]{1,0:T(8,128)(2,1)S(1)}, u32[]{:S(2)}, u32[]{:S(2)}) %collective-permute-start) | collective-permute-done | bytes 524320 | tf_op jit(solution)/shard_map/ppermute | solution.py:326
  106.9 11.4 %collective-permute-done.2 = bf16[256,1024]{1,0:T(8,128)(2,1)S(1)} collective-permute-done((bf16[256,1024]{1,0:T(8,128)(2,1)S(1)}, bf16[256,1024]{1,0:T(8,128)(2,1)S(1)}, u32[]{:S(2)}, u32[]{:S(2)}) %collective-permute-start.2) | collective-permute-done | bytes 524320 | tf_op jit(solution)/shard_map/ppermute | solution.py:325
  118.3 1.1 add_convert_fusion
  (8 shorter events, 0.0 us)
Async XLA Ops:
  0.0 3.4 %copy-start.3 = (bf16[4096,1024]{1,0:T(8,128)(2,1)S(1)}, bf16[4096,1024]{1,0:T(8,128)(2,1)}, u32[]{:S(2)}) copy-start(bf16[4096,1024]{1,0:T(8,128)(2,1)} %w_ref.3) | copy-start | bytes 25165828
  3.4 1.6 %copy-start.4 = (bf16[256,4096]{1,0:T(8,128)(2,1)S(1)}, bf16[256,4096]{1,0:T(8,128)(2,1)}, u32[]{:S(2)}) copy-start(bf16[256,4096]{1,0:T(8,128)(2,1)} %tok_ref.1) | copy-start | bytes 6291460
  5.0 0.7 copy-start.6
  5.7 0.7 copy-start.9
  6.3 40.9 %copy-start.2 = (bf16[1,1024,2048]{2,1,0:T(8,128)(2,1)S(1)}, bf16[1,1024,2048]{2,1,0:T(8,128)(2,1)}, u32[]{:S(2)}) copy-start(bf16[1,1024,2048]{2,1,0:T(8,128)(2,1)} %up_ref.1) | copy-start | bytes 12582916
  11.2 36.0 %copy-start.5 = (bf16[1,1024,1024]{2,1,0:T(8,128)(2,1)S(1)}, bf16[1,1024,1024]{2,1,0:T(8,128)(2,1)}, u32[]{:S(2)}) copy-start(bf16[1,1024,1024]{2,1,0:T(8,128)(2,1)} %down_ref.1) | copy-start | bytes 6291460
  58.7 5.3 %copy-start.7 = (s32[1,256,2]{1,2,0:T(2,128)S(1)}, s32[1,256,2]{1,2,0:T(2,128)}, u32[]{:S(2)}) copy-start(s32[1,256,2]{1,2,0:T(2,128)} %param.13) | copy-start | bytes 6148
  58.7 5.3 %copy-start.8 = (s32[1,256,2]{1,2,0:T(2,128)S(1)}, s32[1,256,2]{1,2,0:T(2,128)}, u32[]{:S(2)}) copy-start(s32[1,256,2]{1,2,0:T(2,128)} %param.14) | copy-start | bytes 6148
  58.7 5.3 %copy-start.10 = (s32[128]{0:T(128)S(1)}, s32[128]{0:T(128)}, u32[]{:S(2)}) copy-start(s32[128]{0:T(128)} %param.15) | copy-start | bytes 1540
  58.7 29.8 %all-to-all-start.1 = ((bf16[128,8,768]{2,1,0:T(8,128)(2,1)}), bf16[128,8,768]{2,1,0:T(8,128)(2,1)}, u32[]{:S(2)}, u32[]{:S(2)}) async-start(bf16[128,8,768]{2,1,0:T(8,128)(2,1)} %bitcast.12), calls=%async_computation.1 | async-start | bytes 3145728 | tf_op jit(solution)/shard_map/all_to_all | solution.py:304
  88.5 3.4 %copy-start = (bf16[1024,4096]{1,0:T(8,128)(2,1)S(1)}, bf16[1024,4096]{1,0:T(8,128)(2,1)}, u32[]{:S(2)}) copy-start(bf16[1024,4096]{1,0:T(8,128)(2,1)} %w_ref.5) | copy-start | bytes 25165828
  97.9 7.1 %collective-permute-start.1 = (bf16[256,1024]{1,0:T(8,128)(2,1)}, bf16[256,1024]{1,0:T(8,128)(2,1)S(1)}, u32[]{:S(2)}, u32[]{:S(2)}) collective-permute-start(bf16[256,1024]{1,0:T(8,128)(2,1)} %get-tuple-element.14), channel_id=1, source_target_pairs={{0,1},{1,0},{2,3},{3,2},{4,5},{5,4},{6,7},{7,6},{8,9},{9,8},{10,11... | collective-permute-start | bytes 1572872 | tf_op jit(solution)/shard_map/ppermute | solution.py:323
  98.6 3.4 %copy-start.1 = (bf16[1024,4096]{1,0:T(8,128)(2,1)S(1)}, bf16[1024,4096]{1,0:T(8,128)(2,1)}, u32[]{:S(2)}) copy-start(bf16[1024,4096]{1,0:T(8,128)(2,1)} %w_ref.5) | copy-start | bytes 25165828
  104.9 2.0 %collective-permute-start = (bf16[256,1024]{1,0:T(8,128)(2,1)S(1)}, bf16[256,1024]{1,0:T(8,128)(2,1)S(1)}, u32[]{:S(2)}, u32[]{:S(2)}) collective-permute-start(bf16[256,1024]{1,0:T(8,128)(2,1)S(1)} %get-tuple-element.12), channel_id=1, source_target_pairs={{0,1},{1,0},{2,3},{3,2},{4,5},{5,4},{6,7},{7,6},{8,9},{9,8},{10,11... | collective-permute-start | bytes 1572872 | tf_op jit(solution)/shard_map/ppermute | solution.py:326
  105.2 13.1 %collective-permute-start.2 = (bf16[256,1024]{1,0:T(8,128)(2,1)S(1)}, bf16[256,1024]{1,0:T(8,128)(2,1)S(1)}, u32[]{:S(2)}, u32[]{:S(2)}) collective-permute-start(bf16[256,1024]{1,0:T(8,128)(2,1)S(1)} %add_convert_fusion.1), channel_id=1, source_target_pairs={{0,2},{1,3},{2,0},{3,1},{4,6},{5,7},{6,4},{7,5},{8,10},{9,11},{10,... | collective-permute-start | bytes 1572872 | tf_op jit(solution)/shard_map/ppermute | solution.py:325

commit v2 on v0

v2 whole, which is shorter than its diff:
```python
import jax
import jax.numpy as jnp
from jax import lax
from jax.experimental import pallas as pl
from jax.experimental.pallas import tpu as pltpu
from jax.sharding import PartitionSpec as P

F32 = jnp.float32
BF16 = jnp.bfloat16
I32 = jnp.int32

SLOTS = 6
CHUNKS = 2
EACH = SLOTS // CHUNKS
ROWS = 8
WIDTH = 1024
LANES = EACH * WIDTH // ROWS
NONE = -4.0
FULL = 60 * 1024 * 1024


def pieces(slot):
    whole = WIDTH // LANES
    out = [(j * EACH + slot, 0, j * LANES, LANES) for j in range(whole)]
    rest = WIDTH - whole * LANES
    if rest:
        free = ROWS - whole * EACH
        each = LANES // EACH if free * LANES // EACH == rest and EACH == 3 else rest
        if EACH == 3:
            out += [(whole * EACH + j, slot * each, whole * LANES + j * each, each) for j in range(free)]
        else:
            out += [(whole * EACH + slot // 3, (slot % 3) * rest, whole * LANES, rest)]
    return out


def iota(shape, dim):
    return lax.broadcasted_iota(I32, shape, dim)


def dot(a, b):
    return jnp.dot(a, b, preferred_element_type=F32)


def bits(mask):
    return mask.astype(F32).astype(BF16)


def to_tiles(out_ref, flat_ref, values):
    peers = values.shape[0] // EACH
    for s in range(EACH):
        for row, lane, col, width in pieces(s):
            for w in range(0, width, 128):
                flat_ref[(lane + w) // 128, pl.ds(row, peers, stride=ROWS), :] = values[
                    s * peers : (s + 1) * peers, col + w : col + w + 128
                ]
    for b in range(LANES // 128):
        out_ref[:, b * 128 : (b + 1) * 128] = flat_ref[b].astype(BF16)


def from_tiles(rows_ref, flat_ref, in_ref):
    peers = in_ref.shape[0] // ROWS
    for b in range(LANES // 128):
        flat_ref[b] = in_ref[:, b * 128 : (b + 1) * 128].astype(F32)
    for s in range(EACH):
        for row, lane, col, width in pieces(s):
            for w in range(0, width, 128):
                rows_ref[s * peers : (s + 1) * peers, col + w : col + w + 128] = flat_ref[
                    (lane + w) // 128, pl.ds(row, peers, stride=ROWS), :
                ].astype(BF16)


def slot_keys(ids, capacity):
    experts = capacity.shape[1]
    tokens = ids.shape[1]
    expert = iota((experts, tokens), 0)
    named = (ids[0:1, :] == expert) | (ids[1:2, :] == expert)
    earlier = bits(iota((tokens, tokens), 0) < iota((tokens, tokens), 1))
    rank = dot(bits(named), earlier)
    own = iota((experts, experts), 0) == iota((experts, experts), 1)
    limit = jnp.sum(jnp.where(own, capacity.astype(F32), 0.0), axis=1, keepdims=True)
    return jnp.where(named & (rank < limit), rank, NONE)


def pack_body(ids_ref, cap_ref, tok_ref, w_ref, *refs):
    out_refs, (acc_ref, pick_ref, flat_ref) = refs[:CHUNKS], refs[CHUNKS:]
    step = pl.program_id(0)

    @pl.when(step == 0)
    def _():
        key = slot_keys(ids_ref[...], cap_ref[...])
        peers = key.shape[0]
        for s in range(SLOTS):
            pick_ref[s * peers : (s + 1) * peers, :] = bits(key == float(s))
        acc_ref[...] = dot(tok_ref[...], w_ref[...])

    @pl.when(step > 0)
    def _():
        acc_ref[...] += dot(tok_ref[...], w_ref[...])

    @pl.when(step == pl.num_programs(0) - 1)
    def _():
        sub = acc_ref[...].astype(BF16)
        rows = pick_ref.shape[0] // CHUNKS
        for c in range(CHUNKS):
            to_tiles(out_refs[c], flat_ref, dot(pick_ref[c * rows : (c + 1) * rows, :], sub))


def flat_scratch(rows):
    return pltpu.VMEM((LANES // 128, rows, 128), F32)


def split_and_pack(ids, capacity, tokens, w_split, steps=4):
    count, depth = tokens.shape
    width = w_split.shape[1]
    experts = capacity.shape[1]
    rows = experts * ROWS
    part = depth // steps
    return pl.pallas_call(
        pack_body,
        grid=(steps,),
        in_specs=[
            pl.BlockSpec(ids.shape, lambda i: (0, 0)),
            pl.BlockSpec(capacity.shape, lambda i: (0, 0)),
            pl.BlockSpec((count, part), lambda i: (0, i)),
            pl.BlockSpec((part, width), lambda i: (i, 0)),
        ],
        out_specs=[pl.BlockSpec((rows, LANES), lambda i: (0, 0))] * CHUNKS,
        out_shape=[jax.ShapeDtypeStruct((rows, LANES), BF16)] * CHUNKS,
        scratch_shapes=[pltpu.VMEM((count, width), F32), pltpu.VMEM((experts * SLOTS, count), BF16), flat_scratch(rows)],
        compiler_params=pltpu.CompilerParams(vmem_limit_bytes=FULL),
        name="split_pack",
    )(ids, capacity, tokens, w_split)


def weights_body(ids_ref, cap_ref, q_ref, out_ref):
    ids = ids_ref[...]
    key = slot_keys(ids, cap_ref[...])
    expert = iota(key.shape, 0)
    scale = q_ref[...].astype(F32) / 65536.0
    weight = jnp.where(ids[0:1, :] == expert, scale[0:1, :], 0.0) + jnp.where(ids[1:2, :] == expert, scale[1:2, :], 0.0)
    key, weight = key.T, weight.T
    peers = key.shape[1]
    for s in range(SLOTS):
        out_ref[:, s * peers : (s + 1) * peers] = jnp.where(key == float(s), weight, 0.0).astype(BF16)


def combine_weights(ids, capacity, q):
    return pl.pallas_call(
        weights_body,
        out_shape=jax.ShapeDtypeStruct((ids.shape[1], capacity.shape[1] * SLOTS), BF16),
        compiler_params=pltpu.CompilerParams(vmem_limit_bytes=FULL),
        name="combine_weights",
    )(ids, capacity, q)


def fetch(copies):
    for c in copies:
        c.start()
    return copies


def expert_body(x_hbm, in_hbm, down_hbm, out_ref, x_ref, in_ref, down_ref, rows_ref, act_ref, flat_ref, sems):
    hidden = down_ref.shape[0]
    part = hidden // 4
    copy = pltpu.make_async_copy
    get_x = fetch([copy(x_hbm, x_ref, sems.at[0])])[0]
    get_in = []
    for j in range(4):
        for n, col in enumerate((j * part, hidden + j * part)):
            cols = pl.ds(col, part)
            get_in.append(copy(in_hbm.at[0, :, cols], in_ref.at[:, cols], sems.at[1 + 2 * j + n]))
    fetch(get_in)
    get_down = fetch([copy(down_hbm.at[0], down_ref, sems.at[9])])[0]
    get_x.wait()
    from_tiles(rows_ref, flat_ref, x_ref)
    rows = rows_ref[...]
    for j in range(4):
        get_in[2 * j].wait()
        get_in[2 * j + 1].wait()
        gate = dot(rows, in_ref[:, j * part : (j + 1) * part])
        up = dot(rows, in_ref[:, hidden + j * part : hidden + (j + 1) * part])
        act_ref[:, j * part : (j + 1) * part] = (gate / (1.0 + jnp.exp(-gate)) * up).astype(BF16)
    get_down.wait()
    to_tiles(out_ref, flat_ref, dot(act_ref[...], down_ref[...]))


def expert_rows(tiles, expert_in, expert_out):
    rows = tiles.shape[0]
    slots = rows // ROWS * EACH
    width = expert_in.shape[1]
    hidden = expert_out.shape[1]
    return pl.pallas_call(
        expert_body,
        out_shape=jax.ShapeDtypeStruct((rows, LANES), BF16),
        in_specs=[pl.BlockSpec(memory_space=pltpu.HBM)] * 3,
        scratch_shapes=[
            pltpu.VMEM((rows, LANES), BF16),
            pltpu.VMEM((width, 2 * hidden), BF16),
            pltpu.VMEM((hidden, width), BF16),
            pltpu.VMEM((slots, width), BF16),
            pltpu.VMEM((slots, hidden), BF16),
            flat_scratch(rows),
            pltpu.SemaphoreType.DMA((10,)),
        ],
        compiler_params=pltpu.CompilerParams(vmem_limit_bytes=FULL),
        name="experts",
    )(tiles, expert_in, expert_out)


def part_body(v_ref, b_ref, out_ref, rows_ref, flat_ref):
    from_tiles(rows_ref, flat_ref, b_ref)
    out_ref[...] = dot(v_ref[...], rows_ref[...])


def combine_part(v, back):
    rows = back.shape[0]
    return pl.pallas_call(
        part_body,
        grid=(1,),
        in_specs=[
            pl.BlockSpec((v.shape[0], v.shape[1] // CHUNKS), lambda i: (0, 0)),
            pl.BlockSpec(back.shape, lambda i: (0, 0)),
        ],
        out_specs=pl.BlockSpec((v.shape[0], WIDTH), lambda i: (0, 0)),
        out_shape=jax.ShapeDtypeStruct((v.shape[0], WIDTH), F32),
        scratch_shapes=[pltpu.VMEM((rows // ROWS * EACH, WIDTH), BF16), flat_scratch(rows)],
        compiler_params=pltpu.CompilerParams(vmem_limit_bytes=FULL),
        name="combine_part",
    )(v, back)


def column_block(w_hbm, at, width):
    return w_hbm.at[:, pl.ds(pl.multiple_of(at * width, width), width)]


def combine_body(at_ref, v_hbm, b_hbm, *refs):
    part_hbm, refs = refs[: CHUNKS - 1], refs[CHUNKS - 1 :]
    w_hbm, head_ref, send_ref, v_ref, b_ref, part_ref, w_ref, rows_ref, flat_ref, sems = refs
    width = w_ref.shape[0]
    copy = pltpu.make_async_copy
    get_b = copy(b_hbm, b_ref, sems.at[0])
    get_v = copy(v_hbm.at[:, pl.ds((CHUNKS - 1) * v_ref.shape[1], v_ref.shape[1])], v_ref, sems.at[1])
    get_w = copy(column_block(w_hbm, at_ref[0], width), w_ref, sems.at[2])
    get_part = [copy(p, part_ref.at[n], sems.at[3 + n]) for n, p in enumerate(part_hbm)]
    fetch([get_b, get_v, get_w] + get_part)
    get_b.wait()
    from_tiles(rows_ref, flat_ref, b_ref)
    get_v.wait()
    head = dot(v_ref[...], rows_ref[...])
    for n, get in enumerate(get_part):
        get.wait()
        head += part_ref[n]
    head = head.astype(BF16)
    head_ref[...] = head
    get_w.wait()
    send_ref[...] = dot(head, w_ref[...]).astype(BF16)


def combine_and_merge(at, v, back, part, w_merge):
    tokens = v.shape[0]
    width = w_merge.shape[0]
    rows = back.shape[0]
    return pl.pallas_call(
        combine_body,
        in_specs=[pl.BlockSpec(memory_space=pltpu.SMEM)] + [pl.BlockSpec(memory_space=pltpu.HBM)] * (CHUNKS + 2),
        out_shape=[jax.ShapeDtypeStruct((tokens, width), BF16)] * 2,
        scratch_shapes=[
            pltpu.VMEM((tokens, v.shape[1] // CHUNKS), BF16),
            pltpu.VMEM(back.shape, BF16),
            pltpu.VMEM((max(CHUNKS - 1, 1), tokens, width), F32),
            pltpu.VMEM((width, width), BF16),
            pltpu.VMEM((rows // ROWS * EACH, width), BF16),
            flat_scratch(rows),
            pltpu.SemaphoreType.DMA((3 + CHUNKS,)),
        ],
        compiler_params=pltpu.CompilerParams(vmem_limit_bytes=FULL),
        name="combine_merge",
    )(at, v, back, *part, w_merge)


def merge_body(at_ref, head_ref, w_hbm, far_ref, send_ref, keep_ref, w_ref, sems):
    width = w_ref.shape[1]
    gets = [
        pltpu.make_async_copy(column_block(w_hbm, at_ref[1 + n], width), w_ref.at[n], sems.at[n]) for n in range(3)
    ]
    fetch(gets)
    head = head_ref[...]
    for n, out_ref in enumerate((far_ref, send_ref, keep_ref)):
        gets[n].wait()
        out_ref[...] = dot(head, w_ref[n]).astype(BF16)


def merge_rest(at, head, w_merge):
    tokens, width = head.shape
    whole = pl.BlockSpec((tokens, width), lambda: (0, 0))
    return pl.pallas_call(
        merge_body,
        in_specs=[pl.BlockSpec(memory_space=pltpu.SMEM), whole, pl.BlockSpec(memory_space=pltpu.HBM)],
        out_specs=[whole] * 3,
        out_shape=[jax.ShapeDtypeStruct((tokens, width), BF16)] * 3,
        scratch_shapes=[pltpu.VMEM((3, width, width), BF16), pltpu.SemaphoreType.DMA((3,))],
        compiler_params=pltpu.CompilerParams(vmem_limit_bytes=FULL),
        name="merge_rest",
    )(at, head, w_merge)


def exchange(tiles, axes):
    peers = tiles.shape[0] // ROWS
    return lax.all_to_all(tiles.reshape(peers, ROWS, LANES), axes, split_axis=0, concat_axis=0, tiled=True).reshape(tiles.shape)


def added(a, b):
    return (a.astype(F32) + b.astype(F32)).astype(BF16)


def body(tokens, w_split, w_merge, expert_in, expert_out, expert_ids, combine_q, capacity):
    ids = expert_ids[0].T
    q = combine_q[0].T
    limit = capacity.reshape(1, -1)
    axes = ("seq", "sub")
    tiles = [exchange(t, axes) for t in split_and_pack(ids, limit, tokens, w_split)]
    v = combine_weights(ids, limit, q)
    back = [exchange(expert_rows(t, expert_in, expert_out), axes) for t in tiles]

    me = lax.axis_index("sub")
    core = [(i, i ^ 1) for i in range(4)]
    chip = [(i, i ^ 2) for i in range(4)]
    at = me ^ jnp.array([3, 2, 1, 0], I32)
    part = [combine_part(v, b) for b in back[:-1]]
    head, far_send = combine_and_merge(at, v, back[-1], part, w_merge)
    far_in = lax.ppermute(far_send, "sub", core)
    far_keep, own_send, own_keep = merge_rest(at, head, w_merge)
    cross = lax.ppermute(added(far_keep, far_in), "sub", chip)
    own_in = lax.ppermute(own_send, "sub", core)
    return (own_keep.astype(F32) + own_in.astype(F32) + cross.astype(F32)).astype(BF16)


def solution(mesh):
    in_specs = (
        P("seq", None),
        P(None, "sub"),
        P("sub", None),
        P(("seq", "sub"), None, None),
        P(("seq", "sub"), None, None),
        P("sub", "seq", None),
        P("sub", "seq", None),
        P(),
    )
    out_specs = P("seq", "sub")
    return jax.shard_map(body, mesh=mesh, in_specs=in_specs, out_specs=out_specs, check_vma=False)
```

time: 161 us -> 127 us (0.79)
  blocking collectives: 70.5 us -> 28.2 us
  Pallas kernels: 0 us -> 35.9 us
  local copies, waits for them, and re-layouts: 23.9 us -> 0.95 us
  matrix products: 21.8 us -> 0 us
  waiting for transfers between devices: 29.1 us -> 45.1 us
  starting transfers between devices: 5.72 us -> 12.5 us
  other arithmetic: 8.83 us -> 3.85 us
    all_to_all x2 -> x1, blocking collectives: 70.5 us -> 28.2 us  [exchange(): lax.all_to_all(tiles.reshape(peers, ROWS, LANES), axes, split_axis=0, con...]
    pallas_call x0 -> x7, Pallas kernels: none -> 35.9 us  [the longest x2 12.4 us: expert_rows(): pl.pallas_call(expert_body, out_shape=jax.ShapeDtypeStruct((rows, LANES),...]
    dot_general x4 -> x0, matrix products: 21.8 us -> none  [the longest x1 7.27 us: body(): jnp.dot(chosen, sub_tok, preferred_element_type=jnp.float32)]
    reshape x5 -> x0, local copies, waits for them, and re-layouts: 15 us -> none  [the longest x1 3.73 us: expert_rows(): rows_flat = received.reshape(-1, dims_in[-1])]
    ppermute x0 -> x3, waiting for transfers between devices: none -> 12.7 us  [the longest x1 12.5 us: body(): cross = lax.ppermute(added(far_keep, far_in), 'sub', chip)]
    reduce_sum x3 -> x0, other arithmetic: 8.21 us -> none  [the longest x1 4.33 us: body(): head_out = jnp.sum(weighted, axis=1).astype(jnp.bfloat16)]
    all_to_all x1 -> x3, starting transfers between devices: 5.72 us -> 11.3 us  [exchange(): lax.all_to_all(tiles.reshape(peers, ROWS, LANES), axes, split_axis=0, con...]
    gather x1 -> x0, local copies, waits for them, and re-layouts: 4.34 us -> none  [body(): gathered = returned_rows[jnp.maximum(slot_index, 0)].astype(jnp.float32)]
  transfers between devices with their start and end apart: 1 -> 6, of which waited for: 1 -> 5; matrix products, arithmetic and copies ran while one was open for 0% -> 1% of each run, Pallas kernels for 0% -> 18%
where the time goes in v2:
time: 127 us
  waiting for transfers between devices  45.1 us (36%)
  Pallas kernels  35.9 us (28%)
  blocking collectives  28.2 us (22%)
  starting transfers between devices  12.5 us (10%)
  other arithmetic  3.85 us (3%)
    all_to_all x3, waiting for transfers between devices, exchange(): lax.all_to_all(tiles.reshape(peers, ROWS, LANES), axes, split_axis=0, con...  32.5 us
    all_to_all x1, blocking collectives, exchange(): lax.all_to_all(tiles.reshape(peers, ROWS, LANES), axes, split_axis=0, con...  28.2 us
    ppermute x1, waiting for transfers between devices, body(): cross = lax.ppermute(added(far_keep, far_in), 'sub', chip)  12.5 us
    pallas_call x2, Pallas kernels, expert_rows(): pl.pallas_call(expert_body, out_shape=jax.ShapeDtypeStruct((rows, LANES),...  12.4 us
    all_to_all x3, starting transfers between devices, exchange(): lax.all_to_all(tiles.reshape(peers, ROWS, LANES), axes, split_axis=0, con...  11.3 us
    pallas_call x1, Pallas kernels, split_and_pack(): pl.pallas_call(pack_body, grid=(steps,), in_specs=[pl.BlockSpec(ids.shape...  8.23 us
    pallas_call x1, Pallas kernels, merge_rest(): pl.pallas_call(merge_body, in_specs=[pl.BlockSpec(memory_space=pltpu.SMEM...  5.64 us
    pallas_call x1, Pallas kernels, combine_and_merge(): pl.pallas_call(combine_body, in_specs=[pl.BlockSpec(memory_space=pltpu.SM...  4.81 us
  transfers between devices with their start and end apart: 6, of which 5 were waited for; matrix products, arithmetic and copies ran while one was open for 1% of the time, Pallas kernels for 18%

profile of v2, /device:TPU:1, one launch (start us, length us, event | category | flops | bytes accessed | tf_op | source)
XLA Modules:
  0.0 126.6 jit_solution(17713909831608506749)
XLA Ops:
  0.0 8.2 %split_pack.1 = (bf16[1024,384]{1,0:T(8,128)(2,1)}, bf16[1024,384]{1,0:T(8,128)(2,1)}) custom-call(s32[2,256]{1,0:T(2,128)} %bitcast.23, s32[1,128]{1,0:T(1,128)} %bitcast.26, bf16[256,4096]{1,0:T(8,128)(2,1)} %tok_ref.1, bf16[4096,1024]{1,0:T(8,128)(2,1)} %w_ref.1), custom_call_target="tpu_custom_call" | custom-call | tf_op jit(solution)/shard_map/split_pack/pallas_call | solution.py:118
  8.2 28.2 %all_to_all.20 = bf16[128,8,384]{2,1,0:T(8,128)(2,1)} all-to-all(bf16[128,8,384]{2,1,0:T(8,128)(2,1)} %bitcast.22), channel_id=1, replica_groups=mesh['seq'=32,'sub'=4] {'seq','sub'}, dimensions={0} | all-to-all | bytes 1572864 | tf_op jit(solution)/shard_map/all_to_all | solution.py:309
  36.4 3.8 %all-to-all-start = ((bf16[128,8,384]{2,1,0:T(8,128)(2,1)}), bf16[128,8,384]{2,1,0:T(8,128)(2,1)S(1)}, u32[]{:S(2)}, u32[]{:S(2)}) async-start(bf16[128,8,384]{2,1,0:T(8,128)(2,1)} %bitcast.21), calls=%async_computation | async-start | bytes 1572864 | tf_op jit(solution)/shard_map/all_to_all | solution.py:309
  40.2 6.2 %experts.3 = bf16[1024,384]{1,0:T(8,128)(2,1)} custom-call(bf16[1024,384]{1,0:T(8,128)(2,1)} %bitcast.20, bf16[1,1024,2048]{2,1,0:T(8,128)(2,1)} %in_hbm.3, bf16[1,1024,1024]{2,1,0:T(8,128)(2,1)} %down_hbm.3), custom_call_target="tpu_custom_call" | custom-call | tf_op jit(solution)/shard_map/experts/pallas_call | solution.py:192
  46.4 10.5 %all-to-all-done = bf16[128,8,384]{2,1,0:T(8,128)(2,1)S(1)} async-done(((bf16[128,8,384]{2,1,0:T(8,128)(2,1)}), bf16[128,8,384]{2,1,0:T(8,128)(2,1)S(1)}, u32[]{:S(2)}, u32[]{:S(2)}) %all-to-all-start) | async-done | bytes 786464 | tf_op jit(solution)/shard_map/all_to_all | solution.py:309
  57.0 0.0 copy-start.2
  57.0 3.8 %all-to-all-start.3 = ((bf16[128,8,384]{2,1,0:T(8,128)(2,1)}), bf16[128,8,384]{2,1,0:T(8,128)(2,1)S(1)}, u32[]{:S(2)}, u32[]{:S(2)}) async-start(bf16[128,8,384]{2,1,0:T(8,128)(2,1)} %bitcast.19), calls=%async_computation.3 | async-start | bytes 1572864 | tf_op jit(solution)/shard_map/all_to_all | solution.py:309
  60.7 0.0 copy-done.2
  60.7 0.0 copy-start.3
  60.7 6.2 %experts.2 = bf16[1024,384]{1,0:T(8,128)(2,1)} custom-call(bf16[1024,384]{1,0:T(8,128)(2,1)} %bitcast.18, bf16[1,1024,2048]{2,1,0:T(8,128)(2,1)} %in_hbm.3, bf16[1,1024,1024]{2,1,0:T(8,128)(2,1)} %down_hbm.3), custom_call_target="tpu_custom_call" | custom-call | tf_op jit(solution)/shard_map/experts/pallas_call | solution.py:192
  67.0 10.5 %all-to-all-done.3 = bf16[128,8,384]{2,1,0:T(8,128)(2,1)S(1)} async-done(((bf16[128,8,384]{2,1,0:T(8,128)(2,1)}), bf16[128,8,384]{2,1,0:T(8,128)(2,1)S(1)}, u32[]{:S(2)}, u32[]{:S(2)}) %all-to-all-start.3) | async-done | bytes 786464 | tf_op jit(solution)/shard_map/all_to_all | solution.py:309
  77.5 0.0 copy-start
  77.5 3.8 %all-to-all-start.1 = ((bf16[128,8,384]{2,1,0:T(8,128)(2,1)}), bf16[128,8,384]{2,1,0:T(8,128)(2,1)S(1)}, u32[]{:S(2)}, u32[]{:S(2)}) async-start(bf16[128,8,384]{2,1,0:T(8,128)(2,1)} %bitcast.17), calls=%async_computation.1 | async-start | bytes 1572864 | tf_op jit(solution)/shard_map/all_to_all | solution.py:309
  81.3 1.8 %combine_weights.1.v_ref.v_hbm = bf16[256,768]{1,0:T(8,128)(2,1)} custom-call(s32[2,256]{1,0:T(2,128)} %bitcast.24, s32[1,128]{1,0:T(1,128)} %bitcast.27, s32[2,256]{1,0:T(2,128)} %bitcast.25), custom_call_target="tpu_custom_call" | custom-call | tf_op jit(solution)/shard_map/combine_weights/pallas_call | solution.py:148
  83.1 0.0 copy-done.3
  83.1 0.5 broadcast_xor_fusion.at_ref
  83.6 0.0 copy-done
  83.6 3.0 %combine_part.1.refs_0_ = f32[256,1024]{1,0:T(8,128)} custom-call(bf16[256,768]{1,0:T(8,128)(2,1)} %combine_weights.1.v_ref.v_hbm, bf16[1024,384]{1,0:T(8,128)(2,1)} %bitcast.15), custom_call_target="tpu_custom_call" | custom-call | tf_op jit(solution)/shard_map/combine_part/pallas_call | solution.py:217
  86.6 11.4 %all-to-all-done.1 = bf16[128,8,384]{2,1,0:T(8,128)(2,1)S(1)} async-done(((bf16[128,8,384]{2,1,0:T(8,128)(2,1)}), bf16[128,8,384]{2,1,0:T(8,128)(2,1)S(1)}, u32[]{:S(2)}, u32[]{:S(2)}) %all-to-all-start.1) | async-done | bytes 786464 | tf_op jit(solution)/shard_map/all_to_all | solution.py:309
  98.0 0.0 copy-start.1
  98.0 0.9 copy-done.1
  98.9 4.8 %combine_merge.1 = (bf16[256,1024]{1,0:T(8,128)(2,1)}, bf16[256,1024]{1,0:T(8,128)(2,1)}) custom-call(s32[4]{0:T(128)} %broadcast_xor_fusion.at_ref, bf16[256,768]{1,0:T(8,128)(2,1)} %combine_weights.1.v_ref.v_hbm, bf16[1024,384]{1,0:T(8,128)(2,1)} %bitcast.16, f32[256,1024]{1,0:T(8,128)} %combine_part.1.refs_0_, bf16[1024,4096]{1,0:T(8,128)(2,1)} %w_hbm.1), custom_call_target="tpu_custom_call" | custom-call | tf_op jit(solution)/shard_map/combine_merge/pallas_call | solution.py:263
  103.8 0.4 collective-permute-start.1
  104.2 5.6 %merge_rest.1 = (bf16[256,1024]{1,0:T(8,128)(2,1)}, bf16[256,1024]{1,0:T(8,128)(2,1)}, bf16[256,1024]{1,0:T(8,128)(2,1)}) custom-call(s32[4]{0:T(128)} %broadcast_xor_fusion.at_ref, bf16[256,1024]{1,0:T(8,128)(2,1)} %get-tuple-element.14.head_ref, bf16[1024,4096]{1,0:T(8,128)(2,1)} %w_hbm.1), custom_call_target="tpu_custom_call" | custom-call | tf_op jit(solution)/shard_map/merge_rest/pallas_call | solution.py:296
  109.8 0.3 collective-permute-start
  110.1 0.0 collective-permute-done.1
  110.1 1.2 add_convert_fusion.1
  111.3 0.6 collective-permute-start.2
  111.9 0.1 collective-permute-done
  112.0 12.5 %collective-permute-done.2 = bf16[256,1024]{1,0:T(8,128)(2,1)S(1)} collective-permute-done((bf16[256,1024]{1,0:T(8,128)(2,1)S(1)}, bf16[256,1024]{1,0:T(8,128)(2,1)S(1)}, u32[]{:S(2)}, u32[]{:S(2)}) %collective-permute-start.2) | collective-permute-done | bytes 524320 | tf_op jit(solution)/shard_map/ppermute | solution.py:333
  124.5 2.1 %add_convert_fusion = bf16[256,1024]{1,0:T(8,128)(2,1)} fusion(bf16[256,1024]{1,0:T(8,128)(2,1)S(1)} %collective-permute-done.2, bf16[256,1024]{1,0:T(8,128)(2,1)S(1)} %collective-permute-done, bf16[256,1024]{1,0:T(8,128)(2,1)} %get-tuple-element.15), kind=kLoop, calls=%fused_computation | loop fusion | flops 1572864 | bytes 2097152 | tf_op jit(solution)/shard_map/convert_element_type | solution.py:335
Async XLA Ops:
  36.4 20.5 %all-to-all-start = ((bf16[128,8,384]{2,1,0:T(8,128)(2,1)}), bf16[128,8,384]{2,1,0:T(8,128)(2,1)S(1)}, u32[]{:S(2)}, u32[]{:S(2)}) async-start(bf16[128,8,384]{2,1,0:T(8,128)(2,1)} %bitcast.21), calls=%async_computation | async-start | bytes 1572864 | tf_op jit(solution)/shard_map/all_to_all | solution.py:309
  57.0 3.8 %copy-start.2 = (bf16[128,8,384]{2,1,0:T(8,128)(2,1)}, bf16[128,8,384]{2,1,0:T(8,128)(2,1)S(1)}, u32[]{:S(2)}) copy-start(bf16[128,8,384]{2,1,0:T(8,128)(2,1)S(1)} %all-to-all-done) | copy-start | bytes 2359300
  57.0 20.5 %all-to-all-start.3 = ((bf16[128,8,384]{2,1,0:T(8,128)(2,1)}), bf16[128,8,384]{2,1,0:T(8,128)(2,1)S(1)}, u32[]{:S(2)}, u32[]{:S(2)}) async-start(bf16[128,8,384]{2,1,0:T(8,128)(2,1)} %bitcast.19), calls=%async_computation.3 | async-start | bytes 1572864 | tf_op jit(solution)/shard_map/all_to_all | solution.py:309
  60.7 22.3 %copy-start.3 = (s32[4]{0:T(128)S(1)}, s32[4]{0:T(128)}, u32[]{:S(2)}) copy-start(s32[4]{0:T(128)} %constant.6.clone) | copy-start | bytes 52
  77.5 6.1 %copy-start = (bf16[128,8,384]{2,1,0:T(8,128)(2,1)}, bf16[128,8,384]{2,1,0:T(8,128)(2,1)S(1)}, u32[]{:S(2)}) copy-start(bf16[128,8,384]{2,1,0:T(8,128)(2,1)S(1)} %all-to-all-done.3) | copy-start | bytes 2359300
  77.5 20.5 %all-to-all-start.1 = ((bf16[128,8,384]{2,1,0:T(8,128)(2,1)}), bf16[128,8,384]{2,1,0:T(8,128)(2,1)S(1)}, u32[]{:S(2)}, u32[]{:S(2)}) async-start(bf16[128,8,384]{2,1,0:T(8,128)(2,1)} %bitcast.17), calls=%async_computation.1 | async-start | bytes 1572864 | tf_op jit(solution)/shard_map/all_to_all | solution.py:309
  98.0 0.9 copy-start.1
  103.8 6.3 %collective-permute-start.1 = (bf16[256,1024]{1,0:T(8,128)(2,1)}, bf16[256,1024]{1,0:T(8,128)(2,1)S(1)}, u32[]{:S(2)}, u32[]{:S(2)}) collective-permute-start(bf16[256,1024]{1,0:T(8,128)(2,1)} %get-tuple-element.18), channel_id=1, source_target_pairs={{0,1},{1,0},{2,3},{3,2},{4,5},{5,4},{6,7},{7,6},{8,9},{9,8},{10,11... | collective-permute-start | bytes 1572872 | tf_op jit(solution)/shard_map/ppermute | solution.py:331
  109.8 2.2 %collective-permute-start = (bf16[256,1024]{1,0:T(8,128)(2,1)}, bf16[256,1024]{1,0:T(8,128)(2,1)S(1)}, u32[]{:S(2)}, u32[]{:S(2)}) collective-permute-start(bf16[256,1024]{1,0:T(8,128)(2,1)} %get-tuple-element.16), channel_id=1, source_target_pairs={{0,1},{1,0},{2,3},{3,2},{4,5},{5,4},{6,7},{7,6},{8,9},{9,8},{10,11... | collective-permute-start | bytes 1572872 | tf_op jit(solution)/shard_map/ppermute | solution.py:334
  111.3 13.2 %collective-permute-start.2 = (bf16[256,1024]{1,0:T(8,128)(2,1)S(1)}, bf16[256,1024]{1,0:T(8,128)(2,1)S(1)}, u32[]{:S(2)}, u32[]{:S(2)}) collective-permute-start(bf16[256,1024]{1,0:T(8,128)(2,1)S(1)} %add_convert_fusion.1), channel_id=1, source_target_pairs={{0,2},{1,3},{2,0},{3,1},{4,6},{5,7},{6,4},{7,5},{8,10},{9,11},{10,... | collective-permute-start | bytes 1572872 | tf_op jit(solution)/shard_map/ppermute | solution.py:333

commit v3 on v0

v3 whole, which is shorter than its diff:
```python
import jax
import jax.numpy as jnp
from jax import lax
from jax.experimental import pallas as pl
from jax.experimental.pallas import tpu as pltpu
from jax.sharding import PartitionSpec as P

F32 = jnp.float32
BF16 = jnp.bfloat16
I32 = jnp.int32

SLOTS = 6
ROWS = 8
WIDTH = 1024
LANES = SLOTS * WIDTH // ROWS
NONE = -4.0


def pieces(slot):
    rest = WIDTH - LANES
    return [(slot, 0, 0, LANES), (SLOTS + slot // 3, slot % 3 * rest, LANES, rest)]


def iota(shape, dim):
    return lax.broadcasted_iota(I32, shape, dim)


def dot(a, b):
    return jnp.dot(a, b, preferred_element_type=F32)


def bits(mask):
    return mask.astype(F32).astype(BF16)


def to_flat(flat_ref, values, first=0):
    peers = values.shape[0] // SLOTS
    last = first + values.shape[1]
    for s in range(SLOTS):
        for row, lane, col, width in pieces(s):
            for w in range(0, width, 128):
                if first <= col + w < last:
                    at = col + w - first
                    flat_ref[(lane + w) // 128, pl.ds(row, peers, stride=ROWS), :] = values[
                        s * peers : (s + 1) * peers, at : at + 128
                    ]


def from_flat(out_ref, flat_ref):
    for b in range(LANES // 128):
        out_ref[:, b * 128 : (b + 1) * 128] = flat_ref[b].astype(BF16)


def from_tiles(rows_ref, flat_ref, in_ref):
    peers = in_ref.shape[0] // ROWS
    for b in range(LANES // 128):
        flat_ref[b] = in_ref[:, b * 128 : (b + 1) * 128].astype(F32)
    for s in range(SLOTS):
        for row, lane, col, width in pieces(s):
            for w in range(0, width, 128):
                rows_ref[s * peers : (s + 1) * peers, col + w : col + w + 128] = flat_ref[
                    (lane + w) // 128, pl.ds(row, peers, stride=ROWS), :
                ].astype(BF16)


def slot_keys(ids, capacity):
    experts = capacity.shape[1]
    tokens = ids.shape[1]
    expert = iota((experts, tokens), 0)
    named = (ids[0:1, :] == expert) | (ids[1:2, :] == expert)
    earlier = bits(iota((tokens, tokens), 0) < iota((tokens, tokens), 1))
    rank = dot(bits(named), earlier)
    own = iota((experts, experts), 0) == iota((experts, experts), 1)
    limit = jnp.sum(jnp.where(own, capacity.astype(F32), 0.0), axis=1, keepdims=True)
    return jnp.where(named & (rank < limit), rank, NONE)


def combine_weights(v_ref, ids, key, q):
    expert = iota(key.shape, 0)
    scale = q.astype(F32) / 65536.0
    weight = jnp.where(ids[0:1, :] == expert, scale[0:1, :], 0.0) + jnp.where(ids[1:2, :] == expert, scale[1:2, :], 0.0)
    key, weight = key.T, weight.T
    peers = key.shape[1]
    for s in range(SLOTS):
        v_ref[:, s * peers : (s + 1) * peers] = jnp.where(key == float(s), weight, 0.0).astype(BF16)


BLOCK = 256
ONCHIP = pl.BlockSpec(memory_space=pltpu.VMEM)
REMOTE = pl.BlockSpec(memory_space=pltpu.HBM)


def fetch(copies):
    for c in copies:
        c.start()
    return copies


def flat_scratch(rows):
    return pltpu.VMEM((LANES // 128, rows, 128), F32)


def pack_body(ids_ref, cap_ref, q_ref, tok_hbm, w_hbm, out_ref, v_ref, tok_ref, w_ref, pick_ref, flat_ref, sems):
    blocks = w_ref.shape[1] // BLOCK
    get_tok = pltpu.make_async_copy(tok_hbm, tok_ref, sems.at[blocks])
    gets = []
    for n in range(blocks):
        cols = pl.ds(n * BLOCK, BLOCK)
        gets.append(pltpu.make_async_copy(w_hbm.at[:, cols], w_ref.at[:, cols], sems.at[n]))
    fetch([get_tok] + gets)
    ids = ids_ref[...]
    key = slot_keys(ids, cap_ref[...])
    peers = key.shape[0]
    for s in range(SLOTS):
        pick_ref[s * peers : (s + 1) * peers, :] = bits(key == float(s))
    combine_weights(v_ref, ids, key, q_ref[...])
    get_tok.wait()
    for n in range(blocks):
        gets[n].wait()
        sub = dot(tok_ref[...], w_ref[:, n * BLOCK : (n + 1) * BLOCK]).astype(BF16)
        to_flat(flat_ref, dot(pick_ref[...], sub), n * BLOCK)
    from_flat(out_ref, flat_ref)


def split_and_pack(ids, capacity, q, tokens, w_split):
    count = tokens.shape[0]
    experts = capacity.shape[1]
    rows = experts * ROWS
    return pl.pallas_call(
        pack_body,
        in_specs=[ONCHIP] * 3 + [REMOTE] * 2,
        out_specs=[ONCHIP] * 2,
        out_shape=[
            jax.ShapeDtypeStruct((rows, LANES), BF16),
            jax.ShapeDtypeStruct((count, experts * SLOTS), BF16),
        ],
        scratch_shapes=[
            pltpu.VMEM(tokens.shape, BF16),
            pltpu.VMEM(w_split.shape, BF16),
            pltpu.VMEM((experts * SLOTS, count), BF16),
            flat_scratch(rows),
            pltpu.SemaphoreType.DMA((w_split.shape[1] // BLOCK + 1,)),
        ],
        compiler_params=pltpu.CompilerParams(vmem_limit_bytes=62 << 20),
        name="split_pack",
    )(ids, capacity, q, tokens, w_split)


def expert_body(x_ref, in_hbm, down_hbm, out_ref, in_ref, down_ref, rows_ref, act_ref, flat_ref, sems):
    hidden, width = down_ref.shape
    steps = hidden // BLOCK
    gets = []
    for j in range(steps):
        for n, col in enumerate((j * BLOCK, hidden + j * BLOCK)):
            cols = pl.ds(col, BLOCK)
            gets.append(pltpu.make_async_copy(in_hbm.at[0, :, cols], in_ref.at[:, cols], sems.at[2 * j + n]))
    gets.append(pltpu.make_async_copy(down_hbm.at[0], down_ref, sems.at[2 * steps]))
    fetch(gets)
    from_tiles(rows_ref, flat_ref, x_ref)
    rows = rows_ref[...]
    for j in range(steps):
        gets[2 * j].wait()
        gets[2 * j + 1].wait()
        cols = slice(j * BLOCK, (j + 1) * BLOCK)
        gate = dot(rows, in_ref[:, cols])
        up = dot(rows, in_ref[:, hidden + j * BLOCK : hidden + (j + 1) * BLOCK])
        act_ref[:, cols] = (gate / (1.0 + jnp.exp(-gate)) * up).astype(BF16)
    gets[2 * steps].wait()
    for j in range(0, width, BLOCK):
        to_flat(flat_ref, dot(act_ref[...], down_ref[:, j : j + BLOCK]), j)
    from_flat(out_ref, flat_ref)


def expert_rows(tiles, expert_in, expert_out):
    rows = tiles.shape[0]
    slots = rows // ROWS * SLOTS
    width = expert_in.shape[1]
    hidden = expert_out.shape[1]
    return pl.pallas_call(
        expert_body,
        in_specs=[ONCHIP, REMOTE, REMOTE],
        out_specs=ONCHIP,
        out_shape=jax.ShapeDtypeStruct((rows, LANES), BF16),
        scratch_shapes=[
            pltpu.VMEM((width, 2 * hidden), BF16),
            pltpu.VMEM((hidden, width), BF16),
            pltpu.VMEM((slots, width), BF16),
            pltpu.VMEM((slots, hidden), BF16),
            flat_scratch(rows),
            pltpu.SemaphoreType.DMA((2 * hidden // BLOCK + 1,)),
        ],
        compiler_params=pltpu.CompilerParams(vmem_limit_bytes=60 << 20),
        name="experts",
    )(tiles, expert_in, expert_out)


def column_blocks(w_hbm, w_ref, at, sems):
    width = w_hbm.shape[0]
    return fetch(
        [
            pltpu.make_async_copy(w_hbm.at[:, pl.ds(pl.multiple_of(a * width, width), width)], w_ref.at[n], sems.at[n])
            for n, a in enumerate(at)
        ]
    )


def combine_body(at_ref, v_ref, b_ref, w_hbm, head_ref, send_ref, w_ref, rows_ref, flat_ref, sems):
    (get,) = column_blocks(w_hbm, w_ref, [at_ref[0]], sems)
    from_tiles(rows_ref, flat_ref, b_ref)
    head = dot(v_ref[...], rows_ref[...]).astype(BF16)
    head_ref[...] = head
    get.wait()
    send_ref[...] = dot(head, w_ref[0]).astype(BF16)


MERGE = pltpu.CompilerParams(vmem_limit_bytes=48 << 20)


def combine_and_merge(at, v, back, w_merge):
    tokens = v.shape[0]
    width = w_merge.shape[0]
    rows = back.shape[0]
    return pl.pallas_call(
        combine_body,
        in_specs=[pl.BlockSpec(memory_space=pltpu.SMEM), ONCHIP, ONCHIP, REMOTE],
        out_specs=[ONCHIP] * 2,
        out_shape=[jax.ShapeDtypeStruct((tokens, width), BF16)] * 2,
        scratch_shapes=[
            pltpu.VMEM((1, width, width), BF16),
            pltpu.VMEM((rows // ROWS * SLOTS, width), BF16),
            flat_scratch(rows),
            pltpu.SemaphoreType.DMA((1,)),
        ],
        compiler_params=MERGE,
        name="combine_merge",
    )(at, v, back, w_merge)


def merge_body(at_ref, head_ref, w_hbm, far_ref, send_ref, keep_ref, w_ref, sems):
    gets = column_blocks(w_hbm, w_ref, [at_ref[n] for n in (1, 2, 3)], sems)
    head = head_ref[...]
    for n, out_ref in enumerate((far_ref, send_ref, keep_ref)):
        gets[n].wait()
        out_ref[...] = dot(head, w_ref[n]).astype(BF16)


def merge_rest(at, head, w_merge):
    width = w_merge.shape[0]
    return pl.pallas_call(
        merge_body,
        in_specs=[pl.BlockSpec(memory_space=pltpu.SMEM), ONCHIP, REMOTE],
        out_specs=[ONCHIP] * 3,
        out_shape=[jax.ShapeDtypeStruct(head.shape, BF16)] * 3,
        scratch_shapes=[pltpu.VMEM((3, width, width), BF16), pltpu.SemaphoreType.DMA((3,))],
        compiler_params=MERGE,
        name="merge_rest",
    )(at, head, w_merge)


def exchange(tiles, axes):
    peers = tiles.shape[0] // ROWS
    return lax.all_to_all(tiles.reshape(peers, ROWS, LANES), axes, split_axis=0, concat_axis=0, tiled=True).reshape(tiles.shape)


def added(a, b):
    return (a.astype(F32) + b.astype(F32)).astype(BF16)


def body(tokens, w_split, w_merge, expert_in, expert_out, expert_ids, combine_q, capacity):
    ids = expert_ids[0].T
    q = combine_q[0].T
    limit = capacity.reshape(1, -1)
    axes = ("seq", "sub")
    packed, v = split_and_pack(ids, limit, q, tokens, w_split)
    tiles = exchange(packed, axes)
    back = exchange(expert_rows(tiles, expert_in, expert_out), axes)

    me = lax.axis_index("sub")
    core = [(i, i ^ 1) for i in range(4)]
    chip = [(i, i ^ 2) for i in range(4)]
    at = me ^ jnp.array([3, 2, 1, 0], I32)
    head, far_send = combine_and_merge(at, v, back, w_merge)
    far_in = lax.ppermute(far_send, "sub", core)
    far_keep, own_send, own_keep = merge_rest(at, head, w_merge)
    cross = lax.ppermute(added(far_keep, far_in), "sub", chip)
    own_in = lax.ppermute(own_send, "sub", core)
    return (own_keep.astype(F32) + own_in.astype(F32) + cross.astype(F32)).astype(BF16)


def solution(mesh):
    in_specs = (
        P("seq", None),
        P(None, "sub"),
        P("sub", None),
        P(("seq", "sub"), None, None),
        P(("seq", "sub"), None, None),
        P("sub", "seq", None),
        P("sub", "seq", None),
        P(),
    )
    out_specs = P("seq", "sub")
    return jax.shard_map(body, mesh=mesh, in_specs=in_specs, out_specs=out_specs, check_vma=False)
```

time: 161 us -> 109 us (0.68)
  blocking collectives: 70.5 us -> 36.3 us
  Pallas kernels: 0 us -> 27.9 us
  local copies, waits for them, and re-layouts: 23.9 us -> 0.01 us
  matrix products: 21.8 us -> 0 us
  waiting for transfers between devices: 29.1 us -> 37.4 us
  other arithmetic: 8.83 us -> 1.26 us
    all_to_all x2 -> x1, blocking collectives: 70.5 us -> 36.3 us  [exchange(): lax.all_to_all(tiles.reshape(peers, ROWS, LANES), axes, split_axis=0, con...]
    pallas_call x0 -> x4, Pallas kernels: none -> 27.9 us  [the longest x1 10.5 us: split_and_pack(): pl.pallas_call(pack_body, in_specs=[ONCHIP] * 3 + [REMOTE] * 2, out_specs...]
    dot_general x4 -> x0, matrix products: 21.8 us -> none  [the longest x1 7.27 us: body(): jnp.dot(chosen, sub_tok, preferred_element_type=jnp.float32)]
    reshape x5 -> x0, local copies, waits for them, and re-layouts: 15 us -> none  [the longest x1 3.73 us: expert_rows(): rows_flat = received.reshape(-1, dims_in[-1])]
    ppermute x0 -> x3, waiting for transfers between devices: none -> 12.6 us  [the longest x1 11.4 us: body(): cross = lax.ppermute(added(far_keep, far_in), 'sub', chip)]
    reduce_sum x3 -> x0, other arithmetic: 8.21 us -> none  [the longest x1 4.33 us: body(): head_out = jnp.sum(weighted, axis=1).astype(jnp.bfloat16)]
    gather x1 -> x0, local copies, waits for them, and re-layouts: 4.34 us -> none  [body(): gathered = returned_rows[jnp.maximum(slot_index, 0)].astype(jnp.float32)]
    all_to_all x1, waiting for transfers between devices: 29.1 us -> 24.8 us  [exchange(): lax.all_to_all(tiles.reshape(peers, ROWS, LANES), axes, split_axis=0, con...]
  transfers between devices with their start and end apart: 1 -> 4, of which waited for: 1 -> 3; matrix products, arithmetic and copies ran while one was open for 0% -> 0% of each run, Pallas kernels for 0% -> 4%
where the time goes in v3:
time: 109 us
  waiting for transfers between devices  37.4 us (34%)
  blocking collectives  36.3 us (33%)
  Pallas kernels  27.9 us (26%)
  starting transfers between devices  5.62 us (5%)
  other arithmetic  1.26 us (1%)
    all_to_all x1, blocking collectives, exchange(): lax.all_to_all(tiles.reshape(peers, ROWS, LANES), axes, split_axis=0, con...  36.3 us
    all_to_all x1, waiting for transfers between devices, exchange(): lax.all_to_all(tiles.reshape(peers, ROWS, LANES), axes, split_axis=0, con...  24.8 us
    ppermute x1, waiting for transfers between devices, body(): cross = lax.ppermute(added(far_keep, far_in), 'sub', chip)  11.4 us
    pallas_call x1, Pallas kernels, split_and_pack(): pl.pallas_call(pack_body, in_specs=[ONCHIP] * 3 + [REMOTE] * 2, out_specs...  10.5 us
    pallas_call x1, Pallas kernels, expert_rows(): pl.pallas_call(expert_body, in_specs=[ONCHIP, REMOTE, REMOTE], out_specs=...  10.1 us
    pallas_call x1, Pallas kernels, merge_rest(): pl.pallas_call(merge_body, in_specs=[pl.BlockSpec(memory_space=pltpu.SMEM...  4.3 us
    all_to_all x1, starting transfers between devices, exchange(): lax.all_to_all(tiles.reshape(peers, ROWS, LANES), axes, split_axis=0, con...  4.27 us
    pallas_call x1, Pallas kernels, combine_and_merge(): pl.pallas_call(combine_body, in_specs=[pl.BlockSpec(memory_space=pltpu.SM...  2.92 us
  transfers between devices with their start and end apart: 4, of which 3 were waited for; matrix products, arithmetic and copies ran while one was open for 0% of the time, Pallas kernels for 4%

profile of v3, /device:TPU:1, one launch (start us, length us, event | category | flops | bytes accessed | tf_op | source)
XLA Modules:
  0.0 108.6 jit_solution(15096908910402149453)
XLA Ops:
  0.0 10.5 %split_pack.1 = (bf16[1024,768]{1,0:T(8,128)(2,1)}, bf16[256,768]{1,0:T(8,128)(2,1)}) custom-call(s32[2,256]{1,0:T(2,128)} %bitcast.15, s32[1,128]{1,0:T(1,128)} %bitcast.17, s32[2,256]{1,0:T(2,128)} %bitcast.16, bf16[256,4096]{1,0:T(8,128)(2,1)} %tok_hbm.1, bf16[4096,1024]{1,0:T(8,128)(2,1)} %w_hbm.3), custom_call_target="tpu_custom_call" | custom-call | tf_op jit(solution)/shard_map/split_pack/pallas_call | solution.py:129
  10.5 36.3 %all_to_all.10 = bf16[128,8,768]{2,1,0:T(8,128)(2,1)} all-to-all(bf16[128,8,768]{2,1,0:T(8,128)(2,1)} %bitcast.14), channel_id=1, replica_groups=mesh['seq'=32,'sub'=4] {'seq','sub'}, dimensions={0} | all-to-all | bytes 3145728 | tf_op jit(solution)/shard_map/all_to_all | solution.py:262
  46.8 10.1 %experts.1 = bf16[1024,768]{1,0:T(8,128)(2,1)} custom-call(bf16[1024,768]{1,0:T(8,128)(2,1)} %bitcast.13, bf16[1,1024,2048]{2,1,0:T(8,128)(2,1)} %in_hbm.1, bf16[1,1024,1024]{2,1,0:T(8,128)(2,1)} %down_hbm.1), custom_call_target="tpu_custom_call" | custom-call | tf_op jit(solution)/shard_map/experts/pallas_call | solution.py:179
  57.0 0.0 copy-start.1
  57.0 0.0 copy-start
  57.0 4.3 %all-to-all-start.1 = ((bf16[128,8,768]{2,1,0:T(8,128)(2,1)}), bf16[128,8,768]{2,1,0:T(8,128)(2,1)S(1)}, u32[]{:S(2)}, u32[]{:S(2)}) async-start(bf16[128,8,768]{2,1,0:T(8,128)(2,1)} %bitcast.12), calls=%async_computation.1 | async-start | bytes 3145728 | tf_op jit(solution)/shard_map/all_to_all | solution.py:262
  61.3 0.0 copy-done.1
  61.3 24.8 %all-to-all-done.1 = bf16[128,8,768]{2,1,0:T(8,128)(2,1)S(1)} async-done(((bf16[128,8,768]{2,1,0:T(8,128)(2,1)}), bf16[128,8,768]{2,1,0:T(8,128)(2,1)S(1)}, u32[]{:S(2)}, u32[]{:S(2)}) %all-to-all-start.1) | async-done | bytes 1572896 | tf_op jit(solution)/shard_map/all_to_all | solution.py:262
  86.1 0.0 copy-done
  86.2 2.9 %combine_merge.1 = (bf16[256,1024]{1,0:T(8,128)(2,1)S(1)}, bf16[256,1024]{1,0:T(8,128)(2,1)S(1)}) custom-call(s32[4]{0:T(128)S(1)} %broadcast_xor_fusion.at_ref, bf16[256,768]{1,0:T(8,128)(2,1)S(1)} %copy-done, bf16[1024,768]{1,0:T(8,128)(2,1)S(1)} %bitcast.11, bf16[1024,4096]{1,0:T(8,128)(2,1)} %w_hbm.5), custom_call_target="tpu_custom_call" | custom-call | tf_op jit(solution)/shard_map/combine_merge/pallas_call | solution.py:223
  89.1 0.8 collective-permute-start.1
  89.8 4.3 %merge_rest.1 = (bf16[256,1024]{1,0:T(8,128)(2,1)S(1)}, bf16[256,1024]{1,0:T(8,128)(2,1)S(1)}, bf16[256,1024]{1,0:T(8,128)(2,1)S(1)}) custom-call(s32[4]{0:T(128)S(1)} %broadcast_xor_fusion.at_ref, bf16[256,1024]{1,0:T(8,128)(2,1)S(1)} %get-tuple-element.14.head_ref, bf16[1024,4096]{1,0:T(8,128)(2,1)} %w_hbm.5), custom_call_target="tpu_custom_call" | custom-call | tf_op jit(solution)/shard_map/merge_rest/pallas_call | solution.py:249
  94.1 0.1 collective-permute-start
  94.2 0.0 collective-permute-done.1
  94.2 0.2 add_convert_fusion.1
  94.4 0.5 collective-permute-start.2
  94.9 1.2 %collective-permute-done = bf16[256,1024]{1,0:T(8,128)(2,1)S(1)} collective-permute-done((bf16[256,1024]{1,0:T(8,128)(2,1)S(1)}, bf16[256,1024]{1,0:T(8,128)(2,1)S(1)}, u32[]{:S(2)}, u32[]{:S(2)}) %collective-permute-start) | collective-permute-done | bytes 524320 | tf_op jit(solution)/shard_map/ppermute | solution.py:286
  96.1 11.4 %collective-permute-done.2 = bf16[256,1024]{1,0:T(8,128)(2,1)S(1)} collective-permute-done((bf16[256,1024]{1,0:T(8,128)(2,1)S(1)}, bf16[256,1024]{1,0:T(8,128)(2,1)S(1)}, u32[]{:S(2)}, u32[]{:S(2)}) %collective-permute-start.2) | collective-permute-done | bytes 524320 | tf_op jit(solution)/shard_map/ppermute | solution.py:285
  107.5 1.1 add_convert_fusion
  (1 shorter events, 0.0 us)
Async XLA Ops:
  57.0 4.3 %copy-start.1 = (s32[4]{0:T(128)S(1)}, s32[4]{0:T(128)}, u32[]{:S(2)}) copy-start(s32[4]{0:T(128)} %constant.6.clone) | copy-start | bytes 52
  57.0 29.1 %copy-start = (bf16[256,768]{1,0:T(8,128)(2,1)S(1)}, bf16[256,768]{1,0:T(8,128)(2,1)}, u32[]{:S(2)}) copy-start(bf16[256,768]{1,0:T(8,128)(2,1)} %get-tuple-element.12.v_ref) | copy-start | bytes 1179652
  57.0 29.1 %all-to-all-start.1 = ((bf16[128,8,768]{2,1,0:T(8,128)(2,1)}), bf16[128,8,768]{2,1,0:T(8,128)(2,1)S(1)}, u32[]{:S(2)}, u32[]{:S(2)}) async-start(bf16[128,8,768]{2,1,0:T(8,128)(2,1)} %bitcast.12), calls=%async_computation.1 | async-start | bytes 3145728 | tf_op jit(solution)/shard_map/all_to_all | solution.py:262
  89.1 5.2 %collective-permute-start.1 = (bf16[256,1024]{1,0:T(8,128)(2,1)S(1)}, bf16[256,1024]{1,0:T(8,128)(2,1)S(1)}, u32[]{:S(2)}, u32[]{:S(2)}) collective-permute-start(bf16[256,1024]{1,0:T(8,128)(2,1)S(1)} %get-tuple-element.18), channel_id=1, source_target_pairs={{0,1},{1,0},{2,3},{3,2},{4,5},{5,4},{6,7},{7,6},{8,9},{9,8},{10,11... | collective-permute-start | bytes 1572872 | tf_op jit(solution)/shard_map/ppermute | solution.py:283
  94.1 2.0 %collective-permute-start = (bf16[256,1024]{1,0:T(8,128)(2,1)S(1)}, bf16[256,1024]{1,0:T(8,128)(2,1)S(1)}, u32[]{:S(2)}, u32[]{:S(2)}) collective-permute-start(bf16[256,1024]{1,0:T(8,128)(2,1)S(1)} %get-tuple-element.16), channel_id=1, source_target_pairs={{0,1},{1,0},{2,3},{3,2},{4,5},{5,4},{6,7},{7,6},{8,9},{9,8},{10,11... | collective-permute-start | bytes 1572872 | tf_op jit(solution)/shard_map/ppermute | solution.py:286
  94.4 13.1 %collective-permute-start.2 = (bf16[256,1024]{1,0:T(8,128)(2,1)S(1)}, bf16[256,1024]{1,0:T(8,128)(2,1)S(1)}, u32[]{:S(2)}, u32[]{:S(2)}) collective-permute-start(bf16[256,1024]{1,0:T(8,128)(2,1)S(1)} %add_convert_fusion.1), channel_id=1, source_target_pairs={{0,2},{1,3},{2,0},{3,1},{4,6},{5,7},{6,4},{7,5},{8,10},{9,11},{10,... | collective-permute-start | bytes 1572872 | tf_op jit(solution)/shard_map/ppermute | solution.py:285

commit v4 on v3

--- a/solution.py
+++ b/solution.py
@@ -19,6 +19,9 @@
 def pieces(slot):
     rest = WIDTH - LANES
     return [(slot, 0, 0, LANES), (SLOTS + slot // 3, slot % 3 * rest, LANES, rest)]
+
+
+SPLIT, EXPERTS, MERGE_MIB = 52, 50, 48
 
 
 def iota(shape, dim):
@@ -107,7 +110,7 @@
     for n in range(blocks):
         cols = pl.ds(n * BLOCK, BLOCK)
         gets.append(pltpu.make_async_copy(w_hbm.at[:, cols], w_ref.at[:, cols], sems.at[n]))
-    fetch([get_tok] + gets)
+    fetch([get_tok] + gets[:1])
     ids = ids_ref[...]
     key = slot_keys(ids, cap_ref[...])
     peers = key.shape[0]
@@ -116,6 +119,7 @@
     combine_weights(v_ref, ids, key, q_ref[...])
     get_tok.wait()
     for n in range(blocks):
+        fetch(gets[n + 1 : n + 2])
         gets[n].wait()
         sub = dot(tok_ref[...], w_ref[:, n * BLOCK : (n + 1) * BLOCK]).astype(BF16)
         to_flat(flat_ref, dot(pick_ref[...], sub), n * BLOCK)
@@ -141,7 +145,7 @@
             flat_scratch(rows),
             pltpu.SemaphoreType.DMA((w_split.shape[1] // BLOCK + 1,)),
         ],
-        compiler_params=pltpu.CompilerParams(vmem_limit_bytes=62 << 20),
+        compiler_params=pltpu.CompilerParams(vmem_limit_bytes=SPLIT << 20),
         name="split_pack",
     )(ids, capacity, q, tokens, w_split)
 
@@ -155,10 +159,11 @@
             cols = pl.ds(col, BLOCK)
             gets.append(pltpu.make_async_copy(in_hbm.at[0, :, cols], in_ref.at[:, cols], sems.at[2 * j + n]))
     gets.append(pltpu.make_async_copy(down_hbm.at[0], down_ref, sems.at[2 * steps]))
-    fetch(gets)
+    fetch(gets[:4])
     from_tiles(rows_ref, flat_ref, x_ref)
     rows = rows_ref[...]
     for j in range(steps):
+        fetch(gets[2 * j + 4 : 2 * j + 6])
         gets[2 * j].wait()
         gets[2 * j + 1].wait()
         cols = slice(j * BLOCK, (j + 1) * BLOCK)
@@ -189,23 +194,24 @@
             flat_scratch(rows),
             pltpu.SemaphoreType.DMA((2 * hidden // BLOCK + 1,)),
         ],
-        compiler_params=pltpu.CompilerParams(vmem_limit_bytes=60 << 20),
+        compiler_params=pltpu.CompilerParams(vmem_limit_bytes=EXPERTS << 20),
         name="experts",
     )(tiles, expert_in, expert_out)
 
 
-def column_blocks(w_hbm, w_ref, at, sems):
+def column_blocks(w_hbm, w_ref, order, sems):
     width = w_hbm.shape[0]
-    return fetch(
-        [
-            pltpu.make_async_copy(w_hbm.at[:, pl.ds(pl.multiple_of(a * width, width), width)], w_ref.at[n], sems.at[n])
-            for n, a in enumerate(at)
-        ]
-    )
-
-
-def combine_body(at_ref, v_ref, b_ref, w_hbm, head_ref, send_ref, w_ref, rows_ref, flat_ref, sems):
-    (get,) = column_blocks(w_hbm, w_ref, [at_ref[0]], sems)
+    me = lax.axis_index("sub")
+    return [
+        pltpu.make_async_copy(
+            w_hbm.at[:, pl.ds(pl.multiple_of((me ^ other) * width, width), width)], w_ref.at[n], sems.at[n]
+        )
+        for n, other in enumerate(order)
+    ]
+
+
+def combine_body(v_ref, b_ref, w_hbm, head_ref, send_ref, w_ref, rows_ref, flat_ref, sems):
+    (get,) = fetch(column_blocks(w_hbm, w_ref, (3,), sems))
     from_tiles(rows_ref, flat_ref, b_ref)
     head = dot(v_ref[...], rows_ref[...]).astype(BF16)
     head_ref[...] = head
@@ -213,16 +219,16 @@
     send_ref[...] = dot(head, w_ref[0]).astype(BF16)
 
 
-MERGE = pltpu.CompilerParams(vmem_limit_bytes=48 << 20)
-
-
-def combine_and_merge(at, v, back, w_merge):
+MERGE = pltpu.CompilerParams(vmem_limit_bytes=MERGE_MIB << 20)
+
+
+def combine_and_merge(v, back, w_merge):
     tokens = v.shape[0]
     width = w_merge.shape[0]
     rows = back.shape[0]
     return pl.pallas_call(
         combine_body,
-        in_specs=[pl.BlockSpec(memory_space=pltpu.SMEM), ONCHIP, ONCHIP, REMOTE],
+        in_specs=[ONCHIP, ONCHIP, REMOTE],
         out_specs=[ONCHIP] * 2,
         out_shape=[jax.ShapeDtypeStruct((tokens, width), BF16)] * 2,
         scratch_shapes=[
@@ -233,28 +239,30 @@
         ],
         compiler_params=MERGE,
         name="combine_merge",
-    )(at, v, back, w_merge)
-
-
-def merge_body(at_ref, head_ref, w_hbm, far_ref, send_ref, keep_ref, w_ref, sems):
-    gets = column_blocks(w_hbm, w_ref, [at_ref[n] for n in (1, 2, 3)], sems)
+    )(v, back, w_merge)
+
+
+def merge_body(head_ref, w_hbm, far_ref, send_ref, keep_ref, w_ref, sems):
+    gets = column_blocks(w_hbm, w_ref, (2, 1, 0), sems)
+    fetch(gets[:2])
     head = head_ref[...]
     for n, out_ref in enumerate((far_ref, send_ref, keep_ref)):
         gets[n].wait()
+        fetch(gets[n + 2 : n + 3])
         out_ref[...] = dot(head, w_ref[n]).astype(BF16)
 
 
-def merge_rest(at, head, w_merge):
+def merge_rest(head, w_merge):
     width = w_merge.shape[0]
     return pl.pallas_call(
         merge_body,
-        in_specs=[pl.BlockSpec(memory_space=pltpu.SMEM), ONCHIP, REMOTE],
+        in_specs=[ONCHIP, REMOTE],
         out_specs=[ONCHIP] * 3,
         out_shape=[jax.ShapeDtypeStruct(head.shape, BF16)] * 3,
         scratch_shapes=[pltpu.VMEM((3, width, width), BF16), pltpu.SemaphoreType.DMA((3,))],
         compiler_params=MERGE,
         name="merge_rest",
-    )(at, head, w_merge)
+    )(head, w_merge)
 
 
 def exchange(tiles, axes):
@@ -275,13 +283,11 @@
     tiles = exchange(packed, axes)
     back = exchange(expert_rows(tiles, expert_in, expert_out), axes)
 
-    me = lax.axis_index("sub")
     core = [(i, i ^ 1) for i in range(4)]
     chip = [(i, i ^ 2) for i in range(4)]
-    at = me ^ jnp.array([3, 2, 1, 0], I32)
-    head, far_send = combine_and_merge(at, v, back, w_merge)
+    head, far_send = combine_and_merge(v, back, w_merge)
     far_in = lax.ppermute(far_send, "sub", core)
-    far_keep, own_send, own_keep = merge_rest(at, head, w_merge)
+    far_keep, own_send, own_keep = merge_rest(head, w_merge)
     cross = lax.ppermute(added(far_keep, far_in), "sub", chip)
     own_in = lax.ppermute(own_send, "sub", core)
     return (own_keep.astype(F32) + own_in.astype(F32) + cross.astype(F32)).astype(BF16)

time: 109 us -> 106 us (0.972)
  blocking collectives: 36.3 us -> 64.4 us
  waiting for transfers between devices: 37.4 us -> 12.6 us
  starting transfers between devices: 5.62 us -> 1.35 us
  Pallas kernels: 27.9 us -> 23.8 us
  local copies, waits for them, and re-layouts: 0.01 us -> 2.02 us
    all_to_all x1 -> x2, blocking collectives: 36.3 us -> 64.4 us  [exchange(): lax.all_to_all(tiles.reshape(peers, ROWS, LANES), axes, split_axis=0, con...]
    all_to_all x1 -> x0, waiting for transfers between devices: 24.8 us -> none  [exchange(): lax.all_to_all(tiles.reshape(peers, ROWS, LANES), axes, split_axis=0, con...]
    all_to_all x1 -> x0, starting transfers between devices: 4.27 us -> none  [exchange(): lax.all_to_all(tiles.reshape(peers, ROWS, LANES), axes, split_axis=0, con...]
    pallas_call x1, Pallas kernels: 10.1 us -> 7.6 us  [expert_rows(): pl.pallas_call(expert_body, in_specs=[ONCHIP, REMOTE, REMOTE], out_specs=...]
    unnamed x4 -> x6, local copies, waits for them, and re-layouts: 0.01 us -> 2.02 us
    pallas_call x1, Pallas kernels: 10.5 us -> 8.66 us  [split_and_pack(): pl.pallas_call(pack_body, in_specs=[ONCHIP] * 3 + [REMOTE] * 2, out_specs...]
  transfers between devices with their start and end apart: 4 -> 3, of which waited for: 3 -> 2; matrix products, arithmetic and copies ran while one was open for 0% -> 0% of each run, Pallas kernels for 4% -> 4%
where the time goes in v4:
time: 106 us
  blocking collectives  64.4 us (61%)
  Pallas kernels  23.8 us (22%)
  waiting for transfers between devices  12.6 us (12%)
  local copies, waits for them, and re-layouts  2.02 us (2%)
  starting transfers between devices  1.35 us (1%)
  other arithmetic  1.25 us (1%)
    all_to_all x2, blocking collectives, exchange(): lax.all_to_all(tiles.reshape(peers, ROWS, LANES), axes, split_axis=0, con...  64.4 us
    ppermute x1, waiting for transfers between devices, body(): cross = lax.ppermute(added(far_keep, far_in), 'sub', chip)  11.4 us
    pallas_call x1, Pallas kernels, split_and_pack(): pl.pallas_call(pack_body, in_specs=[ONCHIP] * 3 + [REMOTE] * 2, out_specs...  8.66 us
    pallas_call x1, Pallas kernels, expert_rows(): pl.pallas_call(expert_body, in_specs=[ONCHIP, REMOTE, REMOTE], out_specs=...  7.6 us
    pallas_call x1, Pallas kernels, merge_rest(): pl.pallas_call(merge_body, in_specs=[ONCHIP, REMOTE], out_specs=[ONCHIP]...  4.09 us
    pallas_call x1, Pallas kernels, combine_and_merge(): pl.pallas_call(combine_body, in_specs=[ONCHIP, ONCHIP, REMOTE], out_specs...  3.5 us
  transfers between devices with their start and end apart: 3, of which 2 were waited for; matrix products, arithmetic and copies ran while one was open for 0% of the time, Pallas kernels for 4%

profile of v4, /device:TPU:1, one launch (start us, length us, event | category | flops | bytes accessed | tf_op | source)
XLA Modules:
  0.0 105.5 jit_solution(13859172097660164274)
XLA Ops:
  0.0 0.0 copy-start
  0.0 0.7 copy-done
  0.7 0.0 copy-start.1
  0.7 0.7 copy-done.1
  1.4 0.0 copy-start.2
  1.4 0.7 copy-done.2
  2.0 8.7 %split_pack.1 = (bf16[1024,768]{1,0:T(8,128)(2,1)S(1)}, bf16[256,768]{1,0:T(8,128)(2,1)S(1)}) custom-call(s32[2,256]{1,0:T(2,128)S(1)} %bitcast.15, s32[1,128]{1,0:T(1,128)S(1)} %bitcast.17, s32[2,256]{1,0:T(2,128)S(1)} %bitcast.16, bf16[256,4096]{1,0:T(8,128)(2,1)} %tok_hbm.1, bf16[4096,1024]{1,0:T(8,128)(2,1)} %w_hbm.3), custom_call_target="tpu_custom_call" | custom-call | tf_op jit(solution)/shard_map/split_pack/pallas_call | solution.py:133
  10.7 36.0 %all_to_all.10 = bf16[128,8,768]{2,1,0:T(8,128)(2,1)S(1)} all-to-all(bf16[128,8,768]{2,1,0:T(8,128)(2,1)S(1)} %bitcast.14), channel_id=1, replica_groups=mesh['seq'=32,'sub'=4] {'seq','sub'}, dimensions={0} | all-to-all | bytes 3145728 | tf_op jit(solution)/shard_map/all_to_all | solution.py:270
  46.7 7.6 %experts.1 = bf16[1024,768]{1,0:T(8,128)(2,1)S(1)} custom-call(bf16[1024,768]{1,0:T(8,128)(2,1)S(1)} %bitcast.12, bf16[1,1024,2048]{2,1,0:T(8,128)(2,1)} %in_hbm.1, bf16[1,1024,1024]{2,1,0:T(8,128)(2,1)} %down_hbm.1), custom_call_target="tpu_custom_call" | custom-call | tf_op jit(solution)/shard_map/experts/pallas_call | solution.py:184
  54.3 28.4 %all_to_all.11 = bf16[128,8,768]{2,1,0:T(8,128)(2,1)S(1)} all-to-all(bf16[128,8,768]{2,1,0:T(8,128)(2,1)S(1)} %bitcast.13), channel_id=1, replica_groups=mesh['seq'=32,'sub'=4] {'seq','sub'}, dimensions={0} | all-to-all | bytes 3145728 | tf_op jit(solution)/shard_map/all_to_all | solution.py:270
  82.7 3.5 %combine_merge.1 = (bf16[256,1024]{1,0:T(8,128)(2,1)S(1)}, bf16[256,1024]{1,0:T(8,128)(2,1)S(1)}) custom-call(bf16[256,768]{1,0:T(8,128)(2,1)S(1)} %get-tuple-element.12.v_ref, bf16[1024,768]{1,0:T(8,128)(2,1)S(1)} %bitcast.11, bf16[1024,4096]{1,0:T(8,128)(2,1)} %w_hbm.5), custom_call_target="tpu_custom_call" | custom-call | tf_op jit(solution)/shard_map/combine_merge/pallas_call | solution.py:229
  86.2 0.8 collective-permute-start.1
  87.0 4.1 %merge_rest.1 = (bf16[256,1024]{1,0:T(8,128)(2,1)S(1)}, bf16[256,1024]{1,0:T(8,128)(2,1)S(1)}, bf16[256,1024]{1,0:T(8,128)(2,1)S(1)}) custom-call(bf16[256,1024]{1,0:T(8,128)(2,1)S(1)} %get-tuple-element.14.head_ref, bf16[1024,4096]{1,0:T(8,128)(2,1)} %w_hbm.5), custom_call_target="tpu_custom_call" | custom-call | tf_op jit(solution)/shard_map/merge_rest/pallas_call | solution.py:257
  91.1 0.1 collective-permute-start
  91.2 0.0 collective-permute-done.1
  91.2 0.2 add_convert_fusion.1
  91.4 0.5 collective-permute-start.2
  91.9 1.2 %collective-permute-done = bf16[256,1024]{1,0:T(8,128)(2,1)S(1)} collective-permute-done((bf16[256,1024]{1,0:T(8,128)(2,1)S(1)}, bf16[256,1024]{1,0:T(8,128)(2,1)S(1)}, u32[]{:S(2)}, u32[]{:S(2)}) %collective-permute-start) | collective-permute-done | bytes 524320 | tf_op jit(solution)/shard_map/ppermute | solution.py:292
  93.1 11.4 %collective-permute-done.2 = bf16[256,1024]{1,0:T(8,128)(2,1)S(1)} collective-permute-done((bf16[256,1024]{1,0:T(8,128)(2,1)S(1)}, bf16[256,1024]{1,0:T(8,128)(2,1)S(1)}, u32[]{:S(2)}, u32[]{:S(2)}) %collective-permute-start.2) | collective-permute-done | bytes 524320 | tf_op jit(solution)/shard_map/ppermute | solution.py:291
  104.5 1.1 %add_convert_fusion = bf16[256,1024]{1,0:T(8,128)(2,1)} fusion(bf16[256,1024]{1,0:T(8,128)(2,1)S(1)} %collective-permute-done.2, bf16[256,1024]{1,0:T(8,128)(2,1)S(1)} %collective-permute-done, bf16[256,1024]{1,0:T(8,128)(2,1)S(1)} %get-tuple-element.15), kind=kLoop, calls=%fused_computation | loop fusion | flops 1572864 | bytes 2097152 | tf_op jit(solution)/shard_map/convert_element_type | solution.py:293
Async XLA Ops:
  0.0 0.7 copy-start
  0.7 0.7 copy-start.1
  1.4 0.7 copy-start.2
  86.2 5.0 %collective-permute-start.1 = (bf16[256,1024]{1,0:T(8,128)(2,1)S(1)}, bf16[256,1024]{1,0:T(8,128)(2,1)S(1)}, u32[]{:S(2)}, u32[]{:S(2)}) collective-permute-start(bf16[256,1024]{1,0:T(8,128)(2,1)S(1)} %get-tuple-element.18), channel_id=1, source_target_pairs={{0,1},{1,0},{2,3},{3,2},{4,5},{5,4},{6,7},{7,6},{8,9},{9,8},{10,11... | collective-permute-start | bytes 1572872 | tf_op jit(solution)/shard_map/ppermute | solution.py:289
  91.1 2.0 %collective-permute-start = (bf16[256,1024]{1,0:T(8,128)(2,1)S(1)}, bf16[256,1024]{1,0:T(8,128)(2,1)S(1)}, u32[]{:S(2)}, u32[]{:S(2)}) collective-permute-start(bf16[256,1024]{1,0:T(8,128)(2,1)S(1)} %get-tuple-element.16), channel_id=1, source_target_pairs={{0,1},{1,0},{2,3},{3,2},{4,5},{5,4},{6,7},{7,6},{8,9},{9,8},{10,11... | collective-permute-start | bytes 1572872 | tf_op jit(solution)/shard_map/ppermute | solution.py:292
  91.4 13.1 %collective-permute-start.2 = (bf16[256,1024]{1,0:T(8,128)(2,1)S(1)}, bf16[256,1024]{1,0:T(8,128)(2,1)S(1)}, u32[]{:S(2)}, u32[]{:S(2)}) collective-permute-start(bf16[256,1024]{1,0:T(8,128)(2,1)S(1)} %add_convert_fusion.1), channel_id=1, source_target_pairs={{0,2},{1,3},{2,0},{3,1},{4,6},{5,7},{6,4},{7,5},{8,10},{9,11},{10,... | collective-permute-start | bytes 1572872 | tf_op jit(solution)/shard_map/ppermute | solution.py:291

commit v5 on v4

v5 whole, which is shorter than its diff:
```python
import jax
import jax.numpy as jnp
from jax import lax
from jax.experimental import pallas as pl
from jax.experimental.pallas import tpu as pltpu
from jax.sharding import PartitionSpec as P


F32 = jnp.float32
BF16 = jnp.bfloat16
I32 = jnp.int32

SLOTS = 6
ROWS = 8
WIDTH = 1024
LANES = SLOTS * WIDTH // ROWS
NONE = -4.0


def pieces(slot):
    rest = WIDTH - LANES
    return [(slot, 0, 0, LANES), (SLOTS + slot // 3, slot % 3 * rest, LANES, rest)]


SPLIT, EXPERTS, MERGE_MIB = 52, 24, 24


def iota(shape, dim):
    return lax.broadcasted_iota(I32, shape, dim)


def dot(a, b):
    return jnp.dot(a, b, preferred_element_type=F32)


def bits(mask):
    return mask.astype(F32).astype(BF16)


def to_flat(flat_ref, values, first=0):
    peers = values.shape[0] // SLOTS
    last = first + values.shape[1]
    for s in range(SLOTS):
        for row, lane, col, width in pieces(s):
            for w in range(0, width, 128):
                if first <= col + w < last:
                    at = col + w - first
                    flat_ref[(lane + w) // 128, pl.ds(row, peers, stride=ROWS), :] = values[
                        s * peers : (s + 1) * peers, at : at + 128
                    ]


def from_flat(out_ref, flat_ref):
    for b in range(LANES // 128):
        out_ref[:, b * 128 : (b + 1) * 128] = flat_ref[b].astype(BF16)


def from_tiles(rows_ref, flat_ref, in_ref):
    peers = in_ref.shape[0] // ROWS
    for b in range(LANES // 128):
        flat_ref[b] = in_ref[:, b * 128 : (b + 1) * 128].astype(F32)
    for s in range(SLOTS):
        for row, lane, col, width in pieces(s):
            for w in range(0, width, 128):
                rows_ref[s * peers : (s + 1) * peers, col + w : col + w + 128] = flat_ref[
                    (lane + w) // 128, pl.ds(row, peers, stride=ROWS), :
                ].astype(BF16)


def slot_keys(ids, capacity):
    experts = capacity.shape[1]
    tokens = ids.shape[1]
    expert = iota((experts, tokens), 0)
    named = (ids[0:1, :] == expert) | (ids[1:2, :] == expert)
    earlier = bits(iota((tokens, tokens), 0) < iota((tokens, tokens), 1))
    rank = dot(bits(named), earlier)
    own = iota((experts, experts), 0) == iota((experts, experts), 1)
    limit = jnp.sum(jnp.where(own, capacity.astype(F32), 0.0), axis=1, keepdims=True)
    return jnp.where(named & (rank < limit), rank, NONE)


def combine_weights(v_ref, ids, key, q):
    expert = iota(key.shape, 0)
    scale = q.astype(F32) / 65536.0
    weight = jnp.where(ids[0:1, :] == expert, scale[0:1, :], 0.0) + jnp.where(ids[1:2, :] == expert, scale[1:2, :], 0.0)
    key, weight = key.T, weight.T
    peers = key.shape[1]
    for s in range(SLOTS):
        v_ref[:, s * peers : (s + 1) * peers] = jnp.where(key == float(s), weight, 0.0).astype(BF16)


BLOCK = 256
ONCHIP = pl.BlockSpec(memory_space=pltpu.VMEM)
REMOTE = pl.BlockSpec(memory_space=pltpu.HBM)


def fetch(copies):
    for c in copies:
        c.start()
    return copies


def flat_scratch(rows):
    return pltpu.VMEM((LANES // 128, rows, 128), F32)


PARTS = 8


def pack_body(small_ref, tok_hbm, w_hbm, out_ref, v_ref, tok_ref, w_ref, acc_ref, pick_ref, flat_ref, sems):
    part = w_ref.shape[0] // PARTS
    gets = []
    for n in range(PARTS):
        at = pl.ds(n * part, part)
        gets.append(pltpu.make_async_copy(tok_hbm.at[:, at], tok_ref.at[:, at], sems.at[2 * n]))
        gets.append(pltpu.make_async_copy(w_hbm.at[at, :], w_ref.at[at, :], sems.at[2 * n + 1]))
    fetch(gets)
    ids = small_ref[0:2, :]
    peers = pick_ref.shape[0] // SLOTS
    key = slot_keys(ids, small_ref[4:5, :peers])
    for s in range(SLOTS):
        pick_ref[s * peers : (s + 1) * peers, :] = bits(key == float(s))
    combine_weights(v_ref, ids, key, small_ref[2:4, :])
    for n in range(PARTS):
        gets[2 * n].wait()
        gets[2 * n + 1].wait()
        at = slice(n * part, (n + 1) * part)
        product = dot(tok_ref[:, at], w_ref[at, :])
        acc_ref[...] = product if n == 0 else acc_ref[...] + product
    to_flat(flat_ref, dot(pick_ref[...], acc_ref[...].astype(BF16)))
    from_flat(out_ref, flat_ref)


def split_and_pack(ids, capacity, q, tokens, w_split):
    count = tokens.shape[0]
    experts = capacity.shape[0]
    rows = experts * ROWS
    limits = jnp.pad(capacity[None, :], ((0, 0), (0, count - experts)))
    small = jnp.concatenate([ids, q, limits], axis=0)
    return pl.pallas_call(
        pack_body,
        in_specs=[ONCHIP] + [REMOTE] * 2,
        out_specs=[ONCHIP] * 2,
        out_shape=[
            jax.ShapeDtypeStruct((rows, LANES), BF16),
            jax.ShapeDtypeStruct((count, experts * SLOTS), BF16),
        ],
        scratch_shapes=[
            pltpu.VMEM(tokens.shape, BF16),
            pltpu.VMEM(w_split.shape, BF16),
            pltpu.VMEM((count, w_split.shape[1]), F32),
            pltpu.VMEM((experts * SLOTS, count), BF16),
            flat_scratch(rows),
            pltpu.SemaphoreType.DMA((2 * PARTS,)),
        ],
        compiler_params=pltpu.CompilerParams(vmem_limit_bytes=SPLIT << 20),
        name="split_pack",
    )(small, tokens, w_split)


def expert_body(x_ref, in_ref, down_ref, out_ref, rows_ref, act_ref, flat_ref):
    hidden, width = down_ref.shape[1:]
    from_tiles(rows_ref, flat_ref, x_ref)
    rows = rows_ref[...]
    for j in range(0, hidden, BLOCK):
        gate = dot(rows, in_ref[0, :, j : j + BLOCK])
        up = dot(rows, in_ref[0, :, hidden + j : hidden + j + BLOCK])
        act_ref[:, j : j + BLOCK] = (gate / (1.0 + jnp.exp(-gate)) * up).astype(BF16)
    for j in range(0, width, BLOCK):
        to_flat(flat_ref, dot(act_ref[...], down_ref[0, :, j : j + BLOCK]), j)
    from_flat(out_ref, flat_ref)


def expert_rows(tiles, expert_in, expert_out):
    rows = tiles.shape[0]
    slots = rows // ROWS * SLOTS
    width = expert_in.shape[1]
    hidden = expert_out.shape[1]
    return pl.pallas_call(
        expert_body,
        in_specs=[ONCHIP] * 3,
        out_specs=ONCHIP,
        out_shape=jax.ShapeDtypeStruct((rows, LANES), BF16),
        scratch_shapes=[pltpu.VMEM((slots, width), BF16), pltpu.VMEM((slots, hidden), BF16), flat_scratch(rows)],
        compiler_params=pltpu.CompilerParams(vmem_limit_bytes=EXPERTS << 20),
        name="experts",
    )(tiles, expert_in, expert_out)


def column_block(w_ref, other):
    width = w_ref.shape[0]
    return w_ref[:, pl.ds(pl.multiple_of((lax.axis_index("sub") ^ other) * width, width), width)]


MERGE = pltpu.CompilerParams(vmem_limit_bytes=MERGE_MIB << 20)


def combine_body(v_ref, b_ref, w_ref, head_ref, send_ref, rows_ref, flat_ref):
    from_tiles(rows_ref, flat_ref, b_ref)
    head = dot(v_ref[...], rows_ref[...]).astype(BF16)
    head_ref[...] = head
    send_ref[...] = dot(head, column_block(w_ref, 3)).astype(BF16)


def combine_and_merge(v, back, w_merge):
    tokens = v.shape[0]
    width = w_merge.shape[0]
    rows = back.shape[0]
    return pl.pallas_call(
        combine_body,
        in_specs=[ONCHIP] * 3,
        out_specs=[ONCHIP] * 2,
        out_shape=[jax.ShapeDtypeStruct((tokens, width), BF16)] * 2,
        scratch_shapes=[pltpu.VMEM((rows // ROWS * SLOTS, width), BF16), flat_scratch(rows)],
        compiler_params=MERGE,
        name="combine_merge",
    )(v, back, w_merge)


def far_body(head_ref, w_ref, far_ref):
    far_ref[...] = dot(head_ref[...], column_block(w_ref, 2)).astype(BF16)


def merge_far(head, w_merge):
    return pl.pallas_call(
        far_body,
        in_specs=[ONCHIP] * 2,
        out_specs=ONCHIP,
        out_shape=jax.ShapeDtypeStruct(head.shape, BF16),
        compiler_params=MERGE,
        name="merge_far",
    )(head, w_merge)


def own_body(head_ref, w_ref, after_ref, send_ref, keep_ref):
    del after_ref
    head = head_ref[...]
    send_ref[...] = dot(head, column_block(w_ref, 1)).astype(BF16)
    keep_ref[...] = dot(head, column_block(w_ref, 0)).astype(BF16)


def merge_own(head, w_merge, after):
    return pl.pallas_call(
        own_body,
        in_specs=[ONCHIP] * 2 + [REMOTE],
        out_specs=[ONCHIP] * 2,
        out_shape=[jax.ShapeDtypeStruct(head.shape, BF16)] * 2,
        compiler_params=MERGE,
        name="merge_own",
    )(head, w_merge, after)


def exchange(tiles, axes):
    peers = tiles.shape[0] // ROWS
    return lax.all_to_all(tiles.reshape(peers, ROWS, LANES), axes, split_axis=0, concat_axis=0, tiled=True).reshape(tiles.shape)


def added(a, b):
    return (a.astype(F32) + b.astype(F32)).astype(BF16)


def body(tokens, w_split, w_merge, expert_in, expert_out, expert_ids, combine_q, capacity):
    ids = expert_ids[0].T
    q = combine_q[0].T
    axes = ("seq", "sub")
    packed, v = split_and_pack(ids, capacity, q, tokens, w_split)
    tiles = exchange(packed, axes)
    back = exchange(expert_rows(tiles, expert_in, expert_out), axes)

    core = [(i, i ^ 1) for i in range(4)]
    chip = [(i, i ^ 2) for i in range(4)]
    head, far_send = combine_and_merge(v, back, w_merge)
    far_in = lax.ppermute(far_send, "sub", core)
    far_keep = merge_far(head, w_merge)
    far = added(far_keep, far_in)
    cross = lax.ppermute(far, "sub", chip)
    own_send, own_keep = merge_own(head, w_merge, far)
    own_in = lax.ppermute(own_send, "sub", core)
    return (own_keep.astype(F32) + own_in.astype(F32) + cross.astype(F32)).astype(BF16)


def solution(mesh):
    in_specs = (
        P("seq", None),
        P(None, "sub"),
        P("sub", None),
        P(("seq", "sub"), None, None),
        P(("seq", "sub"), None, None),
        P("sub", "seq", None),
        P("sub", "seq", None),
        P(),
    )
    out_specs = P("seq", "sub")
    return jax.shard_map(body, mesh=mesh, in_specs=in_specs, out_specs=out_specs, check_vma=False)
```

time: 106 us -> 97.7 us (0.922)
  Pallas kernels: 23.8 us -> 15.7 us
  local copies, waits for them, and re-layouts: 2.02 us -> 0.02 us
  waiting for transfers between devices: 12.6 us -> 13.8 us
    pallas_call x4 -> x5, Pallas kernels: 23.8 us -> 15.7 us  [the longest x1 6.11 us: expert_rows(): pl.pallas_call(expert_body, in_specs=[ONCHIP] * 3, out_specs=ONCHIP, out_...]
    unnamed x6 -> x8, local copies, waits for them, and re-layouts: 2.02 us -> 0.02 us
  transfers between devices with their start and end apart: 3 -> 3, of which waited for: 2 -> 3; matrix products, arithmetic and copies ran while one was open for 0% -> 0% of each run, Pallas kernels for 4% -> 1%
where the time goes in v5:
time: 97.7 us; the launch traced here: 97.5 us
  blocking collectives  64.4 us (66%)
  Pallas kernels  15.7 us (16%)
  waiting for transfers between devices  13.8 us (14%)
  other arithmetic  1.98 us (2%)
  starting transfers between devices  1.62 us (2%)
    all_to_all x2, blocking collectives, exchange(): lax.all_to_all(tiles.reshape(peers, ROWS, LANES), axes, split_axis=0, con...  64.4 us
    ppermute x1, waiting for transfers between devices, body(): cross = lax.ppermute(far, 'sub', chip)  11.8 us
    pallas_call x1, Pallas kernels, expert_rows(): pl.pallas_call(expert_body, in_specs=[ONCHIP] * 3, out_specs=ONCHIP, out_...  6.11 us
    pallas_call x1, Pallas kernels, split_and_pack(): pl.pallas_call(pack_body, in_specs=[ONCHIP] + [REMOTE] * 2, out_specs=[ON...  5.69 us
  transfers between devices with their start and end apart: 3, of which 3 were waited for; matrix products, arithmetic and copies ran while one was open for 0% of the time, Pallas kernels for 1%

profile of v5, /device:TPU:1, one launch (start us, length us, event | category | flops | bytes accessed | tf_op | source)
XLA Modules:
  0.0 97.5 jit_solution(5670113885190597146)
XLA Ops:
  0.0 0.7 pad_add_fusion.small_ref
  0.7 0.0 copy-start
  0.7 5.7 %split_pack.1 = (bf16[1024,768]{1,0:T(8,128)(2,1)S(1)}, bf16[256,768]{1,0:T(8,128)(2,1)S(1)}) custom-call(s32[5,256]{1,0:T(8,128)S(1)} %pad_add_fusion.small_ref, bf16[256,4096]{1,0:T(8,128)(2,1)} %tok_hbm.1, bf16[4096,1024]{1,0:T(8,128)(2,1)} %w_hbm.1), custom_call_target="tpu_custom_call" | custom-call | tf_op jit(solution)/shard_map/split_pack/pallas_call | solution.py:140
  6.4 0.0 copy-start.1
  6.4 0.0 slice-start
  6.4 36.0 %all_to_all.10 = bf16[128,8,768]{2,1,0:T(8,128)(2,1)S(1)} all-to-all(bf16[128,8,768]{2,1,0:T(8,128)(2,1)S(1)} %bitcast.16), channel_id=1, replica_groups=mesh['seq'=32,'sub'=4] {'seq','sub'}, dimensions={0} | all-to-all | bytes 3145728 | tf_op jit(solution)/shard_map/all_to_all | solution.py:255
  42.5 0.0 copy-done
  42.5 0.0 copy-done.1
  42.5 0.0 slice-start.1
  42.5 6.1 %experts.1 = bf16[1024,768]{1,0:T(8,128)(2,1)S(1)} custom-call(bf16[1024,768]{1,0:T(8,128)(2,1)S(1)} %bitcast.14, bf16[1,1024,2048]{2,1,0:T(8,128)(2,1)S(1)} %copy-done, bf16[1,1024,1024]{2,1,0:T(8,128)(2,1)S(1)} %copy-done.1), custom_call_target="tpu_custom_call" | custom-call | tf_op jit(solution)/shard_map/experts/pallas_call | solution.py:179
  48.6 28.4 %all_to_all.11 = bf16[128,8,768]{2,1,0:T(8,128)(2,1)S(1)} all-to-all(bf16[128,8,768]{2,1,0:T(8,128)(2,1)S(1)} %bitcast.15), channel_id=1, replica_groups=mesh['seq'=32,'sub'=4] {'seq','sub'}, dimensions={0} | all-to-all | bytes 3145728 | tf_op jit(solution)/shard_map/all_to_all | solution.py:255
  77.0 0.0 slice-done
  77.0 0.0 slice-done.1
  77.0 1.9 %combine_merge.1 = (bf16[256,1024]{1,0:T(8,128)(2,1)S(1)}, bf16[256,1024]{1,0:T(8,128)(2,1)S(1)}) custom-call(bf16[256,768]{1,0:T(8,128)(2,1)S(1)} %get-tuple-element.11.v_ref, bf16[1024,768]{1,0:T(8,128)(2,1)S(1)} %bitcast.13, bf16[1024,4096]{1,0:T(8,128)(2,1)S(1)} %bitcast.12), custom_call_target="tpu_custom_call" | custom-call | tf_op jit(solution)/shard_map/combine_merge/pallas_call | solution.py:209
  78.9 0.8 collective-permute-start
  79.7 0.7 merge_far.1
  80.4 0.8 collective-permute-done
  81.2 0.2 add_convert_fusion.1.after_ref
  81.4 1.3 %merge_own.1 = (bf16[256,1024]{1,0:T(8,128)(2,1)S(1)}, bf16[256,1024]{1,0:T(8,128)(2,1)S(1)}) custom-call(bf16[256,1024]{1,0:T(8,128)(2,1)S(1)} %get-tuple-element.13.head_ref, bf16[1024,4096]{1,0:T(8,128)(2,1)S(1)} %bitcast.12, bf16[256,1024]{1,0:T(8,128)(2,1)S(1)} %add_convert_fusion.1.after_ref), custom_call_target="tpu_custom_call" | custom-call | tf_op jit(solution)/shard_map/merge_own/pallas_call | solution.py:243
  82.7 0.5 collective-permute-start.1
  83.1 0.4 collective-permute-start.2
  83.5 1.1 %collective-permute-done.1 = bf16[256,1024]{1,0:T(8,128)(2,1)S(1)} collective-permute-done((bf16[256,1024]{1,0:T(8,128)(2,1)S(1)}, bf16[256,1024]{1,0:T(8,128)(2,1)S(1)}, u32[]{:S(2)}, u32[]{:S(2)}) %collective-permute-start.1) | collective-permute-done | bytes 524320 | tf_op jit(solution)/shard_map/ppermute | solution.py:278
  84.7 11.8 %collective-permute-done.2 = bf16[256,1024]{1,0:T(8,128)(2,1)S(1)} collective-permute-done((bf16[256,1024]{1,0:T(8,128)(2,1)S(1)}, bf16[256,1024]{1,0:T(8,128)(2,1)S(1)}, u32[]{:S(2)}, u32[]{:S(2)}) %collective-permute-start.2) | collective-permute-done | bytes 524320 | tf_op jit(solution)/shard_map/ppermute | solution.py:276
  96.5 1.1 %add_convert_fusion = bf16[256,1024]{1,0:T(8,128)(2,1)} fusion(bf16[256,1024]{1,0:T(8,128)(2,1)S(1)} %collective-permute-done.2, bf16[256,1024]{1,0:T(8,128)(2,1)S(1)} %collective-permute-done.1, bf16[256,1024]{1,0:T(8,128)(2,1)S(1)} %get-tuple-element.15), kind=kLoop, calls=%fused_computation | loop fusion | flops 1572864 | bytes 2097152 | tf_op jit(solution)/shard_map/convert_element_type | solution.py:279
  (1 shorter events, 0.0 us)
Async XLA Ops:
  0.7 41.7 %copy-start = (bf16[1,1024,2048]{2,1,0:T(8,128)(2,1)S(1)}, bf16[1,1024,2048]{2,1,0:T(8,128)(2,1)}, u32[]{:S(2)}) copy-start(bf16[1,1024,2048]{2,1,0:T(8,128)(2,1)} %in_ref.1) | copy-start | bytes 12582916
  6.4 36.0 %copy-start.1 = (bf16[1,1024,1024]{2,1,0:T(8,128)(2,1)S(1)}, bf16[1,1024,1024]{2,1,0:T(8,128)(2,1)}, u32[]{:S(2)}) copy-start(bf16[1,1024,1024]{2,1,0:T(8,128)(2,1)} %down_ref.1) | copy-start | bytes 6291460
  6.4 70.5 %slice-start = ((s8[8388608]{0:T(1024)(128)(4,1)}), s8[4194304]{0:T(1024)(128)(4,1)S(1)}, s32[]{:S(2)}) async-start(s8[8388608]{0:T(1024)(128)(4,1)} %bitcast.11), calls=%async_computation.2 | async-start | bytes 8388608
  42.5 34.5 %slice-start.1 = ((s8[8388608]{0:T(1024)(128)(4,1)}), s8[4194304]{0:T(1024)(128)(4,1)S(1)}, s32[]{:S(2)}) async-start(s8[8388608]{0:T(1024)(128)(4,1)} %bitcast.11), calls=%async_computation.3 | async-start | bytes 8388608
  78.9 2.3 %collective-permute-start = (bf16[256,1024]{1,0:T(8,128)(2,1)S(1)}, bf16[256,1024]{1,0:T(8,128)(2,1)S(1)}, u32[]{:S(2)}, u32[]{:S(2)}) collective-permute-start(bf16[256,1024]{1,0:T(8,128)(2,1)S(1)} %get-tuple-element.14), channel_id=1, source_target_pairs={{0,1},{1,0},{2,3},{3,2},{4,5},{5,4},{6,7},{7,6},{8,9},{9,8},{10,11... | collective-permute-start | bytes 1572872 | tf_op jit(solution)/shard_map/ppermute | solution.py:273
  82.7 2.0 %collective-permute-start.1 = (bf16[256,1024]{1,0:T(8,128)(2,1)S(1)}, bf16[256,1024]{1,0:T(8,128)(2,1)S(1)}, u32[]{:S(2)}, u32[]{:S(2)}) collective-permute-start(bf16[256,1024]{1,0:T(8,128)(2,1)S(1)} %get-tuple-element.16), channel_id=1, source_target_pairs={{0,1},{1,0},{2,3},{3,2},{4,5},{5,4},{6,7},{7,6},{8,9},{9,8},{10,11... | collective-permute-start | bytes 1572872 | tf_op jit(solution)/shard_map/ppermute | solution.py:278
  83.1 13.3 %collective-permute-start.2 = (bf16[256,1024]{1,0:T(8,128)(2,1)S(1)}, bf16[256,1024]{1,0:T(8,128)(2,1)S(1)}, u32[]{:S(2)}, u32[]{:S(2)}) collective-permute-start(bf16[256,1024]{1,0:T(8,128)(2,1)S(1)} %add_convert_fusion.1.after_ref), channel_id=1, source_target_pairs={{0,2},{1,3},{2,0},{3,1},{4,6},{5,7},{6,4},{7,5},{8,10},{9,11},{10,... | collective-permute-start | bytes 1572872 | tf_op jit(solution)/shard_map/ppermute | solution.py:276

commit v6 on v5

--- a/solution.py
+++ b/solution.py
@@ -1,3 +1,5 @@
+import functools
+
 import jax
 import jax.numpy as jnp
 from jax import lax
@@ -187,9 +189,12 @@
     )(tiles, expert_in, expert_out)
 
 
-def column_block(w_ref, other):
+def column_block(w_ref, other, half=None):
     width = w_ref.shape[0]
-    return w_ref[:, pl.ds(pl.multiple_of((lax.axis_index("sub") ^ other) * width, width), width)]
+    start = (lax.axis_index("sub") ^ other) * width
+    if half is None:
+        return w_ref[:, pl.ds(pl.multiple_of(start, width), width)]
+    return w_ref[:, pl.ds(pl.multiple_of(start + half * (width // 2), width // 2), width // 2)]
 
 
 MERGE = pltpu.CompilerParams(vmem_limit_bytes=MERGE_MIB << 20)
@@ -199,7 +204,7 @@
     from_tiles(rows_ref, flat_ref, b_ref)
     head = dot(v_ref[...], rows_ref[...]).astype(BF16)
     head_ref[...] = head
-    send_ref[...] = dot(head, column_block(w_ref, 3)).astype(BF16)
+    send_ref[...] = dot(head, column_block(w_ref, 3, 0)).astype(BF16)
 
 
 def combine_and_merge(v, back, w_merge):
@@ -210,25 +215,29 @@
         combine_body,
         in_specs=[ONCHIP] * 3,
         out_specs=[ONCHIP] * 2,
-        out_shape=[jax.ShapeDtypeStruct((tokens, width), BF16)] * 2,
+        out_shape=[
+            jax.ShapeDtypeStruct((tokens, width), BF16),
+            jax.ShapeDtypeStruct((tokens, width // 2), BF16),
+        ],
         scratch_shapes=[pltpu.VMEM((rows // ROWS * SLOTS, width), BF16), flat_scratch(rows)],
         compiler_params=MERGE,
         name="combine_merge",
     )(v, back, w_merge)
 
 
-def far_body(head_ref, w_ref, far_ref):
-    far_ref[...] = dot(head_ref[...], column_block(w_ref, 2)).astype(BF16)
-
-
-def merge_far(head, w_merge):
-    return pl.pallas_call(
-        far_body,
+def far_body(blocks, head_ref, w_ref, *out_refs):
+    for (other, half), out_ref in zip(blocks, out_refs):
+        out_ref[...] = dot(head_ref[...], column_block(w_ref, other, half)).astype(BF16)
+
+
+def merge_far(head, w_merge, blocks):
+    tokens, width = head.shape
+    return pl.pallas_call(
+        functools.partial(far_body, blocks),
         in_specs=[ONCHIP] * 2,
-        out_specs=ONCHIP,
-        out_shape=jax.ShapeDtypeStruct(head.shape, BF16),
+        out_specs=[ONCHIP] * len(blocks),
+        out_shape=[jax.ShapeDtypeStruct((tokens, width // 2), BF16)] * len(blocks),
         compiler_params=MERGE,
-        name="merge_far",
     )(head, w_merge)
 
 
@@ -269,13 +278,18 @@
 
     core = [(i, i ^ 1) for i in range(4)]
     chip = [(i, i ^ 2) for i in range(4)]
-    head, far_send = combine_and_merge(v, back, w_merge)
-    far_in = lax.ppermute(far_send, "sub", core)
-    far_keep = merge_far(head, w_merge)
-    far = added(far_keep, far_in)
-    cross = lax.ppermute(far, "sub", chip)
-    own_send, own_keep = merge_own(head, w_merge, far)
+    head, send_0 = combine_and_merge(v, back, w_merge)
+    in_0 = lax.ppermute(send_0, "sub", core)
+    (send_1,) = merge_far(head, w_merge, ((3, 1),))
+    in_1 = lax.ppermute(send_1, "sub", core)
+    keep_0, keep_1 = merge_far(head, w_merge, ((2, 0), (2, 1)))
+    far_0 = added(keep_0, in_0)
+    cross_0 = lax.ppermute(far_0, "sub", chip)
+    far_1 = added(keep_1, in_1)
+    cross_1 = lax.ppermute(far_1, "sub", chip)
+    own_send, own_keep = merge_own(head, w_merge, far_1)
     own_in = lax.ppermute(own_send, "sub", core)
+    cross = jnp.concatenate([cross_0, cross_1], axis=1)
     return (own_keep.astype(F32) + own_in.astype(F32) + cross.astype(F32)).astype(BF16)
 
 

time: 97.7 us -> 97.5 us (level)
  waiting for transfers between devices: 13.8 us -> 12.2 us
  starting transfers between devices: 1.62 us -> 2.86 us
    ppermute x2 -> x4, starting transfers between devices: 1.17 us -> 2.41 us  [the longest x1 1.05 us: body(): cross_1 = lax.ppermute(far_1, 'sub', chip)]
    ppermute x1, waiting for transfers between devices: 1.12 us -> 0.01 us  [body(): own_in = lax.ppermute(own_send, 'sub', core)]
    ppermute x2 -> x4, waiting for transfers between devices: 12.6 us -> 12.2 us  [the longest x1 6.26 us: body(): cross_0 = lax.ppermute(far_0, 'sub', chip)]
  transfers between devices with their start and end apart: 3 -> 5, of which waited for: 3 -> 3; matrix products, arithmetic and copies ran while one was open for 0% -> 0% of each run, Pallas kernels for 1% -> 2%
where the time goes in v6:
time: 97.5 us; the launch traced here: 97.4 us
  blocking collectives  64.4 us (66%)
  Pallas kernels  15.9 us (16%)
  waiting for transfers between devices  12.2 us (13%)
  starting transfers between devices  2.86 us (3%)
  other arithmetic  1.89 us (2%)
    all_to_all x2, blocking collectives, exchange(): lax.all_to_all(tiles.reshape(peers, ROWS, LANES), axes, split_axis=0, con...  64.4 us
    ppermute x1, waiting for transfers between devices, body(): cross_0 = lax.ppermute(far_0, 'sub', chip)  6.26 us
    pallas_call x1, Pallas kernels, expert_rows(): pl.pallas_call(expert_body, in_specs=[ONCHIP] * 3, out_specs=ONCHIP, out_...  6.11 us
    pallas_call x1, Pallas kernels, split_and_pack(): pl.pallas_call(pack_body, in_specs=[ONCHIP] + [REMOTE] * 2, out_specs=[ON...  5.69 us
    ppermute x1, waiting for transfers between devices, body(): cross_1 = lax.ppermute(far_1, 'sub', chip)  5.62 us
  transfers between devices with their start and end apart: 5, of which 3 were waited for; matrix products, arithmetic and copies ran while one was open for 0% of the time, Pallas kernels for 2%

profile of v6, /device:TPU:1, one launch (start us, length us, event | category | flops | bytes accessed | tf_op | source)
XLA Modules:
  0.0 97.4 jit_solution(2178031098991700454)
XLA Ops:
  0.0 0.7 pad_add_fusion.small_ref
  0.7 0.0 copy-start
  0.7 5.7 %split_pack.1 = (bf16[1024,768]{1,0:T(8,128)(2,1)S(1)}, bf16[256,768]{1,0:T(8,128)(2,1)S(1)}) custom-call(s32[5,256]{1,0:T(8,128)S(1)} %pad_add_fusion.small_ref, bf16[256,4096]{1,0:T(8,128)(2,1)} %tok_hbm.1, bf16[4096,1024]{1,0:T(8,128)(2,1)} %w_hbm.1), custom_call_target="tpu_custom_call" | custom-call | tf_op jit(solution)/shard_map/split_pack/pallas_call | solution.py:142
  6.4 0.0 copy-start.1
  6.4 0.0 slice-start
  6.4 36.0 %all_to_all.10 = bf16[128,8,768]{2,1,0:T(8,128)(2,1)S(1)} all-to-all(bf16[128,8,768]{2,1,0:T(8,128)(2,1)S(1)} %bitcast.16), channel_id=1, replica_groups=mesh['seq'=32,'sub'=4] {'seq','sub'}, dimensions={0} | all-to-all | bytes 3145728 | tf_op jit(solution)/shard_map/all_to_all | solution.py:264
  42.5 0.0 copy-done
  42.5 0.0 copy-done.1
  42.5 0.0 slice-start.1
  42.5 6.1 %experts.1 = bf16[1024,768]{1,0:T(8,128)(2,1)S(1)} custom-call(bf16[1024,768]{1,0:T(8,128)(2,1)S(1)} %bitcast.14, bf16[1,1024,2048]{2,1,0:T(8,128)(2,1)S(1)} %copy-done, bf16[1,1024,1024]{2,1,0:T(8,128)(2,1)S(1)} %copy-done.1), custom_call_target="tpu_custom_call" | custom-call | tf_op jit(solution)/shard_map/experts/pallas_call | solution.py:181
  48.6 28.4 %all_to_all.11 = bf16[128,8,768]{2,1,0:T(8,128)(2,1)S(1)} all-to-all(bf16[128,8,768]{2,1,0:T(8,128)(2,1)S(1)} %bitcast.15), channel_id=1, replica_groups=mesh['seq'=32,'sub'=4] {'seq','sub'}, dimensions={0} | all-to-all | bytes 3145728 | tf_op jit(solution)/shard_map/all_to_all | solution.py:264
  77.0 0.0 slice-done
  77.0 0.0 slice-done.1
  77.0 1.7 %combine_merge.1 = (bf16[256,1024]{1,0:T(8,128)(2,1)S(1)}, bf16[256,512]{1,0:T(8,128)(2,1)S(1)}) custom-call(bf16[256,768]{1,0:T(8,128)(2,1)S(1)} %get-tuple-element.13.v_ref, bf16[1024,768]{1,0:T(8,128)(2,1)S(1)} %bitcast.13, bf16[1024,4096]{1,0:T(8,128)(2,1)S(1)} %bitcast.12), custom_call_target="tpu_custom_call" | custom-call | tf_op jit(solution)/shard_map/combine_merge/pallas_call | solution.py:214
  78.6 0.4 shard_map.83
  79.1 0.8 collective-permute-start
  79.9 0.7 shard_map.82
  80.6 0.1 collective-permute-start.2
  80.7 0.3 collective-permute-done
  81.0 0.1 add_convert_fusion.2.after_ref
  81.1 1.3 %merge_own.1 = (bf16[256,1024]{1,0:T(8,128)(2,1)S(1)}, bf16[256,1024]{1,0:T(8,128)(2,1)S(1)}) custom-call(bf16[256,1024]{1,0:T(8,128)(2,1)S(1)} %get-tuple-element.15.head_ref, bf16[1024,4096]{1,0:T(8,128)(2,1)S(1)} %bitcast.12, bf16[256,512]{1,0:T(8,128)(2,1)S(1)} %add_convert_fusion.2.after_ref), custom_call_target="tpu_custom_call" | custom-call | tf_op jit(solution)/shard_map/merge_own/pallas_call | solution.py:252
  82.4 0.5 collective-permute-start.1
  82.8 0.0 collective-permute-done.2
  82.8 0.1 add_convert_fusion.1
  82.9 0.5 collective-permute-start.3
  83.4 1.0 %collective-permute-start.4 = (bf16[256,512]{1,0:T(8,128)(2,1)S(1)}, bf16[256,512]{1,0:T(8,128)(2,1)S(1)}, u32[]{:S(2)}, u32[]{:S(2)}) collective-permute-start(bf16[256,512]{1,0:T(8,128)(2,1)S(1)} %add_convert_fusion.2.after_ref), channel_id=1, source_target_pairs={{0,2},{1,3},{2,0},{3,1},{4,6},{5,7},{6,4},{7,5},{8,10},{9,11},{10,... | collective-permute-start | bytes 786440 | tf_op jit(solution)/shard_map/ppermute | solution.py:289
  84.4 6.3 %collective-permute-done.3 = bf16[256,512]{1,0:T(8,128)(2,1)S(1)} collective-permute-done((bf16[256,512]{1,0:T(8,128)(2,1)S(1)}, bf16[256,512]{1,0:T(8,128)(2,1)S(1)}, u32[]{:S(2)}, u32[]{:S(2)}) %collective-permute-start.3) | collective-permute-done | bytes 262176 | tf_op jit(solution)/shard_map/ppermute | solution.py:287
  90.7 5.6 %collective-permute-done.4 = bf16[256,512]{1,0:T(8,128)(2,1)S(1)} collective-permute-done((bf16[256,512]{1,0:T(8,128)(2,1)S(1)}, bf16[256,512]{1,0:T(8,128)(2,1)S(1)}, u32[]{:S(2)}, u32[]{:S(2)}) %collective-permute-start.4) | collective-permute-done | bytes 262176 | tf_op jit(solution)/shard_map/ppermute | solution.py:289
  96.3 0.0 collective-permute-done.1
  96.3 1.0 %add_convert_fusion = bf16[256,1024]{1,0:T(8,128)(2,1)} fusion(bf16[256,1024]{1,0:T(8,128)(2,1)S(1)} %collective-permute-done.1, bf16[256,1024]{1,0:T(8,128)(2,1)S(1)} %get-tuple-element.17, bf16[256,512]{1,0:T(8,128)(2,1)S(1)} %collective-permute-done.4, bf16[256,512]{1,0:T(8,128)(2,1)S(1)} %collective-permute-done.3), kind=kLoop, calls=%fused_computation | loop fusion | flops 2359296 | bytes 2097152 | tf_op jit(solution)/shard_map/convert_element_type | solution.py:293
  (1 shorter events, 0.0 us)
Async XLA Ops:
  0.7 41.7 %copy-start = (bf16[1,1024,2048]{2,1,0:T(8,128)(2,1)S(1)}, bf16[1,1024,2048]{2,1,0:T(8,128)(2,1)}, u32[]{:S(2)}) copy-start(bf16[1,1024,2048]{2,1,0:T(8,128)(2,1)} %in_ref.1) | copy-start | bytes 12582916
  6.4 36.0 %copy-start.1 = (bf16[1,1024,1024]{2,1,0:T(8,128)(2,1)S(1)}, bf16[1,1024,1024]{2,1,0:T(8,128)(2,1)}, u32[]{:S(2)}) copy-start(bf16[1,1024,1024]{2,1,0:T(8,128)(2,1)} %down_ref.1) | copy-start | bytes 6291460
  6.4 70.5 %slice-start = ((s8[8388608]{0:T(1024)(128)(4,1)}), s8[4194304]{0:T(1024)(128)(4,1)S(1)}, s32[]{:S(2)}) async-start(s8[8388608]{0:T(1024)(128)(4,1)} %bitcast.11), calls=%async_computation.2 | async-start | bytes 8388608
  42.5 34.5 %slice-start.1 = ((s8[8388608]{0:T(1024)(128)(4,1)}), s8[4194304]{0:T(1024)(128)(4,1)S(1)}, s32[]{:S(2)}) async-start(s8[8388608]{0:T(1024)(128)(4,1)} %bitcast.11), calls=%async_computation.3 | async-start | bytes 8388608
  79.1 1.9 %collective-permute-start = (bf16[256,512]{1,0:T(8,128)(2,1)S(1)}, bf16[256,512]{1,0:T(8,128)(2,1)S(1)}, u32[]{:S(2)}, u32[]{:S(2)}) collective-permute-start(bf16[256,512]{1,0:T(8,128)(2,1)S(1)} %shard_map.83), channel_id=1, source_target_pairs={{0,1},{1,0},{2,3},{3,2},{4,5},{5,4},{6,7},{7,6},{8,9},{9,8},{10,11... | collective-permute-start | bytes 786440 | tf_op jit(solution)/shard_map/ppermute | solution.py:284
  80.6 2.2 %collective-permute-start.2 = (bf16[256,512]{1,0:T(8,128)(2,1)S(1)}, bf16[256,512]{1,0:T(8,128)(2,1)S(1)}, u32[]{:S(2)}, u32[]{:S(2)}) collective-permute-start(bf16[256,512]{1,0:T(8,128)(2,1)S(1)} %get-tuple-element.20), channel_id=1, source_target_pairs={{0,1},{1,0},{2,3},{3,2},{4,5},{5,4},{6,7},{7,6},{8,9},{9,8},{10,11... | collective-permute-start | bytes 786440 | tf_op jit(solution)/shard_map/ppermute | solution.py:282
  82.4 14.0 %collective-permute-start.1 = (bf16[256,1024]{1,0:T(8,128)(2,1)S(1)}, bf16[256,1024]{1,0:T(8,128)(2,1)S(1)}, u32[]{:S(2)}, u32[]{:S(2)}) collective-permute-start(bf16[256,1024]{1,0:T(8,128)(2,1)S(1)} %get-tuple-element.18), channel_id=1, source_target_pairs={{0,1},{1,0},{2,3},{3,2},{4,5},{5,4},{6,7},{7,6},{8,9},{9,8},{10,11... | collective-permute-start | bytes 1572872 | tf_op jit(solution)/shard_map/ppermute | solution.py:291
  82.9 7.8 %collective-permute-start.3 = (bf16[256,512]{1,0:T(8,128)(2,1)S(1)}, bf16[256,512]{1,0:T(8,128)(2,1)S(1)}, u32[]{:S(2)}, u32[]{:S(2)}) collective-permute-start(bf16[256,512]{1,0:T(8,128)(2,1)S(1)} %add_convert_fusion.1), channel_id=1, source_target_pairs={{0,2},{1,3},{2,0},{3,1},{4,6},{5,7},{6,4},{7,5},{8,10},{9,11},{10,... | collective-permute-start | bytes 786440 | tf_op jit(solution)/shard_map/ppermute | solution.py:287
  83.4 12.9 %collective-permute-start.4 = (bf16[256,512]{1,0:T(8,128)(2,1)S(1)}, bf16[256,512]{1,0:T(8,128)(2,1)S(1)}, u32[]{:S(2)}, u32[]{:S(2)}) collective-permute-start(bf16[256,512]{1,0:T(8,128)(2,1)S(1)} %add_convert_fusion.2.after_ref), channel_id=1, source_target_pairs={{0,2},{1,3},{2,0},{3,1},{4,6},{5,7},{6,4},{7,5},{8,10},{9,11},{10,... | collective-permute-start | bytes 786440 | tf_op jit(solution)/shard_map/ppermute | solution.py:289

commit v7 on v6

--- a/solution.py
+++ b/solution.py
@@ -24,7 +24,8 @@
     return [(slot, 0, 0, LANES), (SLOTS + slot // 3, slot % 3 * rest, LANES, rest)]
 
 
-SPLIT, EXPERTS, MERGE_MIB = 52, 24, 24
+EXPERTS, MERGE_MIB = 24, 24
+SPLIT = 52 << 10
 
 
 def iota(shape, dim):
@@ -109,20 +110,30 @@
 PARTS = 8
 
 
-def pack_body(small_ref, tok_hbm, w_hbm, out_ref, v_ref, tok_ref, w_ref, acc_ref, pick_ref, flat_ref, sems):
+def pack_body(
+    ids_hbm, cap_hbm, q_hbm, tok_hbm, w_hbm, out_ref, v_ref, ids_ref, cap_ref, q_ref, tok_ref, w_ref, acc_ref, pick_ref,
+    flat_ref, sems,
+):
     part = w_ref.shape[0] // PARTS
+    small = [
+        pltpu.make_async_copy(frm, to, sems.at[2 * PARTS + n])
+        for n, (frm, to) in enumerate(((ids_hbm, ids_ref), (cap_hbm, cap_ref), (q_hbm, q_ref)))
+    ]
+    fetch(small)
     gets = []
     for n in range(PARTS):
         at = pl.ds(n * part, part)
         gets.append(pltpu.make_async_copy(tok_hbm.at[:, at], tok_ref.at[:, at], sems.at[2 * n]))
         gets.append(pltpu.make_async_copy(w_hbm.at[at, :], w_ref.at[at, :], sems.at[2 * n + 1]))
     fetch(gets)
-    ids = small_ref[0:2, :]
+    for get in small:
+        get.wait()
+    ids = ids_ref[...]
     peers = pick_ref.shape[0] // SLOTS
-    key = slot_keys(ids, small_ref[4:5, :peers])
+    key = slot_keys(ids, cap_ref[...])
     for s in range(SLOTS):
         pick_ref[s * peers : (s + 1) * peers, :] = bits(key == float(s))
-    combine_weights(v_ref, ids, key, small_ref[2:4, :])
+    combine_weights(v_ref, ids, key, q_ref[...])
     for n in range(PARTS):
         gets[2 * n].wait()
         gets[2 * n + 1].wait()
@@ -135,29 +146,31 @@
 
 def split_and_pack(ids, capacity, q, tokens, w_split):
     count = tokens.shape[0]
-    experts = capacity.shape[0]
+    limits = capacity[None, :]
+    experts = limits.shape[1]
     rows = experts * ROWS
-    limits = jnp.pad(capacity[None, :], ((0, 0), (0, count - experts)))
-    small = jnp.concatenate([ids, q, limits], axis=0)
     return pl.pallas_call(
         pack_body,
-        in_specs=[ONCHIP] + [REMOTE] * 2,
+        in_specs=[REMOTE] * 5,
         out_specs=[ONCHIP] * 2,
         out_shape=[
             jax.ShapeDtypeStruct((rows, LANES), BF16),
             jax.ShapeDtypeStruct((count, experts * SLOTS), BF16),
         ],
         scratch_shapes=[
+            pltpu.VMEM(ids.shape, I32),
+            pltpu.VMEM(limits.shape, I32),
+            pltpu.VMEM(q.shape, I32),
             pltpu.VMEM(tokens.shape, BF16),
             pltpu.VMEM(w_split.shape, BF16),
             pltpu.VMEM((count, w_split.shape[1]), F32),
             pltpu.VMEM((experts * SLOTS, count), BF16),
             flat_scratch(rows),
-            pltpu.SemaphoreType.DMA((2 * PARTS,)),
+            pltpu.SemaphoreType.DMA((2 * PARTS + 3,)),
         ],
-        compiler_params=pltpu.CompilerParams(vmem_limit_bytes=SPLIT << 20),
+        compiler_params=pltpu.CompilerParams(vmem_limit_bytes=SPLIT << 10),
         name="split_pack",
-    )(small, tokens, w_split)
+    )(*[pltpu.with_memory_space_constraint(a, pltpu.HBM) for a in (ids, limits, q, tokens, w_split)])
 
 
 def expert_body(x_ref, in_ref, down_ref, out_ref, rows_ref, act_ref, flat_ref):
@@ -200,9 +213,22 @@
 MERGE = pltpu.CompilerParams(vmem_limit_bytes=MERGE_MIB << 20)
 
 
-def combine_body(v_ref, b_ref, w_ref, head_ref, send_ref, rows_ref, flat_ref):
-    from_tiles(rows_ref, flat_ref, b_ref)
-    head = dot(v_ref[...], rows_ref[...]).astype(BF16)
+def combine_body(v_ref, b_ref, w_ref, head_ref, send_ref, flat_ref):
+    peers = b_ref.shape[0] // ROWS
+    for b in range(LANES // 128):
+        flat_ref[b] = b_ref[:, b * 128 : (b + 1) * 128].astype(F32)
+    head = jnp.zeros(head_ref.shape, F32)
+    for first in range(0, SLOTS, 2):
+        answers = []
+        for s in (first, first + 1):
+            parts = [
+                flat_ref[(lane + w) // 128, pl.ds(row, peers, stride=ROWS), :].astype(BF16)
+                for row, lane, col, width in pieces(s)
+                for w in range(0, width, 128)
+            ]
+            answers.append(jnp.concatenate(parts, axis=1))
+        head += dot(v_ref[:, first * peers : (first + 2) * peers], jnp.concatenate(answers, axis=0))
+    head = head.astype(BF16)
     head_ref[...] = head
     send_ref[...] = dot(head, column_block(w_ref, 3, 0)).astype(BF16)
 
@@ -219,7 +245,7 @@
             jax.ShapeDtypeStruct((tokens, width), BF16),
             jax.ShapeDtypeStruct((tokens, width // 2), BF16),
         ],
-        scratch_shapes=[pltpu.VMEM((rows // ROWS * SLOTS, width), BF16), flat_scratch(rows)],
+        scratch_shapes=[flat_scratch(rows)],
         compiler_params=MERGE,
         name="combine_merge",
     )(v, back, w_merge)

time: 97.5 us -> 96.3 us (0.988)
  no operation moved by 1% of the time
where the time goes in v7:
time: 96.3 us; the launch traced here: 96.2 us
  blocking collectives  64.4 us (67%)
  Pallas kernels  15.4 us (16%)
  waiting for transfers between devices  12.2 us (13%)
  starting transfers between devices  2.86 us (3%)
  other arithmetic  1.16 us (1%)
    all_to_all x2, blocking collectives, exchange(): lax.all_to_all(tiles.reshape(peers, ROWS, LANES), axes, split_axis=0, con...  64.4 us
    ppermute x1, waiting for transfers between devices, body(): cross_0 = lax.ppermute(far_0, 'sub', chip)  6.26 us
    pallas_call x1, Pallas kernels, expert_rows(): pl.pallas_call(expert_body, in_specs=[ONCHIP] * 3, out_specs=ONCHIP, out_...  6.01 us
    pallas_call x1, Pallas kernels, split_and_pack(): pl.pallas_call(pack_body, in_specs=[REMOTE] * 5, out_specs=[ONCHIP] * 2,...  5.72 us
    ppermute x1, waiting for transfers between devices, body(): cross_1 = lax.ppermute(far_1, 'sub', chip)  5.62 us
  transfers between devices with their start and end apart: 5, of which 3 were waited for; matrix products, arithmetic and copies ran while one was open for 0% of the time, Pallas kernels for 2%

profile of v7, /device:TPU:1, one launch (start us, length us, event | category | flops | bytes accessed | tf_op | source)
XLA Modules:
  0.0 96.2 jit_solution(833519982938367289)
XLA Ops:
  0.0 0.0 copy-start
  0.0 5.7 %split_pack.1 = (bf16[1024,768]{1,0:T(8,128)(2,1)S(1)}, bf16[256,768]{1,0:T(8,128)(2,1)S(1)}) custom-call(s32[2,256]{1,0:T(2,128)} %bitcast.17, s32[1,128]{1,0:T(1,128)} %bitcast.19, s32[2,256]{1,0:T(2,128)} %bitcast.18, bf16[256,4096]{1,0:T(8,128)(2,1)} %tok_hbm.1, bf16[4096,1024]{1,0:T(8,128)(2,1)} %w_hbm.1), custom_call_target="tpu_custom_call" | custom-call | tf_op jit(solution)/shard_map/split_pack/pallas_call | solution.py:152
  5.7 0.0 copy-start.1
  5.7 0.0 slice-start
  5.8 36.0 %all_to_all.10 = bf16[128,8,768]{2,1,0:T(8,128)(2,1)S(1)} all-to-all(bf16[128,8,768]{2,1,0:T(8,128)(2,1)S(1)} %bitcast.16), channel_id=1, replica_groups=mesh['seq'=32,'sub'=4] {'seq','sub'}, dimensions={0} | all-to-all | bytes 3145728 | tf_op jit(solution)/shard_map/all_to_all | solution.py:290
  41.8 0.0 copy-done
  41.8 0.0 copy-done.1
  41.8 0.0 slice-start.1
  41.8 6.0 %experts.1 = bf16[1024,768]{1,0:T(8,128)(2,1)S(1)} custom-call(bf16[1024,768]{1,0:T(8,128)(2,1)S(1)} %bitcast.14, bf16[1,1024,2048]{2,1,0:T(8,128)(2,1)S(1)} %copy-done, bf16[1,1024,1024]{2,1,0:T(8,128)(2,1)S(1)} %copy-done.1), custom_call_target="tpu_custom_call" | custom-call | tf_op jit(solution)/shard_map/experts/pallas_call | solution.py:194
  47.8 28.4 %all_to_all.11 = bf16[128,8,768]{2,1,0:T(8,128)(2,1)S(1)} all-to-all(bf16[128,8,768]{2,1,0:T(8,128)(2,1)S(1)} %bitcast.15), channel_id=1, replica_groups=mesh['seq'=32,'sub'=4] {'seq','sub'}, dimensions={0} | all-to-all | bytes 3145728 | tf_op jit(solution)/shard_map/all_to_all | solution.py:290
  76.2 0.0 slice-done
  76.2 0.0 slice-done.1
  76.2 1.3 %combine_merge.1 = (bf16[256,1024]{1,0:T(8,128)(2,1)S(1)}, bf16[256,512]{1,0:T(8,128)(2,1)S(1)}) custom-call(bf16[256,768]{1,0:T(8,128)(2,1)S(1)} %get-tuple-element.13.v_ref, bf16[1024,768]{1,0:T(8,128)(2,1)S(1)} %bitcast.13, bf16[1024,4096]{1,0:T(8,128)(2,1)S(1)} %bitcast.12), custom_call_target="tpu_custom_call" | custom-call | tf_op jit(solution)/shard_map/combine_merge/pallas_call | solution.py:240
  77.5 0.4 shard_map.83
  77.9 0.8 collective-permute-start
  78.7 0.7 shard_map.82
  79.4 0.1 collective-permute-start.2
  79.5 0.3 collective-permute-done
  79.8 0.1 add_convert_fusion.2.after_ref
  79.9 1.3 %merge_own.1 = (bf16[256,1024]{1,0:T(8,128)(2,1)S(1)}, bf16[256,1024]{1,0:T(8,128)(2,1)S(1)}) custom-call(bf16[256,1024]{1,0:T(8,128)(2,1)S(1)} %get-tuple-element.15.head_ref, bf16[1024,4096]{1,0:T(8,128)(2,1)S(1)} %bitcast.12, bf16[256,512]{1,0:T(8,128)(2,1)S(1)} %add_convert_fusion.2.after_ref), custom_call_target="tpu_custom_call" | custom-call | tf_op jit(solution)/shard_map/merge_own/pallas_call | solution.py:278
  81.2 0.5 collective-permute-start.1
  81.6 0.0 collective-permute-done.2
  81.6 0.1 add_convert_fusion.1
  81.7 0.5 collective-permute-start.3
  82.2 1.1 %collective-permute-start.4 = (bf16[256,512]{1,0:T(8,128)(2,1)S(1)}, bf16[256,512]{1,0:T(8,128)(2,1)S(1)}, u32[]{:S(2)}, u32[]{:S(2)}) collective-permute-start(bf16[256,512]{1,0:T(8,128)(2,1)S(1)} %add_convert_fusion.2.after_ref), channel_id=1, source_target_pairs={{0,2},{1,3},{2,0},{3,1},{4,6},{5,7},{6,4},{7,5},{8,10},{9,11},{10,... | collective-permute-start | bytes 786440 | tf_op jit(solution)/shard_map/ppermute | solution.py:315
  83.3 6.3 %collective-permute-done.3 = bf16[256,512]{1,0:T(8,128)(2,1)S(1)} collective-permute-done((bf16[256,512]{1,0:T(8,128)(2,1)S(1)}, bf16[256,512]{1,0:T(8,128)(2,1)S(1)}, u32[]{:S(2)}, u32[]{:S(2)}) %collective-permute-start.3) | collective-permute-done | bytes 262176 | tf_op jit(solution)/shard_map/ppermute | solution.py:313
  89.5 5.6 %collective-permute-done.4 = bf16[256,512]{1,0:T(8,128)(2,1)S(1)} collective-permute-done((bf16[256,512]{1,0:T(8,128)(2,1)S(1)}, bf16[256,512]{1,0:T(8,128)(2,1)S(1)}, u32[]{:S(2)}, u32[]{:S(2)}) %collective-permute-start.4) | collective-permute-done | bytes 262176 | tf_op jit(solution)/shard_map/ppermute | solution.py:315
  95.1 0.0 collective-permute-done.1
  95.1 1.0 %add_convert_fusion = bf16[256,1024]{1,0:T(8,128)(2,1)} fusion(bf16[256,1024]{1,0:T(8,128)(2,1)S(1)} %collective-permute-done.1, bf16[256,1024]{1,0:T(8,128)(2,1)S(1)} %get-tuple-element.17, bf16[256,512]{1,0:T(8,128)(2,1)S(1)} %collective-permute-done.4, bf16[256,512]{1,0:T(8,128)(2,1)S(1)} %collective-permute-done.3), kind=kLoop, calls=%fused_computation | loop fusion | flops 2359296 | bytes 2097152 | tf_op jit(solution)/shard_map/convert_element_type | solution.py:319
  (1 shorter events, 0.0 us)
Async XLA Ops:
  0.0 41.8 %copy-start = (bf16[1,1024,2048]{2,1,0:T(8,128)(2,1)S(1)}, bf16[1,1024,2048]{2,1,0:T(8,128)(2,1)}, u32[]{:S(2)}) copy-start(bf16[1,1024,2048]{2,1,0:T(8,128)(2,1)} %in_ref.1) | copy-start | bytes 12582916
  5.7 36.0 %copy-start.1 = (bf16[1,1024,1024]{2,1,0:T(8,128)(2,1)S(1)}, bf16[1,1024,1024]{2,1,0:T(8,128)(2,1)}, u32[]{:S(2)}) copy-start(bf16[1,1024,1024]{2,1,0:T(8,128)(2,1)} %down_ref.1) | copy-start | bytes 6291460
  5.7 70.5 %slice-start = ((s8[8388608]{0:T(1024)(128)(4,1)}), s8[4194304]{0:T(1024)(128)(4,1)S(1)}, s32[]{:S(2)}) async-start(s8[8388608]{0:T(1024)(128)(4,1)} %bitcast.11), calls=%async_computation.2 | async-start | bytes 8388608
  41.8 34.4 %slice-start.1 = ((s8[8388608]{0:T(1024)(128)(4,1)}), s8[4194304]{0:T(1024)(128)(4,1)S(1)}, s32[]{:S(2)}) async-start(s8[8388608]{0:T(1024)(128)(4,1)} %bitcast.11), calls=%async_computation.3 | async-start | bytes 8388608
  77.9 1.9 %collective-permute-start = (bf16[256,512]{1,0:T(8,128)(2,1)S(1)}, bf16[256,512]{1,0:T(8,128)(2,1)S(1)}, u32[]{:S(2)}, u32[]{:S(2)}) collective-permute-start(bf16[256,512]{1,0:T(8,128)(2,1)S(1)} %shard_map.83), channel_id=1, source_target_pairs={{0,1},{1,0},{2,3},{3,2},{4,5},{5,4},{6,7},{7,6},{8,9},{9,8},{10,11... | collective-permute-start | bytes 786440 | tf_op jit(solution)/shard_map/ppermute | solution.py:310
  79.4 2.2 %collective-permute-start.2 = (bf16[256,512]{1,0:T(8,128)(2,1)S(1)}, bf16[256,512]{1,0:T(8,128)(2,1)S(1)}, u32[]{:S(2)}, u32[]{:S(2)}) collective-permute-start(bf16[256,512]{1,0:T(8,128)(2,1)S(1)} %get-tuple-element.20), channel_id=1, source_target_pairs={{0,1},{1,0},{2,3},{3,2},{4,5},{5,4},{6,7},{7,6},{8,9},{9,8},{10,11... | collective-permute-start | bytes 786440 | tf_op jit(solution)/shard_map/ppermute | solution.py:308
  81.2 14.0 %collective-permute-start.1 = (bf16[256,1024]{1,0:T(8,128)(2,1)S(1)}, bf16[256,1024]{1,0:T(8,128)(2,1)S(1)}, u32[]{:S(2)}, u32[]{:S(2)}) collective-permute-start(bf16[256,1024]{1,0:T(8,128)(2,1)S(1)} %get-tuple-element.18), channel_id=1, source_target_pairs={{0,1},{1,0},{2,3},{3,2},{4,5},{5,4},{6,7},{7,6},{8,9},{9,8},{10,11... | collective-permute-start | bytes 1572872 | tf_op jit(solution)/shard_map/ppermute | solution.py:317
  81.7 7.8 %collective-permute-start.3 = (bf16[256,512]{1,0:T(8,128)(2,1)S(1)}, bf16[256,512]{1,0:T(8,128)(2,1)S(1)}, u32[]{:S(2)}, u32[]{:S(2)}) collective-permute-start(bf16[256,512]{1,0:T(8,128)(2,1)S(1)} %add_convert_fusion.1), channel_id=1, source_target_pairs={{0,2},{1,3},{2,0},{3,1},{4,6},{5,7},{6,4},{7,5},{8,10},{9,11},{10,... | collective-permute-start | bytes 786440 | tf_op jit(solution)/shard_map/ppermute | solution.py:313
  82.2 12.9 %collective-permute-start.4 = (bf16[256,512]{1,0:T(8,128)(2,1)S(1)}, bf16[256,512]{1,0:T(8,128)(2,1)S(1)}, u32[]{:S(2)}, u32[]{:S(2)}) collective-permute-start(bf16[256,512]{1,0:T(8,128)(2,1)S(1)} %add_convert_fusion.2.after_ref), channel_id=1, source_target_pairs={{0,2},{1,3},{2,0},{3,1},{4,6},{5,7},{6,4},{7,5},{8,10},{9,11},{10,... | collective-permute-start | bytes 786440 | tf_op jit(solution)/shard_map/ppermute | solution.py:315

commit v8 on v7

--- a/solution.py
+++ b/solution.py
@@ -202,18 +202,19 @@
     )(tiles, expert_in, expert_out)
 
 
+FIRST = 256
+
+
 def column_block(w_ref, other, half=None):
     width = w_ref.shape[0]
-    start = (lax.axis_index("sub") ^ other) * width
-    if half is None:
-        return w_ref[:, pl.ds(pl.multiple_of(start, width), width)]
-    return w_ref[:, pl.ds(pl.multiple_of(start + half * (width // 2), width // 2), width // 2)]
+    start, size = {None: (0, width), 0: (0, FIRST), 1: (FIRST, width - FIRST)}[half]
+    return w_ref[:, pl.ds(pl.multiple_of((lax.axis_index("sub") ^ other) * width + start, 128), size)]
 
 
 MERGE = pltpu.CompilerParams(vmem_limit_bytes=MERGE_MIB << 20)
 
 
-def combine_body(v_ref, b_ref, w_ref, head_ref, send_ref, flat_ref):
+def combine_body(v_ref, b_ref, w_ref, head_ref, send_ref, keep_ref, flat_ref):
     peers = b_ref.shape[0] // ROWS
     for b in range(LANES // 128):
         flat_ref[b] = b_ref[:, b * 128 : (b + 1) * 128].astype(F32)
@@ -231,6 +232,7 @@
     head = head.astype(BF16)
     head_ref[...] = head
     send_ref[...] = dot(head, column_block(w_ref, 3, 0)).astype(BF16)
+    keep_ref[...] = dot(head, column_block(w_ref, 2, 0)).astype(BF16)
 
 
 def combine_and_merge(v, back, w_merge):
@@ -240,10 +242,11 @@
     return pl.pallas_call(
         combine_body,
         in_specs=[ONCHIP] * 3,
-        out_specs=[ONCHIP] * 2,
+        out_specs=[ONCHIP] * 3,
         out_shape=[
             jax.ShapeDtypeStruct((tokens, width), BF16),
-            jax.ShapeDtypeStruct((tokens, width // 2), BF16),
+            jax.ShapeDtypeStruct((tokens, FIRST), BF16),
+            jax.ShapeDtypeStruct((tokens, FIRST), BF16),
         ],
         scratch_shapes=[flat_scratch(rows)],
         compiler_params=MERGE,
@@ -262,7 +265,7 @@
         functools.partial(far_body, blocks),
         in_specs=[ONCHIP] * 2,
         out_specs=[ONCHIP] * len(blocks),
-        out_shape=[jax.ShapeDtypeStruct((tokens, width // 2), BF16)] * len(blocks),
+        out_shape=[jax.ShapeDtypeStruct((tokens, (FIRST, width - FIRST)[half]), BF16) for _, half in blocks],
         compiler_params=MERGE,
     )(head, w_merge)
 
@@ -304,11 +307,11 @@
 
     core = [(i, i ^ 1) for i in range(4)]
     chip = [(i, i ^ 2) for i in range(4)]
-    head, send_0 = combine_and_merge(v, back, w_merge)
+    head, send_0, keep_0 = combine_and_merge(v, back, w_merge)
     in_0 = lax.ppermute(send_0, "sub", core)
     (send_1,) = merge_far(head, w_merge, ((3, 1),))
     in_1 = lax.ppermute(send_1, "sub", core)
-    keep_0, keep_1 = merge_far(head, w_merge, ((2, 0), (2, 1)))
+    (keep_1,) = merge_far(head, w_merge, ((2, 1),))
     far_0 = added(keep_0, in_0)
     cross_0 = lax.ppermute(far_0, "sub", chip)
     far_1 = added(keep_1, in_1)

time: 96.3 us -> 96.4 us (level)
    ppermute x1, waiting for transfers between devices: 5.62 us -> 0.01 us  [body(): cross_1 = lax.ppermute(far_1, 'sub', chip)]
    ppermute x1, waiting for transfers between devices: 6.26 us -> 11 us  [body(): cross_0 = lax.ppermute(far_0, 'sub', chip)]
    ppermute x1, waiting for transfers between devices: 0.01 us -> 1.17 us  [body(): in_0 = lax.ppermute(send_0, 'sub', core)]
  transfers between devices with their start and end apart: 5 -> 5, of which waited for: 3 -> 3; matrix products, arithmetic and copies ran while one was open for 0% -> 0% of each run, Pallas kernels for 2% -> 1%
where the time goes in v8:
time: 96.4 us; the launch traced here: 96.3 us
  blocking collectives  64.4 us (67%)
  Pallas kernels  15.4 us (16%)
  waiting for transfers between devices  12.9 us (13%)
  starting transfers between devices  2.26 us (2%)
  other arithmetic  1.14 us (1%)
    all_to_all x2, blocking collectives, exchange(): lax.all_to_all(tiles.reshape(peers, ROWS, LANES), axes, split_axis=0, con...  64.4 us
    ppermute x1, waiting for transfers between devices, body(): cross_0 = lax.ppermute(far_0, 'sub', chip)  11 us
    pallas_call x1, Pallas kernels, expert_rows(): pl.pallas_call(expert_body, in_specs=[ONCHIP] * 3, out_specs=ONCHIP, out_...  6.01 us
    pallas_call x1, Pallas kernels, split_and_pack(): pl.pallas_call(pack_body, in_specs=[REMOTE] * 5, out_specs=[ONCHIP] * 2,...  5.72 us
  transfers between devices with their start and end apart: 5, of which 3 were waited for; matrix products, arithmetic and copies ran while one was open for 0% of the time, Pallas kernels for 1%

profile of v8, /device:TPU:1, one launch (start us, length us, event | category | flops | bytes accessed | tf_op | source)
XLA Modules:
  0.0 96.3 jit_solution(11527688155340557649)
XLA Ops:
  0.0 0.0 copy-start
  0.0 5.7 %split_pack.1 = (bf16[1024,768]{1,0:T(8,128)(2,1)S(1)}, bf16[256,768]{1,0:T(8,128)(2,1)S(1)}) custom-call(s32[2,256]{1,0:T(2,128)} %bitcast.17, s32[1,128]{1,0:T(1,128)} %bitcast.19, s32[2,256]{1,0:T(2,128)} %bitcast.18, bf16[256,4096]{1,0:T(8,128)(2,1)} %tok_hbm.1, bf16[4096,1024]{1,0:T(8,128)(2,1)} %w_hbm.1), custom_call_target="tpu_custom_call" | custom-call | tf_op jit(solution)/shard_map/split_pack/pallas_call | solution.py:152
  5.7 0.0 copy-start.1
  5.7 0.0 slice-start
  5.8 36.0 %all_to_all.10 = bf16[128,8,768]{2,1,0:T(8,128)(2,1)S(1)} all-to-all(bf16[128,8,768]{2,1,0:T(8,128)(2,1)S(1)} %bitcast.16), channel_id=1, replica_groups=mesh['seq'=32,'sub'=4] {'seq','sub'}, dimensions={0} | all-to-all | bytes 3145728 | tf_op jit(solution)/shard_map/all_to_all | solution.py:293
  41.8 0.0 copy-done
  41.8 0.0 copy-done.1
  41.8 0.0 slice-start.1
  41.8 6.0 %experts.1 = bf16[1024,768]{1,0:T(8,128)(2,1)S(1)} custom-call(bf16[1024,768]{1,0:T(8,128)(2,1)S(1)} %bitcast.14, bf16[1,1024,2048]{2,1,0:T(8,128)(2,1)S(1)} %copy-done, bf16[1,1024,1024]{2,1,0:T(8,128)(2,1)S(1)} %copy-done.1), custom_call_target="tpu_custom_call" | custom-call | tf_op jit(solution)/shard_map/experts/pallas_call | solution.py:194
  47.8 28.4 %all_to_all.11 = bf16[128,8,768]{2,1,0:T(8,128)(2,1)S(1)} all-to-all(bf16[128,8,768]{2,1,0:T(8,128)(2,1)S(1)} %bitcast.15), channel_id=1, replica_groups=mesh['seq'=32,'sub'=4] {'seq','sub'}, dimensions={0} | all-to-all | bytes 3145728 | tf_op jit(solution)/shard_map/all_to_all | solution.py:293
  76.2 0.0 slice-done
  76.2 0.0 slice-done.1
  76.2 1.2 %combine_merge.1 = (bf16[256,1024]{1,0:T(8,128)(2,1)S(1)}, bf16[256,256]{1,0:T(8,128)(2,1)S(1)}, bf16[256,256]{1,0:T(8,128)(2,1)S(1)}) custom-call(bf16[256,768]{1,0:T(8,128)(2,1)S(1)} %get-tuple-element.12.v_ref, bf16[1024,768]{1,0:T(8,128)(2,1)S(1)} %bitcast.13, bf16[1024,4096]{1,0:T(8,128)(2,1)S(1)} %bitcast.12), custom_call_target="tpu_custom_call" | custom-call | tf_op jit(solution)/shard_map/combine_merge/pallas_call | solution.py:242
  77.5 0.6 shard_map.83
  78.1 0.8 collective-permute-start
  78.8 0.6 shard_map.82
  79.4 0.8 collective-permute-done
  80.2 0.1 add_convert_fusion.1.after_ref
  80.3 1.3 %merge_own.1 = (bf16[256,1024]{1,0:T(8,128)(2,1)S(1)}, bf16[256,1024]{1,0:T(8,128)(2,1)S(1)}) custom-call(bf16[256,1024]{1,0:T(8,128)(2,1)S(1)} %get-tuple-element.14.head_ref, bf16[1024,4096]{1,0:T(8,128)(2,1)S(1)} %bitcast.12, bf16[256,768]{1,0:T(8,128)(2,1)S(1)} %add_convert_fusion.1.after_ref), custom_call_target="tpu_custom_call" | custom-call | tf_op jit(solution)/shard_map/merge_own/pallas_call | solution.py:281
  81.5 0.5 collective-permute-start.1
  82.0 0.1 collective-permute-start.2
  82.1 0.4 collective-permute-start.4
  82.5 1.2 %collective-permute-done.2 = bf16[256,256]{1,0:T(8,128)(2,1)S(1)} collective-permute-done((bf16[256,256]{1,0:T(8,128)(2,1)S(1)}, bf16[256,256]{1,0:T(8,128)(2,1)S(1)}, u32[]{:S(2)}, u32[]{:S(2)}) %collective-permute-start.2) | collective-permute-done | bytes 131104 | tf_op jit(solution)/shard_map/ppermute | solution.py:311
  83.8 0.5 collective-permute-start.3
  84.2 11.0 %collective-permute-done.3 = bf16[256,256]{1,0:T(8,128)(2,1)S(1)} collective-permute-done((bf16[256,256]{1,0:T(8,128)(2,1)S(1)}, bf16[256,256]{1,0:T(8,128)(2,1)S(1)}, u32[]{:S(2)}, u32[]{:S(2)}) %collective-permute-start.3) | collective-permute-done | bytes 131104 | tf_op jit(solution)/shard_map/ppermute | solution.py:316
  95.2 0.0 collective-permute-done.4
  95.2 0.0 collective-permute-done.1
  95.2 1.0 %add_convert_fusion = bf16[256,1024]{1,0:T(8,128)(2,1)} fusion(bf16[256,1024]{1,0:T(8,128)(2,1)S(1)} %collective-permute-done.1, bf16[256,1024]{1,0:T(8,128)(2,1)S(1)} %get-tuple-element.15, bf16[256,768]{1,0:T(8,128)(2,1)S(1)} %collective-permute-done.4, bf16[256,256]{1,0:T(8,128)(2,1)S(1)} %collective-permute-done.3), kind=kLoop, calls=%fused_computation | loop fusion | flops 2359296 | bytes 2097152 | tf_op jit(solution)/shard_map/convert_element_type | solution.py:322
  (2 shorter events, 0.0 us)
Async XLA Ops:
  0.0 41.8 %copy-start = (bf16[1,1024,2048]{2,1,0:T(8,128)(2,1)S(1)}, bf16[1,1024,2048]{2,1,0:T(8,128)(2,1)}, u32[]{:S(2)}) copy-start(bf16[1,1024,2048]{2,1,0:T(8,128)(2,1)} %in_ref.1) | copy-start | bytes 12582916
  5.7 36.0 %copy-start.1 = (bf16[1,1024,1024]{2,1,0:T(8,128)(2,1)S(1)}, bf16[1,1024,1024]{2,1,0:T(8,128)(2,1)}, u32[]{:S(2)}) copy-start(bf16[1,1024,1024]{2,1,0:T(8,128)(2,1)} %down_ref.1) | copy-start | bytes 6291460
  5.7 70.5 %slice-start = ((s8[8388608]{0:T(1024)(128)(4,1)}), s8[4194304]{0:T(1024)(128)(4,1)S(1)}, s32[]{:S(2)}) async-start(s8[8388608]{0:T(1024)(128)(4,1)} %bitcast.11), calls=%async_computation.2 | async-start | bytes 8388608
  41.8 34.4 %slice-start.1 = ((s8[8388608]{0:T(1024)(128)(4,1)}), s8[4194304]{0:T(1024)(128)(4,1)S(1)}, s32[]{:S(2)}) async-start(s8[8388608]{0:T(1024)(128)(4,1)} %bitcast.11), calls=%async_computation.3 | async-start | bytes 8388608
  78.1 2.1 %collective-permute-start = (bf16[256,768]{1,0:T(8,128)(2,1)S(1)}, bf16[256,768]{1,0:T(8,128)(2,1)S(1)}, u32[]{:S(2)}, u32[]{:S(2)}) collective-permute-start(bf16[256,768]{1,0:T(8,128)(2,1)S(1)} %shard_map.83), channel_id=1, source_target_pairs={{0,1},{1,0},{2,3},{3,2},{4,5},{5,4},{6,7},{7,6},{8,9},{9,8},{10,11... | collective-permute-start | bytes 1179656 | tf_op jit(solution)/shard_map/ppermute | solution.py:313
  81.5 13.7 %collective-permute-start.1 = (bf16[256,1024]{1,0:T(8,128)(2,1)S(1)}, bf16[256,1024]{1,0:T(8,128)(2,1)S(1)}, u32[]{:S(2)}, u32[]{:S(2)}) collective-permute-start(bf16[256,1024]{1,0:T(8,128)(2,1)S(1)} %get-tuple-element.16), channel_id=1, source_target_pairs={{0,1},{1,0},{2,3},{3,2},{4,5},{5,4},{6,7},{7,6},{8,9},{9,8},{10,11... | collective-permute-start | bytes 1572872 | tf_op jit(solution)/shard_map/ppermute | solution.py:320
  82.0 1.7 %collective-permute-start.2 = (bf16[256,256]{1,0:T(8,128)(2,1)S(1)}, bf16[256,256]{1,0:T(8,128)(2,1)S(1)}, u32[]{:S(2)}, u32[]{:S(2)}) collective-permute-start(bf16[256,256]{1,0:T(8,128)(2,1)S(1)} %get-tuple-element.18), channel_id=1, source_target_pairs={{0,1},{1,0},{2,3},{3,2},{4,5},{5,4},{6,7},{7,6},{8,9},{9,8},{10,11... | collective-permute-start | bytes 393224 | tf_op jit(solution)/shard_map/ppermute | solution.py:311
  82.1 13.1 %collective-permute-start.4 = (bf16[256,768]{1,0:T(8,128)(2,1)S(1)}, bf16[256,768]{1,0:T(8,128)(2,1)S(1)}, u32[]{:S(2)}, u32[]{:S(2)}) collective-permute-start(bf16[256,768]{1,0:T(8,128)(2,1)S(1)} %add_convert_fusion.1.after_ref), channel_id=1, source_target_pairs={{0,2},{1,3},{2,0},{3,1},{4,6},{5,7},{6,4},{7,5},{8,10},{9,11},{10,... | collective-permute-start | bytes 1179656 | tf_op jit(solution)/shard_map/ppermute | solution.py:318
  83.8 11.5 %collective-permute-start.3 = (bf16[256,256]{1,0:T(8,128)(2,1)S(1)}, bf16[256,256]{1,0:T(8,128)(2,1)S(1)}, u32[]{:S(2)}, u32[]{:S(2)}) collective-permute-start(bf16[256,256]{1,0:T(8,128)(2,1)S(1)} %add_convert_fusion.2), channel_id=1, source_target_pairs={{0,2},{1,3},{2,0},{3,1},{4,6},{5,7},{6,4},{7,5},{8,10},{9,11},{10,... | collective-permute-start | bytes 393224 | tf_op jit(solution)/shard_map/ppermute | solution.py:316

commit v9 on v8

--- a/solution.py
+++ b/solution.py
@@ -288,6 +288,35 @@
     )(head, w_merge, after)
 
 
+WRITES = 4
+
+
+def last_body(keep_ref, in_ref, cross_0_ref, cross_1_ref, out_hbm, sum_ref, sems):
+    rows = sum_ref.shape[0] // WRITES
+    puts = []
+    for n in range(WRITES):
+        at = slice(n * rows, (n + 1) * rows)
+        own = keep_ref[at, :].astype(F32) + in_ref[at, :].astype(F32)
+        sum_ref[at, :FIRST] = (own[:, :FIRST] + cross_0_ref[at, :].astype(F32)).astype(BF16)
+        sum_ref[at, FIRST:] = (own[:, FIRST:] + cross_1_ref[at, :].astype(F32)).astype(BF16)
+        piece = pl.ds(n * rows, rows)
+        puts += fetch([pltpu.make_async_copy(sum_ref.at[piece, :], out_hbm.at[piece, :], sems.at[n])])
+    for put in puts:
+        put.wait()
+
+
+def last_sum(own_keep, own_in, cross_0, cross_1):
+    return pl.pallas_call(
+        last_body,
+        in_specs=[ONCHIP] * 4,
+        out_specs=REMOTE,
+        out_shape=jax.ShapeDtypeStruct(own_keep.shape, BF16),
+        scratch_shapes=[pltpu.VMEM(own_keep.shape, BF16), pltpu.SemaphoreType.DMA((WRITES,))],
+        compiler_params=MERGE,
+        name="last_sum",
+    )(own_keep, own_in, cross_0, cross_1)
+
+
 def exchange(tiles, axes):
     peers = tiles.shape[0] // ROWS
     return lax.all_to_all(tiles.reshape(peers, ROWS, LANES), axes, split_axis=0, concat_axis=0, tiled=True).reshape(tiles.shape)
@@ -318,8 +347,7 @@
     cross_1 = lax.ppermute(far_1, "sub", chip)
     own_send, own_keep = merge_own(head, w_merge, far_1)
     own_in = lax.ppermute(own_send, "sub", core)
-    cross = jnp.concatenate([cross_0, cross_1], axis=1)
-    return (own_keep.astype(F32) + own_in.astype(F32) + cross.astype(F32)).astype(BF16)
+    return last_sum(own_keep, own_in, cross_0, cross_1)
 
 
 def solution(mesh):

time: 96.4 us -> 96.2 us (level)
  other arithmetic: 1.14 us -> 0.13 us
    convert_element_type x1 -> x0, other arithmetic: 1.02 us -> none  [body(): (own_keep.astype(F32) + own_in.astype(F32) + cross.astype(F32)).astype(BF16)]
where the time goes in v9:
time: 96.2 us; the launch traced here: 96.1 us
  blocking collectives  64.4 us (67%)
  Pallas kernels  16.3 us (17%)
  waiting for transfers between devices  12.9 us (13%)
  starting transfers between devices  2.26 us (2%)
    all_to_all x2, blocking collectives, exchange(): lax.all_to_all(tiles.reshape(peers, ROWS, LANES), axes, split_axis=0, con...  64.4 us
    ppermute x1, waiting for transfers between devices, body(): cross_0 = lax.ppermute(far_0, 'sub', chip)  11 us
    pallas_call x1, Pallas kernels, expert_rows(): pl.pallas_call(expert_body, in_specs=[ONCHIP] * 3, out_specs=ONCHIP, out_...  6.01 us
    pallas_call x1, Pallas kernels, split_and_pack(): pl.pallas_call(pack_body, in_specs=[REMOTE] * 5, out_specs=[ONCHIP] * 2,...  5.72 us
  transfers between devices with their start and end apart: 5, of which 3 were waited for; matrix products, arithmetic and copies ran while one was open for 0% of the time, Pallas kernels for 1%

profile of v9, /device:TPU:1, one launch (start us, length us, event | category | flops | bytes accessed | tf_op | source)
XLA Modules:
  0.0 96.1 jit_solution(15529335432424109808)
XLA Ops:
  0.0 0.0 copy-start
  0.0 5.7 %split_pack.1 = (bf16[1024,768]{1,0:T(8,128)(2,1)S(1)}, bf16[256,768]{1,0:T(8,128)(2,1)S(1)}) custom-call(s32[2,256]{1,0:T(2,128)} %bitcast.17, s32[1,128]{1,0:T(1,128)} %bitcast.19, s32[2,256]{1,0:T(2,128)} %bitcast.18, bf16[256,4096]{1,0:T(8,128)(2,1)} %tok_hbm.1, bf16[4096,1024]{1,0:T(8,128)(2,1)} %w_hbm.1), custom_call_target="tpu_custom_call" | custom-call | tf_op jit(solution)/shard_map/split_pack/pallas_call | solution.py:152
  5.7 0.0 copy-start.1
  5.7 0.0 slice-start
  5.8 36.0 %all_to_all.10 = bf16[128,8,768]{2,1,0:T(8,128)(2,1)S(1)} all-to-all(bf16[128,8,768]{2,1,0:T(8,128)(2,1)S(1)} %bitcast.16), channel_id=1, replica_groups=mesh['seq'=32,'sub'=4] {'seq','sub'}, dimensions={0} | all-to-all | bytes 3145728 | tf_op jit(solution)/shard_map/all_to_all | solution.py:322
  41.8 0.0 copy-done
  41.8 0.0 copy-done.1
  41.8 0.0 slice-start.1
  41.8 6.0 %experts.1 = bf16[1024,768]{1,0:T(8,128)(2,1)S(1)} custom-call(bf16[1024,768]{1,0:T(8,128)(2,1)S(1)} %bitcast.14, bf16[1,1024,2048]{2,1,0:T(8,128)(2,1)S(1)} %copy-done, bf16[1,1024,1024]{2,1,0:T(8,128)(2,1)S(1)} %copy-done.1), custom_call_target="tpu_custom_call" | custom-call | tf_op jit(solution)/shard_map/experts/pallas_call | solution.py:194
  47.8 28.4 %all_to_all.11 = bf16[128,8,768]{2,1,0:T(8,128)(2,1)S(1)} all-to-all(bf16[128,8,768]{2,1,0:T(8,128)(2,1)S(1)} %bitcast.15), channel_id=1, replica_groups=mesh['seq'=32,'sub'=4] {'seq','sub'}, dimensions={0} | all-to-all | bytes 3145728 | tf_op jit(solution)/shard_map/all_to_all | solution.py:322
  76.2 0.0 slice-done
  76.2 0.0 slice-done.1
  76.2 1.2 %combine_merge.1 = (bf16[256,1024]{1,0:T(8,128)(2,1)S(1)}, bf16[256,256]{1,0:T(8,128)(2,1)S(1)}, bf16[256,256]{1,0:T(8,128)(2,1)S(1)}) custom-call(bf16[256,768]{1,0:T(8,128)(2,1)S(1)} %get-tuple-element.12.v_ref, bf16[1024,768]{1,0:T(8,128)(2,1)S(1)} %bitcast.13, bf16[1024,4096]{1,0:T(8,128)(2,1)S(1)} %bitcast.12), custom_call_target="tpu_custom_call" | custom-call | tf_op jit(solution)/shard_map/combine_merge/pallas_call | solution.py:242
  77.5 0.6 shard_map.83
  78.1 0.8 collective-permute-start
  78.8 0.6 shard_map.82
  79.4 0.8 collective-permute-done
  80.2 0.1 add_convert_fusion.after_ref
  80.3 1.3 %merge_own.1 = (bf16[256,1024]{1,0:T(8,128)(2,1)S(1)}, bf16[256,1024]{1,0:T(8,128)(2,1)S(1)}) custom-call(bf16[256,1024]{1,0:T(8,128)(2,1)S(1)} %get-tuple-element.14.head_ref, bf16[1024,4096]{1,0:T(8,128)(2,1)S(1)} %bitcast.12, bf16[256,768]{1,0:T(8,128)(2,1)S(1)} %add_convert_fusion.after_ref), custom_call_target="tpu_custom_call" | custom-call | tf_op jit(solution)/shard_map/merge_own/pallas_call | solution.py:281
  81.5 0.5 collective-permute-start.1
  82.0 0.1 collective-permute-start.2
  82.1 0.4 collective-permute-start.4
  82.5 1.2 %collective-permute-done.2 = bf16[256,256]{1,0:T(8,128)(2,1)S(1)} collective-permute-done((bf16[256,256]{1,0:T(8,128)(2,1)S(1)}, bf16[256,256]{1,0:T(8,128)(2,1)S(1)}, u32[]{:S(2)}, u32[]{:S(2)}) %collective-permute-start.2) | collective-permute-done | bytes 131104 | tf_op jit(solution)/shard_map/ppermute | solution.py:340
  83.8 0.5 collective-permute-start.3
  84.2 11.0 %collective-permute-done.3.cross_0_ref = bf16[256,256]{1,0:T(8,128)(2,1)S(1)} collective-permute-done((bf16[256,256]{1,0:T(8,128)(2,1)S(1)}, bf16[256,256]{1,0:T(8,128)(2,1)S(1)}, u32[]{:S(2)}, u32[]{:S(2)}) %collective-permute-start.3) | collective-permute-done | bytes 131104 | tf_op jit(solution)/shard_map/ppermute | solution.py:345
  95.2 0.0 collective-permute-done.4.cross_1_ref
  95.2 0.0 collective-permute-done.1.in_ref
  95.2 0.9 last_sum.1
  (2 shorter events, 0.0 us)
Async XLA Ops:
  0.0 41.8 %copy-start = (bf16[1,1024,2048]{2,1,0:T(8,128)(2,1)S(1)}, bf16[1,1024,2048]{2,1,0:T(8,128)(2,1)}, u32[]{:S(2)}) copy-start(bf16[1,1024,2048]{2,1,0:T(8,128)(2,1)} %in_ref.1) | copy-start | bytes 12582916
  5.7 36.0 %copy-start.1 = (bf16[1,1024,1024]{2,1,0:T(8,128)(2,1)S(1)}, bf16[1,1024,1024]{2,1,0:T(8,128)(2,1)}, u32[]{:S(2)}) copy-start(bf16[1,1024,1024]{2,1,0:T(8,128)(2,1)} %down_ref.1) | copy-start | bytes 6291460
  5.7 70.5 %slice-start = ((s8[8388608]{0:T(1024)(128)(4,1)}), s8[4194304]{0:T(1024)(128)(4,1)S(1)}, s32[]{:S(2)}) async-start(s8[8388608]{0:T(1024)(128)(4,1)} %bitcast.11), calls=%async_computation.2 | async-start | bytes 8388608
  41.8 34.4 %slice-start.1 = ((s8[8388608]{0:T(1024)(128)(4,1)}), s8[4194304]{0:T(1024)(128)(4,1)S(1)}, s32[]{:S(2)}) async-start(s8[8388608]{0:T(1024)(128)(4,1)} %bitcast.11), calls=%async_computation.3 | async-start | bytes 8388608
  78.1 2.1 %collective-permute-start = (bf16[256,768]{1,0:T(8,128)(2,1)S(1)}, bf16[256,768]{1,0:T(8,128)(2,1)S(1)}, u32[]{:S(2)}, u32[]{:S(2)}) collective-permute-start(bf16[256,768]{1,0:T(8,128)(2,1)S(1)} %shard_map.83), channel_id=1, source_target_pairs={{0,1},{1,0},{2,3},{3,2},{4,5},{5,4},{6,7},{7,6},{8,9},{9,8},{10,11... | collective-permute-start | bytes 1179656 | tf_op jit(solution)/shard_map/ppermute | solution.py:342
  81.5 13.7 %collective-permute-start.1 = (bf16[256,1024]{1,0:T(8,128)(2,1)S(1)}, bf16[256,1024]{1,0:T(8,128)(2,1)S(1)}, u32[]{:S(2)}, u32[]{:S(2)}) collective-permute-start(bf16[256,1024]{1,0:T(8,128)(2,1)S(1)} %get-tuple-element.16), channel_id=1, source_target_pairs={{0,1},{1,0},{2,3},{3,2},{4,5},{5,4},{6,7},{7,6},{8,9},{9,8},{10,11... | collective-permute-start | bytes 1572872 | tf_op jit(solution)/shard_map/ppermute | solution.py:349
  82.0 1.7 %collective-permute-start.2 = (bf16[256,256]{1,0:T(8,128)(2,1)S(1)}, bf16[256,256]{1,0:T(8,128)(2,1)S(1)}, u32[]{:S(2)}, u32[]{:S(2)}) collective-permute-start(bf16[256,256]{1,0:T(8,128)(2,1)S(1)} %get-tuple-element.18), channel_id=1, source_target_pairs={{0,1},{1,0},{2,3},{3,2},{4,5},{5,4},{6,7},{7,6},{8,9},{9,8},{10,11... | collective-permute-start | bytes 393224 | tf_op jit(solution)/shard_map/ppermute | solution.py:340
  82.1 13.1 %collective-permute-start.4 = (bf16[256,768]{1,0:T(8,128)(2,1)S(1)}, bf16[256,768]{1,0:T(8,128)(2,1)S(1)}, u32[]{:S(2)}, u32[]{:S(2)}) collective-permute-start(bf16[256,768]{1,0:T(8,128)(2,1)S(1)} %add_convert_fusion.after_ref), channel_id=1, source_target_pairs={{0,2},{1,3},{2,0},{3,1},{4,6},{5,7},{6,4},{7,5},{8,10},{9,11},{10,... | collective-permute-start | bytes 1179656 | tf_op jit(solution)/shard_map/ppermute | solution.py:347
  83.8 11.5 %collective-permute-start.3 = (bf16[256,256]{1,0:T(8,128)(2,1)S(1)}, bf16[256,256]{1,0:T(8,128)(2,1)S(1)}, u32[]{:S(2)}, u32[]{:S(2)}) collective-permute-start(bf16[256,256]{1,0:T(8,128)(2,1)S(1)} %add_convert_fusion.1), channel_id=1, source_target_pairs={{0,2},{1,3},{2,0},{3,1},{4,6},{5,7},{6,4},{7,5},{8,10},{9,11},{10,... | collective-permute-start | bytes 393224 | tf_op jit(solution)/shard_map/ppermute | solution.py:345

commit v10 on v9

--- a/solution.py
+++ b/solution.py
@@ -291,12 +291,27 @@
 WRITES = 4
 
 
-def last_body(keep_ref, in_ref, cross_0_ref, cross_1_ref, out_hbm, sum_ref, sems):
+def own_sum_body(keep_ref, in_ref, out_ref):
+    out_ref[...] = keep_ref[...].astype(F32) + in_ref[...].astype(F32)
+
+
+def own_sum(own_keep, own_in):
+    return pl.pallas_call(
+        own_sum_body,
+        in_specs=[ONCHIP] * 2,
+        out_specs=ONCHIP,
+        out_shape=jax.ShapeDtypeStruct(own_keep.shape, F32),
+        compiler_params=MERGE,
+        name="own_sum",
+    )(own_keep, own_in)
+
+
+def last_body(own_ref, cross_0_ref, cross_1_ref, out_hbm, sum_ref, sems):
     rows = sum_ref.shape[0] // WRITES
     puts = []
     for n in range(WRITES):
         at = slice(n * rows, (n + 1) * rows)
-        own = keep_ref[at, :].astype(F32) + in_ref[at, :].astype(F32)
+        own = own_ref[at, :]
         sum_ref[at, :FIRST] = (own[:, :FIRST] + cross_0_ref[at, :].astype(F32)).astype(BF16)
         sum_ref[at, FIRST:] = (own[:, FIRST:] + cross_1_ref[at, :].astype(F32)).astype(BF16)
         piece = pl.ds(n * rows, rows)
@@ -305,16 +320,16 @@
         put.wait()
 
 
-def last_sum(own_keep, own_in, cross_0, cross_1):
+def last_sum(own, cross_0, cross_1):
     return pl.pallas_call(
         last_body,
-        in_specs=[ONCHIP] * 4,
+        in_specs=[ONCHIP] * 3,
         out_specs=REMOTE,
-        out_shape=jax.ShapeDtypeStruct(own_keep.shape, BF16),
-        scratch_shapes=[pltpu.VMEM(own_keep.shape, BF16), pltpu.SemaphoreType.DMA((WRITES,))],
+        out_shape=jax.ShapeDtypeStruct(own.shape, BF16),
+        scratch_shapes=[pltpu.VMEM(own.shape, BF16), pltpu.SemaphoreType.DMA((WRITES,))],
         compiler_params=MERGE,
         name="last_sum",
-    )(own_keep, own_in, cross_0, cross_1)
+    )(own, cross_0, cross_1)
 
 
 def exchange(tiles, axes):
@@ -347,7 +362,8 @@
     cross_1 = lax.ppermute(far_1, "sub", chip)
     own_send, own_keep = merge_own(head, w_merge, far_1)
     own_in = lax.ppermute(own_send, "sub", core)
-    return last_sum(own_keep, own_in, cross_0, cross_1)
+    own = own_sum(own_keep, own_in)
+    return last_sum(own, cross_0, cross_1)
 
 
 def solution(mesh):

time: 96.2 us -> 96.2 us (level)
  no operation moved by 1% of the time
where the time goes in v10:
time: 96.2 us; the launch traced here: 96.1 us
  blocking collectives  64.4 us (67%)
  Pallas kernels  16.4 us (17%)
  waiting for transfers between devices  12.8 us (13%)
  starting transfers between devices  2.26 us (2%)
    all_to_all x2, blocking collectives, exchange(): lax.all_to_all(tiles.reshape(peers, ROWS, LANES), axes, split_axis=0, con...  64.4 us
    ppermute x1, waiting for transfers between devices, body(): cross_0 = lax.ppermute(far_0, 'sub', chip)  10.9 us
    pallas_call x1, Pallas kernels, expert_rows(): pl.pallas_call(expert_body, in_specs=[ONCHIP] * 3, out_specs=ONCHIP, out_...  6.01 us
    pallas_call x1, Pallas kernels, split_and_pack(): pl.pallas_call(pack_body, in_specs=[REMOTE] * 5, out_specs=[ONCHIP] * 2,...  5.72 us
  transfers between devices with their start and end apart: 5, of which 3 were waited for; matrix products, arithmetic and copies ran while one was open for 0% of the time, Pallas kernels for 1%

profile of v10, /device:TPU:1, one launch (start us, length us, event | category | flops | bytes accessed | tf_op | source)
XLA Modules:
  0.0 96.1 jit_solution(801294176428742777)
XLA Ops:
  0.0 0.0 copy-start
  0.0 5.7 %split_pack.1 = (bf16[1024,768]{1,0:T(8,128)(2,1)S(1)}, bf16[256,768]{1,0:T(8,128)(2,1)S(1)}) custom-call(s32[2,256]{1,0:T(2,128)} %bitcast.17, s32[1,128]{1,0:T(1,128)} %bitcast.19, s32[2,256]{1,0:T(2,128)} %bitcast.18, bf16[256,4096]{1,0:T(8,128)(2,1)} %tok_hbm.1, bf16[4096,1024]{1,0:T(8,128)(2,1)} %w_hbm.1), custom_call_target="tpu_custom_call" | custom-call | tf_op jit(solution)/shard_map/split_pack/pallas_call | solution.py:152
  5.7 0.0 copy-start.1
  5.7 0.0 slice-start
  5.8 36.0 %all_to_all.10 = bf16[128,8,768]{2,1,0:T(8,128)(2,1)S(1)} all-to-all(bf16[128,8,768]{2,1,0:T(8,128)(2,1)S(1)} %bitcast.16), channel_id=1, replica_groups=mesh['seq'=32,'sub'=4] {'seq','sub'}, dimensions={0} | all-to-all | bytes 3145728 | tf_op jit(solution)/shard_map/all_to_all | solution.py:337
  41.8 0.0 copy-done
  41.8 0.0 copy-done.1
  41.8 0.0 slice-start.1
  41.8 6.0 %experts.1 = bf16[1024,768]{1,0:T(8,128)(2,1)S(1)} custom-call(bf16[1024,768]{1,0:T(8,128)(2,1)S(1)} %bitcast.14, bf16[1,1024,2048]{2,1,0:T(8,128)(2,1)S(1)} %copy-done, bf16[1,1024,1024]{2,1,0:T(8,128)(2,1)S(1)} %copy-done.1), custom_call_target="tpu_custom_call" | custom-call | tf_op jit(solution)/shard_map/experts/pallas_call | solution.py:194
  47.8 28.4 %all_to_all.11 = bf16[128,8,768]{2,1,0:T(8,128)(2,1)S(1)} all-to-all(bf16[128,8,768]{2,1,0:T(8,128)(2,1)S(1)} %bitcast.15), channel_id=1, replica_groups=mesh['seq'=32,'sub'=4] {'seq','sub'}, dimensions={0} | all-to-all | bytes 3145728 | tf_op jit(solution)/shard_map/all_to_all | solution.py:337
  76.2 0.0 slice-done
  76.2 0.0 slice-done.1
  76.2 1.2 %combine_merge.1 = (bf16[256,1024]{1,0:T(8,128)(2,1)S(1)}, bf16[256,256]{1,0:T(8,128)(2,1)S(1)}, bf16[256,256]{1,0:T(8,128)(2,1)S(1)}) custom-call(bf16[256,768]{1,0:T(8,128)(2,1)S(1)} %get-tuple-element.12.v_ref, bf16[1024,768]{1,0:T(8,128)(2,1)S(1)} %bitcast.13, bf16[1024,4096]{1,0:T(8,128)(2,1)S(1)} %bitcast.12), custom_call_target="tpu_custom_call" | custom-call | tf_op jit(solution)/shard_map/combine_merge/pallas_call | solution.py:242
  77.5 0.6 shard_map.83
  78.1 0.8 collective-permute-start
  78.8 0.6 shard_map.82
  79.4 0.8 collective-permute-done
  80.2 0.1 add_convert_fusion.after_ref
  80.3 1.3 %merge_own.1 = (bf16[256,1024]{1,0:T(8,128)(2,1)S(1)}, bf16[256,1024]{1,0:T(8,128)(2,1)S(1)}) custom-call(bf16[256,1024]{1,0:T(8,128)(2,1)S(1)} %get-tuple-element.14.head_ref, bf16[1024,4096]{1,0:T(8,128)(2,1)S(1)} %bitcast.12, bf16[256,768]{1,0:T(8,128)(2,1)S(1)} %add_convert_fusion.after_ref), custom_call_target="tpu_custom_call" | custom-call | tf_op jit(solution)/shard_map/merge_own/pallas_call | solution.py:281
  81.5 0.5 collective-permute-start.1
  82.0 0.1 collective-permute-start.2
  82.1 0.4 collective-permute-start.4
  82.5 1.2 %collective-permute-done.2 = bf16[256,256]{1,0:T(8,128)(2,1)S(1)} collective-permute-done((bf16[256,256]{1,0:T(8,128)(2,1)S(1)}, bf16[256,256]{1,0:T(8,128)(2,1)S(1)}, u32[]{:S(2)}, u32[]{:S(2)}) %collective-permute-start.2) | collective-permute-done | bytes 131104 | tf_op jit(solution)/shard_map/ppermute | solution.py:355
  83.8 0.5 collective-permute-start.3
  84.2 0.0 collective-permute-done.1.in_ref
  84.3 0.1 own_sum.1.own_ref
  84.4 10.9 %collective-permute-done.3.cross_0_ref = bf16[256,256]{1,0:T(8,128)(2,1)S(1)} collective-permute-done((bf16[256,256]{1,0:T(8,128)(2,1)S(1)}, bf16[256,256]{1,0:T(8,128)(2,1)S(1)}, u32[]{:S(2)}, u32[]{:S(2)}) %collective-permute-start.3) | collective-permute-done | bytes 131104 | tf_op jit(solution)/shard_map/ppermute | solution.py:360
  95.2 0.0 collective-permute-done.4.cross_1_ref
  95.2 0.8 last_sum.1
  (2 shorter events, 0.0 us)
Async XLA Ops:
  0.0 41.8 %copy-start = (bf16[1,1024,2048]{2,1,0:T(8,128)(2,1)S(1)}, bf16[1,1024,2048]{2,1,0:T(8,128)(2,1)}, u32[]{:S(2)}) copy-start(bf16[1,1024,2048]{2,1,0:T(8,128)(2,1)} %in_ref.1) | copy-start | bytes 12582916
  5.7 36.0 %copy-start.1 = (bf16[1,1024,1024]{2,1,0:T(8,128)(2,1)S(1)}, bf16[1,1024,1024]{2,1,0:T(8,128)(2,1)}, u32[]{:S(2)}) copy-start(bf16[1,1024,1024]{2,1,0:T(8,128)(2,1)} %down_ref.1) | copy-start | bytes 6291460
  5.7 70.5 %slice-start = ((s8[8388608]{0:T(1024)(128)(4,1)}), s8[4194304]{0:T(1024)(128)(4,1)S(1)}, s32[]{:S(2)}) async-start(s8[8388608]{0:T(1024)(128)(4,1)} %bitcast.11), calls=%async_computation.2 | async-start | bytes 8388608
  41.8 34.4 %slice-start.1 = ((s8[8388608]{0:T(1024)(128)(4,1)}), s8[4194304]{0:T(1024)(128)(4,1)S(1)}, s32[]{:S(2)}) async-start(s8[8388608]{0:T(1024)(128)(4,1)} %bitcast.11), calls=%async_computation.3 | async-start | bytes 8388608
  78.1 2.1 %collective-permute-start = (bf16[256,768]{1,0:T(8,128)(2,1)S(1)}, bf16[256,768]{1,0:T(8,128)(2,1)S(1)}, u32[]{:S(2)}, u32[]{:S(2)}) collective-permute-start(bf16[256,768]{1,0:T(8,128)(2,1)S(1)} %shard_map.83), channel_id=1, source_target_pairs={{0,1},{1,0},{2,3},{3,2},{4,5},{5,4},{6,7},{7,6},{8,9},{9,8},{10,11... | collective-permute-start | bytes 1179656 | tf_op jit(solution)/shard_map/ppermute | solution.py:357
  81.5 2.7 %collective-permute-start.1 = (bf16[256,1024]{1,0:T(8,128)(2,1)S(1)}, bf16[256,1024]{1,0:T(8,128)(2,1)S(1)}, u32[]{:S(2)}, u32[]{:S(2)}) collective-permute-start(bf16[256,1024]{1,0:T(8,128)(2,1)S(1)} %get-tuple-element.16), channel_id=1, source_target_pairs={{0,1},{1,0},{2,3},{3,2},{4,5},{5,4},{6,7},{7,6},{8,9},{9,8},{10,11... | collective-permute-start | bytes 1572872 | tf_op jit(solution)/shard_map/ppermute | solution.py:364
  82.0 1.7 %collective-permute-start.2 = (bf16[256,256]{1,0:T(8,128)(2,1)S(1)}, bf16[256,256]{1,0:T(8,128)(2,1)S(1)}, u32[]{:S(2)}, u32[]{:S(2)}) collective-permute-start(bf16[256,256]{1,0:T(8,128)(2,1)S(1)} %get-tuple-element.18), channel_id=1, source_target_pairs={{0,1},{1,0},{2,3},{3,2},{4,5},{5,4},{6,7},{7,6},{8,9},{9,8},{10,11... | collective-permute-start | bytes 393224 | tf_op jit(solution)/shard_map/ppermute | solution.py:355
  82.1 13.1 %collective-permute-start.4 = (bf16[256,768]{1,0:T(8,128)(2,1)S(1)}, bf16[256,768]{1,0:T(8,128)(2,1)S(1)}, u32[]{:S(2)}, u32[]{:S(2)}) collective-permute-start(bf16[256,768]{1,0:T(8,128)(2,1)S(1)} %add_convert_fusion.after_ref), channel_id=1, source_target_pairs={{0,2},{1,3},{2,0},{3,1},{4,6},{5,7},{6,4},{7,5},{8,10},{9,11},{10,... | collective-permute-start | bytes 1179656 | tf_op jit(solution)/shard_map/ppermute | solution.py:362
  83.8 11.5 %collective-permute-start.3 = (bf16[256,256]{1,0:T(8,128)(2,1)S(1)}, bf16[256,256]{1,0:T(8,128)(2,1)S(1)}, u32[]{:S(2)}, u32[]{:S(2)}) collective-permute-start(bf16[256,256]{1,0:T(8,128)(2,1)S(1)} %add_convert_fusion.1), channel_id=1, source_target_pairs={{0,2},{1,3},{2,0},{3,1},{4,6},{5,7},{6,4},{7,5},{8,10},{9,11},{10,... | collective-permute-start | bytes 393224 | tf_op jit(solution)/shard_map/ppermute | solution.py:360
